TPU v7x, 32 devices: a whole 2x2x4 slice. The times are simulated.
32 devices in a mesh: agent: 4 (over x, core), tp: 8 (over z, y).
Axes of the slice: x: 2, y: 2, z: 4, core: 2. Of those that a mesh axis runs over, the one named last changes fastest.
Arguments:
- tokens: bfloat16 [4, 512, 2048], P('agent', 'tp'), may hold values from -6 to 6
- targets: bfloat16 [4, 512, 2048], P('agent', 'tp'), may hold values from -6 to 6
- params: bfloat16 [4, 2048, 8192], P('agent', None, 'tp'), may hold values from -6 to 6
- tracker: bfloat16 [4, 2048, 8192], P('agent', None, 'tp'), may hold values from -6 to 6
- up_weight: bfloat16 [2048, 8192], P('agent', 'tp'), may hold values from -0.125 to 0.125
- down_weight: bfloat16 [8192, 2048], P('tp', 'agent'), may hold values from -0.0625 to 0.0625
- edge_weight: float32 [4], replicated, may hold values from 0.1 to 0.4
- step_size: float32 [1], replicated, may hold values from 0.1 to 0.5
Outputs:
- new_params: bfloat16 [4, 2048, 8192], P('agent', None, 'tp')
- new_tracker: bfloat16 [4, 2048, 8192], P('agent', None, 'tp')
All inputs are finite; a program needn't handle non-finite values.
Results may differ from a plain program's by a relative error of at most 0.033.
Values may be sent and summed in bfloat16 or wider, within the bound.
No kernel may reach another device: no remote copies, remote signals or barrier semaphores. Data moves between devices by JAX's collectives and lax.ppermute only.
A program may use at most 128 MiB of HBM per device.

v0:
```python
import jax
import jax.numpy as jnp
from jax import lax
from jax.sharding import PartitionSpec as P


def passed_along(value, axis, steps):
    count = lax.axis_size(axis)
    pairs = [(source, (source + steps) % count) for source in range(count)]
    return lax.ppermute(value, axis, pairs)


def on_device(tokens, targets, params, tracker, up_weight, down_weight, edge_weight, step_size):
    target_rows = targets[0]
    param = params[0]
    track = tracker[0]
    left_x, left_y = passed_along((param, track), "agent", 1)
    right_x, right_y = passed_along((param, track), "agent", -1)
    up_full, down_full = (
        lax.all_gather(up_weight, "agent", axis=0, tiled=True),
        lax.all_gather(down_weight, "agent", axis=1, tiled=True),
    )
    whole, whole_targets = (
        lax.all_gather(tokens[0], "tp", axis=0, tiled=True),
        lax.all_gather(target_rows, "tp", axis=0, tiled=True),
    )
    scale = 1.0 / whole.shape[1] ** 0.5
    up = jnp.dot(whole, up_full, preferred_element_type=jnp.float32)

    def dgate_of(weights):
        gate = jnp.dot(whole, weights, preferred_element_type=jnp.float32) * scale
        sig = jax.nn.sigmoid(gate)
        hidden = (sig * gate * up).astype(jnp.bfloat16)
        partial_value = jnp.dot(hidden, down_full, preferred_element_type=jnp.float32)
        summed = lax.psum(partial_value.astype(jnp.bfloat16), "tp").astype(jnp.float32)
        err = (2.0 * (summed - whole_targets.astype(jnp.float32))).astype(jnp.bfloat16)
        back = lax.dot_general(
            err, down_full, (((1,), (1,)), ((), ())), preferred_element_type=jnp.float32
        )
        return (back * up * sig * (1.0 + gate * (1.0 - sig))).astype(jnp.bfloat16)

    def weight_grad(dgate):
        return lax.dot_general(
            whole, dgate, (((0,), (0,)), ((), ())), preferred_element_type=jnp.float32
        )

    old_grad = weight_grad(dgate_of(param))
    count = lax.axis_size("agent")
    index = lax.axis_index("agent")
    e_right = lax.dynamic_slice_in_dim(edge_weight, index, 1)[0]
    e_left = lax.dynamic_slice_in_dim(edge_weight, (index + count - 1) % count, 1)[0]
    own = 1.0 - e_right - e_left
    track32 = track.astype(jnp.float32)
    mixed_x = (
        own * param.astype(jnp.float32)
        + e_right * right_x.astype(jnp.float32)
        + e_left * left_x.astype(jnp.float32)
    )
    mixed_y = (
        own * track32 + e_right * right_y.astype(jnp.float32) + e_left * left_y.astype(jnp.float32)
    )
    fresh = (mixed_x - step_size[0] * track32).astype(jnp.bfloat16)
    new_grad = weight_grad(dgate_of(fresh))
    fresh_track = (mixed_y + (new_grad - old_grad) * scale).astype(jnp.bfloat16)
    return (fresh[None], fresh_track[None])


def solution(mesh):
    return jax.shard_map(
        on_device,
        mesh=mesh,
        in_specs=(
            P("agent", "tp", None),
            P("agent", "tp", None),
            P("agent", None, "tp"),
            P("agent", None, "tp"),
            P("agent", "tp"),
            P("tp", "agent"),
            P(),
            P(),
        ),
        out_specs=(P("agent", None, "tp"), P("agent", None, "tp")),
        check_vma=False,
    )
```

profile of v0, /device:TPU:0, one launch (start us, length us, event | category | flops | bytes accessed | tf_op | source)
XLA Modules:
  0.0 413.9 jit_solution(9907880872152286384)
XLA Ops:
  7.2 0.7 all-gather.11.cloned.1.call-update
  7.9 0.7 all-gather.7.cloned.1.call-update
  8.7 0.7 all-gather.9.cloned.1.call-update
  9.4 6.4 %copy.10 = bf16[1,2048,1024]{1,2,0:T(8,128)(2,1)} copy(bf16[1,2048,1024]{2,1,0:T(8,128)(2,1)} %param.10) | data formatting | bytes 8388608 | tf_op args[2]
  15.9 2.4 collective-permute-start
  19.0 6.6 %copy.11 = bf16[1,2048,1024]{1,2,0:T(8,128)(2,1)} copy(bf16[1,2048,1024]{2,1,0:T(8,128)(2,1)} %param.11) | data formatting | bytes 8388608 | tf_op args[3]
  27.4 34.6 %all-gather.11.cloned.1.call-done = bf16[1,512,2048]{2,1,0:T(8,128)(2,1)} async-done(((bf16[1,64,2048]{2,1,0:T(8,128)(2,1)}), bf16[1,512,2048]{2,1,0:T(8,128)(2,1)}) %all-gather.11.cloned.1.call-update) | async-done | bytes 2097168 | tf_op jit(solution)/shard_map/all_gather | solution.py:24
  61.9 6.7 %fusion.11 = f32[512,1024]{0,1:T(8,128)} fusion(bf16[1,2048,1024]{2,1,0:T(8,128)(2,1)} %param.10, bf16[1,512,2048]{2,1,0:T(8,128)(2,1)} %all-gather.11.cloned.1.call-done), kind=kOutput, calls=%fused_computation.15 | convolution fusion | flops 2147483648 | bytes 8388608 | tf_op jit(solution)/shard_map/dot_general | solution.py:31
  68.6 66.4 %collective-permute-done = bf16[2048,1024]{0,1:T(8,128)(2,1)} collective-permute-done((bf16[2048,1024]{0,1:T(8,128)(2,1)}, bf16[2048,1024]{0,1:T(8,128)(2,1)}, u32[]{:S(2)}, u32[]{:S(2)}) %collective-permute-start) | collective-permute-done | bytes 4194336 | tf_op jit(solution)/shard_map/ppermute | solution.py:10
  135.0 0.7 collective-permute-done.1
  135.8 7.8 %fusion.1 = bf16[2048,1024]{0,1:T(8,128)(2,1)S(1)} fusion(bf16[2048,1024]{0,1:T(8,128)(2,1)} %collective-permute-done.1, bf16[2048,1024]{0,1:T(8,128)(2,1)} %collective-permute-done, f32[]{:T(128)} %bitcast.80, f32[]{:T(128)} %bitcast.1, f32[]{:T(128)} %bitcast, f32[]{:T(128)S(6)} %sub.30, bf16[1,2048,1024]{1,2,0:T(8,128)(2,1)S(1)} %copy-done, ...), kind=kLoop, calls=%fused_computation.3 | loop fusion | flops 25165824 | bytes 20971536 | tf_op jit(solution)/shard_map/convert_element_type | solution.py:62
  143.5 2.0 copy-done.2
  145.6 3.7 fusion.33
  149.2 5.9 %fusion.31 = f32[512,1024]{0,1:T(8,128)} fusion(bf16[2048,1024]{1,0:T(8,128)(2,1)} %all-gather.7.cloned.1.call-done, bf16[1,512,2048]{2,1,0:T(8,128)(2,1)S(1)} %copy-done.5), kind=kOutput, calls=%fused_computation.38 | convolution fusion | flops 2147483648 | bytes 8388608 | tf_op jit(solution)/shard_map/dot_general | solution.py:28
  155.1 1.9 all-gather.9.cloned.1.call-done
  157.0 7.5 %convolution_convert_fusion = bf16[512,2048]{1,0:T(8,128)(2,1)} fusion(bf16[1024,2048]{1,0:T(8,128)(2,1)} %all-gather.9.cloned.1.call-done, f32[512,1024]{0,1:T(8,128)} %fusion.31, f32[512,1024]{0,1:T(8,128)} %fusion.11), kind=kOutput, calls=%fused_computation.17 | convolution fusion | flops 2152202240 | bytes 10485760 | tf_op jit(solution)/shard_map/dot_general | solution.py:34
  164.5 3.9 convolution_convert_fusion.1
  168.5 1.3 collective-permute-start.2
  169.9 6.4 %copy.17 = bf16[1,2048,1024]{2,1,0:T(8,128)(2,1)} copy(bf16[1,2048,1024]{1,2,0:T(8,128)(2,1)} %bitcast.85) | data formatting | bytes 8388608
  176.3 33.1 %all-gather.13.cloned.1.call-done = bf16[1,512,2048]{2,1,0:T(8,128)(2,1)} async-done(((bf16[1,64,2048]{2,1,0:T(8,128)(2,1)}), bf16[1,512,2048]{2,1,0:T(8,128)(2,1)}) %all-gather.13.cloned.1.call-update) | async-done | bytes 2097168 | tf_op jit(solution)/shard_map/all_gather | solution.py:25
  209.3 158.6 %all-reduce.3.cloned.1.call-done = (bf16[512,2048]{1,0:T(8,128)(2,1)}, bf16[512,2048]{1,0:T(8,128)(2,1)}) async-done(((bf16[512,2048]{1,0:T(8,128)(2,1)}, bf16[512,2048]{1,0:T(8,128)(2,1)}), (bf16[512,2048]{1,0:T(8,128)(2,1)}, bf16[512,2048]{1,0:T(8,128)(2,1)})) %all-reduce.3.cloned.1.call-update) | async-done | bytes 4194320 | tf_op jit(solution)/shard_map/psum | solution.py:35
  367.9 12.9 %fusion.29 = f32[1024,2048]{1,0:T(8,128)} fusion(bf16[1,512,2048]{2,1,0:T(8,128)(2,1)S(1)} %copy-done.5, f32[512,1024]{0,1:T(8,128)} %fusion.31, f32[1024,512]{1,0:T(8,128)} %fusion.33, bf16[1024,2048]{1,0:T(8,128)(2,1)} %all-gather.9.cloned.1.call-done, bf16[512,2048]{1,0:T(8,128)(2,1)} %get-tuple-element.4, ...), kind=kOutput, calls=%fused_computation.36 | convolution fusion | flops 4305977344 | bytes 23068672 | tf_op jit(solution)/shard_map/dot_general | solution.py:43
  380.8 20.2 %fusion.10 = bf16[1,2048,1024]{1,2,0:T(8,128)(2,1)} fusion(f32[1024,2048]{1,0:T(8,128)} %fusion.29, bf16[2048,1024]{0,1:T(8,128)(2,1)} %collective-permute-done.3, bf16[2048,1024]{0,1:T(8,128)(2,1)} %collective-permute-done.2, f32[]{:T(128)} %bitcast.1, f32[]{:T(128)} %bitcast, f32[]{:T(128)S(6)} %sub.30, bf16[1,512,2048]{2,1,0:T(8,128)(2,1)S(1)} %copy-done.5, ...), kind=kOutput, calls=%fused_computation.14 | convolution fusion | flops 4331143168 | bytes 39845900 | tf_op jit(solution)/shard_map/dot_general | solution.py:43
  401.0 6.4 %copy.18 = bf16[1,2048,1024]{2,1,0:T(8,128)(2,1)} copy(bf16[1,2048,1024]{1,2,0:T(8,128)(2,1)} %fusion.10) | data formatting | bytes 8388608
  (28 shorter events, 0.9 us)
Async XLA Ops:
  7.2 54.8 %all-gather.11.cloned.1.call-start = ((), (), s32[]{:S(2)}) async-start(), calls=%async_computation.2 | async-start | bytes 2359296 | tf_op jit(solution)/shard_map/all_gather | solution.py:24
  7.9 141.3 %all-gather.7.cloned.1.call-start = ((), (), s32[]{:S(2)}) async-start(), calls=%async_computation | async-start | bytes 5242880 | tf_op jit(solution)/shard_map/all_gather | solution.py:20
  8.6 148.4 %all-gather.9.cloned.1.call-start = ((), (), s32[]{:S(2)}) async-start(), calls=%async_computation.1 | async-start | bytes 5242880 | tf_op jit(solution)/shard_map/all_gather | solution.py:21
  9.4 199.9 %all-gather.13.cloned.1.call-start = ((), (), s32[]{:S(2)}) async-start(), calls=%async_computation.3 | async-start | bytes 2359296 | tf_op jit(solution)/shard_map/all_gather | solution.py:25
  15.9 119.1 %collective-permute-start = (bf16[2048,1024]{0,1:T(8,128)(2,1)}, bf16[2048,1024]{0,1:T(8,128)(2,1)}, u32[]{:S(2)}, u32[]{:S(2)}) collective-permute-start(bf16[2048,1024]{0,1:T(8,128)(2,1)} %bitcast.83), channel_id=1, source_target_pairs={{0,24},{8,0},{16,8},{24,16},{1,25},{9,1},{17,9},{25,17},{2,26},{10... | collective-permute-start | bytes 12582920 | tf_op jit(solution)/shard_map/ppermute | solution.py:10
  18.3 117.5 %collective-permute-start.1 = (bf16[2048,1024]{0,1:T(8,128)(2,1)}, bf16[2048,1024]{0,1:T(8,128)(2,1)}, u32[]{:S(2)}, u32[]{:S(2)}) collective-permute-start(bf16[2048,1024]{0,1:T(8,128)(2,1)} %bitcast.84), channel_id=1, source_target_pairs={{0,8},{8,16},{16,24},{24,0},{1,9},{9,17},{17,25},{25,1},{2,10},{10... | collective-permute-start | bytes 12582920 | tf_op jit(solution)/shard_map/ppermute | solution.py:10
  18.3 349.6 %all-reduce.3.cloned.1.call-start = ((), (), s32[]{:S(2)}) async-start(), calls=%async_computation.4 | async-start | bytes 8388608 | tf_op jit(solution)/shard_map/psum | solution.py:35
  19.0 6.6 %copy-start.3 = (f32[4]{0:T(128)S(1)}, f32[4]{0:T(128)}, u32[]{:S(2)}) copy-start(f32[4]{0:T(128)} %param.14) | copy-start | bytes 52
  61.9 73.8 %copy-start = (bf16[1,2048,1024]{1,2,0:T(8,128)(2,1)S(1)}, bf16[1,2048,1024]{1,2,0:T(8,128)(2,1)}, u32[]{:S(2)}) copy-start(bf16[1,2048,1024]{1,2,0:T(8,128)(2,1)} %copy.11) | copy-start | bytes 12582916
  61.9 73.8 %copy-start.1 = (bf16[1,2048,1024]{1,2,0:T(8,128)(2,1)S(1)}, bf16[1,2048,1024]{1,2,0:T(8,128)(2,1)}, u32[]{:S(2)}) copy-start(bf16[1,2048,1024]{1,2,0:T(8,128)(2,1)} %copy.10) | copy-start | bytes 12582916
  135.7 9.8 %copy-start.5 = (bf16[1,512,2048]{2,1,0:T(8,128)(2,1)S(1)}, bf16[1,512,2048]{2,1,0:T(8,128)(2,1)}, u32[]{:S(2)}) copy-start(bf16[1,512,2048]{2,1,0:T(8,128)(2,1)} %all-gather.11.cloned.1.call-done) | copy-start | bytes 6291460
  143.5 2.0 copy-start.2
  157.0 7.5 %copy-start.4 = (bf16[1024,2048]{1,0:T(8,128)(2,1)S(1)}, bf16[1024,2048]{1,0:T(8,128)(2,1)}, u32[]{:S(2)}) copy-start(bf16[1024,2048]{1,0:T(8,128)(2,1)} %all-gather.9.cloned.1.call-done) | copy-start | bytes 12582916
  157.0 7.5 %copy-start.6 = (f32[512,1024]{0,1:T(8,128)S(1)}, f32[512,1024]{0,1:T(8,128)}, u32[]{:S(2)}) copy-start(f32[512,1024]{0,1:T(8,128)} %fusion.31) | copy-start | bytes 6291460
  157.0 7.5 %copy-start.7 = (f32[1024,512]{1,0:T(8,128)S(1)}, f32[1024,512]{1,0:T(8,128)}, u32[]{:S(2)}) copy-start(f32[1024,512]{1,0:T(8,128)} %fusion.33) | copy-start | bytes 6291460
  168.5 212.3 %collective-permute-start.2 = (bf16[2048,1024]{0,1:T(8,128)(2,1)}, bf16[2048,1024]{0,1:T(8,128)(2,1)}, u32[]{:S(2)}, u32[]{:S(2)}) collective-permute-start(bf16[2048,1024]{0,1:T(8,128)(2,1)} %bitcast.81), channel_id=1, source_target_pairs={{0,24},{8,0},{16,8},{24,16},{1,25},{9,1},{17,9},{25,17},{2,26},{10... | collective-permute-start | bytes 12582920 | tf_op jit(solution)/shard_map/ppermute | solution.py:10
  169.9 211.0 %collective-permute-start.3 = (bf16[2048,1024]{0,1:T(8,128)(2,1)}, bf16[2048,1024]{0,1:T(8,128)(2,1)}, u32[]{:S(2)}, u32[]{:S(2)}) collective-permute-start(bf16[2048,1024]{0,1:T(8,128)(2,1)} %bitcast.82), channel_id=1, source_target_pairs={{0,8},{8,16},{16,24},{24,0},{1,9},{9,17},{17,25},{25,1},{2,10},{10... | collective-permute-start | bytes 12582920 | tf_op jit(solution)/shard_map/ppermute | solution.py:10
Sparse Core Ops, SparseCore 0:
  10.1 51.7 all-gather.10
  63.5 55.5 all-gather.6
  120.7 36.3 all-gather.8
  159.0 50.2 all-gather.12
  212.9 154.9 all-reduce.2
where the time goes:
time: 415 us; the launch traced here: 414 us
  waiting for transfers between devices  297 us (72%)
  matrix products  60.8 us (15%)
  local copies, waits for them, and re-layouts  28.5 us (7%)
  between operations  15.6 us (4%)
  other arithmetic  7.77 us (2%)
    psum x1, waiting for transfers between devices, dgate_of(): lax.psum(partial_value.astype(jnp.bfloat16), 'tp').astype(jnp.float32)  159 us
    ppermute x4, waiting for transfers between devices, passed_along(): return lax.ppermute(value, axis, pairs)  67.1 us
    all_gather x1, waiting for transfers between devices, on_device(): lax.all_gather(tokens[0], 'tp', axis=0, tiled=True)  34.6 us
    dot_general x2, matrix products, weight_grad(): lax.dot_general(whole, dgate, (((0,), (0,)), ((), ())), preferred_element...  33.1 us
    all_gather x1, waiting for transfers between devices, on_device(): lax.all_gather(target_rows, 'tp', axis=0, tiled=True)  33.1 us
    unnamed x20, local copies, waits for them, and re-layouts  27.9 us
    dot_general x2, matrix products, dgate_of(): jnp.dot(hidden, down_full, preferred_element_type=jnp.float32)  11.5 us
    dot_general x2, matrix products, dgate_of(): gate = jnp.dot(whole, weights, preferred_element_type=jnp.float32) * scale  10.3 us
  transfers between devices with their start and end apart: 9, of which 6 were waited for; matrix products, arithmetic and copies ran while one was open for 17% of the time, Pallas kernels for 0%

commit v1 on v0

v1 whole, which is shorter than its diff:
```python
import functools

import jax
import jax.numpy as jnp
from jax import lax
from jax.experimental import pallas as pl
from jax.experimental.pallas import tpu as pltpu
from jax.sharding import PartitionSpec as P


F32 = jnp.float32
BF16 = jnp.bfloat16
CHUNKS = 4


def shifted(value, axis, shift):
    count = lax.axis_size(axis)
    return lax.ppermute(value, axis, [(source, (source + shift) % count) for source in range(count)])


def paired(value, axis):
    return lax.ppermute(value, axis, [(source, source ^ 1) for source in range(lax.axis_size(axis))])


def jumped(value, axis, shift):
    return shifted(value, axis, 2 * shift)


def cost(flops, *arrays):
    return pl.CostEstimate(
        flops=flops, bytes_accessed=sum(a.size * a.dtype.itemsize for a in arrays), transcendentals=0
    )


def block_of(size, most):
    return most if size % most == 0 else size


def gate_kernel(scale, tok_ref, w_ref, out_ref):
    out_ref[...] = jnp.dot(tok_ref[...], w_ref[...], preferred_element_type=F32) * scale


def gate_of(tok, weights, scale):
    rows, depth = tok.shape
    width = weights.shape[1]
    cols = block_of(width, 256)
    out = jax.ShapeDtypeStruct((rows, width), F32)
    return pl.pallas_call(
        functools.partial(gate_kernel, scale),
        grid=(width // cols,),
        in_specs=[
            pl.BlockSpec((rows, depth), lambda i: (0, 0)),
            pl.BlockSpec((depth, cols), lambda i: (0, i)),
        ],
        out_specs=pl.BlockSpec((rows, cols), lambda i: (0, i)),
        out_shape=out,
        cost_estimate=cost(2 * rows * depth * width, tok, weights, out),
        name="gate",
    )(tok, weights)


def chip_index(place, j, half):
    return lax.rem(place[0] - j + half, half)


def up_kernel(place, tok_ref, own_ref, other_ref, out_ref):
    j = pl.program_id(0)
    depth = own_ref.shape[0]

    @pl.when(j == 0)
    def _():
        out_ref[...] = jnp.zeros_like(out_ref)

    def add(first, second):
        out_ref[...] += jnp.dot(tok_ref[:, :depth], first[...], preferred_element_type=F32) + jnp.dot(
            tok_ref[:, depth:], second[...], preferred_element_type=F32
        )

    @pl.when(place[1] == 0)
    def _():
        add(own_ref, other_ref)

    @pl.when(place[1] != 0)
    def _():
        add(other_ref, own_ref)


def up_of(place, tok, own, other):
    half, depth, width = own.shape
    rows = tok.shape[0]
    out = jax.ShapeDtypeStruct((rows, width), F32)
    piece = pl.BlockSpec((None, depth, width), lambda j, place: (j, 0, 0))
    return pl.pallas_call(
        up_kernel,
        grid_spec=pltpu.PrefetchScalarGridSpec(
            num_scalar_prefetch=1,
            grid=(half,),
            in_specs=[
                pl.BlockSpec((rows, 2 * depth), lambda j, place: (0, chip_index(place, j, half))),
                piece,
                piece,
            ],
            out_specs=pl.BlockSpec((rows, width), lambda j, place: (0, 0)),
        ),
        out_shape=out,
        cost_estimate=cost(4 * rows * half * depth * width, tok, own, other, out),
        name="up",
    )(place, tok, own, other)


def share_kernel(place, gate_ref, up_ref, own_ref, other_ref, *rest):
    near_ref, far_refs, hidden = rest[0], rest[1:-1], rest[-1]
    cols = own_ref.shape[1]
    near = near_ref.shape[0]
    piece = far_refs[0].shape[0]

    @pl.when(pl.program_id(0) == 0)
    def _():
        gate = gate_ref[...]
        hidden[...] = (jax.nn.sigmoid(gate) * gate * up_ref[...]).astype(BF16)

    def fill(first, second):
        for at, ref in ((0, first), (cols, second)):
            share = jnp.dot(hidden[...], ref[...], preferred_element_type=F32).astype(BF16)
            near_ref[:, at : at + cols] = share[:near]
            for k, far_ref in enumerate(far_refs):
                start = near + k * piece
                far_ref[:, at : at + cols] = share[start : start + piece]

    @pl.when(place[1] == 0)
    def _():
        fill(own_ref, other_ref)

    @pl.when(place[1] != 0)
    def _():
        fill(other_ref, own_ref)


def share_of(place, gate, up, own, other, pieces):
    half, width, cols = own.shape
    rows = gate.shape[0]
    near, piece = rows // 2, rows // 2 // pieces
    weights = pl.BlockSpec((None, width, cols), lambda j, place: (j, 0, 0))
    whole = pl.BlockSpec((rows, width), lambda j, place: (0, 0))
    depth = 2 * cols * half
    out = [jax.ShapeDtypeStruct((near, depth), BF16)] + [
        jax.ShapeDtypeStruct((piece, depth), BF16) for _ in range(pieces)
    ]
    return pl.pallas_call(
        share_kernel,
        grid_spec=pltpu.PrefetchScalarGridSpec(
            num_scalar_prefetch=1,
            grid=(half,),
            in_specs=[whole, whole, weights, weights],
            out_specs=[
                pl.BlockSpec((o.shape[0], 2 * cols), lambda j, place: (0, chip_index(place, j, half)))
                for o in out
            ],
            scratch_shapes=[pltpu.VMEM((rows, width), BF16)],
        ),
        out_shape=out,
        cost_estimate=cost(2 * rows * width * depth, gate, up, own, other, *out),
        name="share",
    )(place, gate, up, own, other)


def back_kernel(count, place, gate_ref, up_ref, own_ref, other_ref, *rest):
    pieces, out_ref, err, total = rest[:count], rest[count], rest[count + 1], rest[count + 2]
    j = pl.program_id(0)
    cols = own_ref.shape[1]
    piece = pieces[0].shape[0]

    @pl.when(j == 0)
    def _():
        total[...] = jnp.zeros_like(total)

    for k, ref in enumerate(pieces):
        err[k * piece : (k + 1) * piece, :] = ref[...]

    def add(first, second):
        dims = (((1,), (1,)), ((), ()))
        total[...] += lax.dot_general(
            err[:, :cols], first[...], dims, preferred_element_type=F32
        ) + lax.dot_general(err[:, cols:], second[...], dims, preferred_element_type=F32)

    @pl.when(place[1] == 0)
    def _():
        add(own_ref, other_ref)

    @pl.when(place[1] != 0)
    def _():
        add(other_ref, own_ref)

    @pl.when(j == pl.num_programs(0) - 1)
    def _():
        gate = gate_ref[...]
        sig = jax.nn.sigmoid(gate)
        out_ref[...] = (total[...] * up_ref[...] * sig * (1.0 + gate * (1.0 - sig))).astype(BF16)


def dgate_of(place, gate, up, own, other, pieces):
    half, width, cols = own.shape
    rows = gate.shape[0]
    piece = pieces[0].shape[0]
    weights = pl.BlockSpec((None, width, cols), lambda j, place: (j, 0, 0))
    whole = pl.BlockSpec((rows, width), lambda j, place: (0, 0))
    out = jax.ShapeDtypeStruct((rows, width), BF16)
    return pl.pallas_call(
        functools.partial(back_kernel, len(pieces)),
        grid_spec=pltpu.PrefetchScalarGridSpec(
            num_scalar_prefetch=1,
            grid=(half,),
            in_specs=[whole, whole, weights, weights]
            + [pl.BlockSpec((piece, 2 * cols), lambda j, place: (0, chip_index(place, j, half)))] * len(pieces),
            out_specs=whole,
            scratch_shapes=[pltpu.VMEM((rows, 2 * cols), BF16), pltpu.VMEM((rows, width), F32)],
        ),
        out_shape=out,
        cost_estimate=cost(4 * rows * width * cols * half, gate, up, own, other, out, *pieces),
        name="dgate",
    )(place, gate, up, own, other, *pieces)


def fresh_kernel(scale, coef, tok_ref, p_ref, left_ref, right_ref, t_ref, fresh_ref, gate_ref):
    k = pl.program_id(0)

    @pl.when(k == 0)
    def _():
        gate_ref[...] = jnp.zeros_like(gate_ref)

    mixed = (
        coef[0] * p_ref[...].astype(F32)
        + coef[1] * right_ref[...].astype(F32)
        + coef[2] * left_ref[...].astype(F32)
    )
    fresh = (mixed - coef[3] * t_ref[...].astype(F32)).astype(BF16)
    fresh_ref[...] = fresh
    gate_ref[...] += jnp.dot(tok_ref[...], fresh, preferred_element_type=F32)

    @pl.when(k == pl.num_programs(0) - 1)
    def _():
        gate_ref[...] = gate_ref[...] * scale


def fresh_of(coef, tok, param, left, right, track, scale):
    depth, width = param.shape
    rows = tok.shape[0]
    step = block_of(depth, 256)
    block = pl.BlockSpec((step, width), lambda k: (k, 0))
    out = [jax.ShapeDtypeStruct((depth, width), BF16), jax.ShapeDtypeStruct((rows, width), F32)]
    return pl.pallas_call(
        functools.partial(fresh_kernel, scale),
        grid=(depth // step,),
        in_specs=[
            pl.BlockSpec(memory_space=pltpu.SMEM),
            pl.BlockSpec((rows, step), lambda k: (0, k)),
            block,
            block,
            block,
            block,
        ],
        out_specs=[block, pl.BlockSpec((rows, width), lambda k: (0, 0))],
        out_shape=out,
        cost_estimate=cost(2 * rows * depth * width, tok, param, left, right, track, *out),
        name="fresh",
    )(coef, tok, param, left, right, track)


def final_kernel(scale, coef, tok_ref, new_ref, old_ref, t_ref, left_ref, right_ref, *rest):
    out_ref = rest[-1]
    tok = tok_ref[...]
    dims = (((0,), (0,)), ((), ()))
    change = lax.dot_general(tok, new_ref[...], dims, preferred_element_type=F32) - lax.dot_general(
        tok, old_ref[...], dims, preferred_element_type=F32
    )
    mixed = (
        coef[0] * t_ref[...].astype(F32)
        + coef[1] * right_ref[...].astype(F32)
        + coef[2] * left_ref[...].astype(F32)
    )
    out_ref[...] = (mixed + change * scale).astype(BF16)


def final_of(coef, tok, new, old, track, left, right, scale, start, so_far):
    depth, width = track.shape
    rows = tok.shape[0]
    part = left.shape[0]
    step = block_of(part, 256)
    base = start // step
    there = pl.BlockSpec((step, width), lambda k: (base + k, 0))
    here = pl.BlockSpec((step, width), lambda k: (k, 0))
    whole = pl.BlockSpec((rows, width), lambda k: (0, 0))
    operands = [coef, tok, new, old, track, left, right]
    specs = [
        pl.BlockSpec(memory_space=pltpu.SMEM),
        pl.BlockSpec((rows, step), lambda k: (0, base + k)),
        whole,
        whole,
        there,
        here,
        here,
    ]
    aliases = {}
    if so_far is not None:
        aliases = {len(operands): 0}
        operands.append(so_far)
        specs.append(pl.BlockSpec(memory_space=pl.ANY))
    out = jax.ShapeDtypeStruct((depth, width), BF16)
    return pl.pallas_call(
        functools.partial(final_kernel, scale),
        grid=(part // step,),
        in_specs=specs,
        out_specs=there,
        out_shape=out,
        input_output_aliases=aliases,
        cost_estimate=cost(4 * rows * part * width, left, right, left, left, new, old),
        name="final",
    )(*operands)


def spread(piece, axis, pairs):
    near = [piece] + [jumped(piece, axis, j) for j in range(1, pairs)]
    return near + [paired(part, axis) for part in near]


def on_device(tokens, targets, params, tracker, up_weight, down_weight, edge_weight, step_size):
    token_rows, target_rows, param, track = tokens[0], targets[0], params[0], tracker[0]
    agents, count = lax.axis_size("agent"), lax.axis_size("tp")
    half, pairs = agents // 2, count // 2
    depth = param.shape[0]
    piece = token_rows.shape[0]
    scale = 1.0 / depth**0.5

    index = lax.axis_index("agent")
    place = jnp.stack([index // 2, index % 2]).astype(jnp.int32)
    e_right = lax.dynamic_slice_in_dim(edge_weight, index, 1)[0]
    e_left = lax.dynamic_slice_in_dim(edge_weight, (index + agents - 1) % agents, 1)[0]
    coef = jnp.stack([1.0 - e_right - e_left, e_right, e_left, step_size[0]])

    def gathered(weight):
        return [weight] + [jumped(weight, "agent", j) for j in range(1, half)]

    ups, downs = gathered(up_weight), gathered(down_weight)
    left_x, right_x = shifted(param, "agent", 1), shifted(param, "agent", -1)
    part = depth // CHUNKS
    around = []
    for c in range(CHUNKS):
        t = track[c * part : (c + 1) * part]
        around.append((shifted(t, "agent", 1), shifted(t, "agent", -1)))

    tok = jnp.concatenate(spread(token_rows, "tp", pairs))
    own_up = jnp.stack(ups)
    other_up = paired(own_up, "agent")
    own_down = jnp.stack(downs)
    other_down = paired(own_down, "agent")
    gate = gate_of(tok, param, scale)
    up = up_of(place, tok, own_up, other_up)

    def errors(gate):
        near, *far = share_of(place, gate, up, own_down, other_down, pairs)
        order = list(range(1, pairs)) + [0]
        sent = {j: paired(far[j], "tp") for j in order}

        def joined(j):
            mine = near[j * piece : (j + 1) * piece].astype(F32)
            return mine + sent[j].astype(F32)

        summed = []
        for j in range(1, pairs):
            value = lax.optimization_barrier(joined(j).astype(BF16))
            summed.append(jumped(value, "tp", -j))
        total = joined(0)
        for value in summed:
            total = total + value.astype(F32)
        err = (2.0 * (total - target_rows.astype(F32))).astype(BF16)
        return spread(err, "tp", pairs)

    def dgate(gate, pieces):
        return dgate_of(place, gate, up, own_down, other_down, pieces)

    old_pieces = errors(gate)
    later, old_pieces[0] = lax.optimization_barrier((coef, old_pieces[0]))
    fresh, new_gate = fresh_of(later, tok, param, left_x, right_x, track, scale)
    new_pieces = errors(new_gate)
    old = dgate(gate, old_pieces)
    new = dgate(new_gate, new_pieces)
    out = None
    for c, (left_y, right_y) in enumerate(around):
        out = final_of(coef, tok, new, old, track, left_y, right_y, scale, c * part, out)
    return (fresh[None], out[None])


def solution(mesh):
    return jax.shard_map(
        on_device,
        mesh=mesh,
        in_specs=(
            P("agent", "tp", None),
            P("agent", "tp", None),
            P("agent", None, "tp"),
            P("agent", None, "tp"),
            P("agent", "tp"),
            P("tp", "agent"),
            P(),
            P(),
        ),
        out_specs=(P("agent", None, "tp"), P("agent", None, "tp")),
        check_vma=False,
    )
```

time: 415 us -> 317 us (0.76)
  waiting for transfers between devices: 297 us -> 143 us
  Pallas kernels: 0 us -> 78.1 us
  starting transfers between devices: 3.95 us -> 66.8 us
  matrix products: 60.8 us -> 0 us
  local copies, waits for them, and re-layouts: 28.5 us -> 8.78 us
  between operations: 15.6 us -> 2.82 us
  other arithmetic: 7.77 us -> 13.2 us
    psum x1 -> x0, waiting for transfers between devices: 159 us -> none  [dgate_of(): lax.psum(partial_value.astype(jnp.bfloat16), 'tp').astype(jnp.float32)]
    pallas_call x0 -> x11, Pallas kernels: none -> 78.1 us  [the longest x4 19.5 us: final_of(): pl.pallas_call(functools.partial(final_kernel, scale), grid=(part // step...]
    ppermute x4 -> x49, waiting for transfers between devices: 67.1 us -> 143 us  [the longest x27 77.8 us: shifted(): lax.ppermute(value, axis, [(source, (source + shift) % count) for source...]
    all_gather x4 -> x0, waiting for transfers between devices: 69.5 us -> none  [the longest x1 34.6 us: on_device(): lax.all_gather(tokens[0], 'tp', axis=0, tiled=True)]
    ppermute x4 -> x49, starting transfers between devices: 3.75 us -> 66.8 us  [the longest x27 48.1 us: shifted(): lax.ppermute(value, axis, [(source, (source + shift) % count) for source...]
    dot_general x7 -> x0, matrix products: 60.8 us -> none  [the longest x2 33.1 us: weight_grad(): lax.dot_general(whole, dgate, (((0,), (0,)), ((), ())), preferred_element...]
    unnamed x20 -> x65, local copies, waits for them, and re-layouts: 27.9 us -> 3.89 us
    another operation x0 -> x4, other arithmetic: none -> 8.15 us  [the longest x1 2.92 us: on_device(): own_down = jnp.stack(downs)]
  transfers between devices with their start and end apart: 9 -> 49, of which waited for: 6 -> 24; matrix products, arithmetic and copies ran while one was open for 17% -> 6% of each run, Pallas kernels for 0% -> 23%
where the time goes in v1:
time: 317 us; the launch traced here: 312 us
  waiting for transfers between devices  143 us (45%)
  Pallas kernels  78.1 us (25%)
  starting transfers between devices  66.8 us (21%)
  other arithmetic  13.2 us (4%)
  local copies, waits for them, and re-layouts  8.78 us (3%)
    ppermute x27, waiting for transfers between devices, shifted(): lax.ppermute(value, axis, [(source, (source + shift) % count) for source...  77.8 us
    ppermute x22, waiting for transfers between devices, paired(): lax.ppermute(value, axis, [(source, source ^ 1) for source in range(lax.a...  64.7 us
    ppermute x27, starting transfers between devices, shifted(): lax.ppermute(value, axis, [(source, (source + shift) % count) for source...  48.1 us
    pallas_call x4, Pallas kernels, final_of(): pl.pallas_call(functools.partial(final_kernel, scale), grid=(part // step...  19.5 us
    ppermute x22, starting transfers between devices, paired(): lax.ppermute(value, axis, [(source, source ^ 1) for source in range(lax.a...  18.6 us
    pallas_call x2, Pallas kernels, dgate_of(): pl.pallas_call(functools.partial(back_kernel, len(pieces)), grid_spec=plt...  17.1 us
    pallas_call x2, Pallas kernels, share_of(): pl.pallas_call(share_kernel, grid_spec=pltpu.PrefetchScalarGridSpec(num_s...  15.2 us
    pallas_call x1, Pallas kernels, fresh_of(): pl.pallas_call(functools.partial(fresh_kernel, scale), grid=(depth // ste...  13.3 us
  transfers between devices with their start and end apart: 49, of which 24 were waited for; matrix products, arithmetic and copies ran while one was open for 6% of the time, Pallas kernels for 23%

profile of v1, /device:TPU:0, one launch (start us, length us, event | category | flops | bytes accessed | tf_op | source)
XLA Modules:
  0.0 312.2 jit_solution(7755448351628447814)
XLA Ops:
  9.7 18.2 %collective-permute-done.7 = bf16[512,1024]{1,0:T(8,128)(2,1)S(1)} collective-permute-done((bf16[512,1024]{1,0:T(8,128)(2,1)}, bf16[512,1024]{1,0:T(8,128)(2,1)S(1)}, u32[]{:S(2)}, u32[]{:S(2)}) %collective-permute-start.7) | collective-permute-done | bytes 1048608 | tf_op jit(solution)/shard_map/ppermute | solution.py:18
  33.7 16.8 %collective-permute-done.9 = bf16[1024,512]{1,0:T(8,128)(2,1)} collective-permute-done((bf16[1024,512]{1,0:T(8,128)(2,1)}, bf16[1024,512]{1,0:T(8,128)(2,1)}, u32[]{:S(2)}, u32[]{:S(2)}) %collective-permute-start.9) | collective-permute-done | bytes 1048608 | tf_op jit(solution)/shard_map/ppermute | solution.py:18
  58.9 5.8 %collective-permute-done.4 = bf16[64,2048]{1,0:T(8,128)(2,1)S(1)} collective-permute-done((bf16[64,2048]{1,0:T(8,128)(2,1)S(1)}, bf16[64,2048]{1,0:T(8,128)(2,1)S(1)}, u32[]{:S(2)}, u32[]{:S(2)}) %collective-permute-start.4) | collective-permute-done | bytes 262176 | tf_op jit(solution)/shard_map/ppermute | solution.py:22
  66.3 5.4 %collective-permute-done.5 = bf16[64,2048]{1,0:T(8,128)(2,1)S(1)} collective-permute-done((bf16[64,2048]{1,0:T(8,128)(2,1)S(1)}, bf16[64,2048]{1,0:T(8,128)(2,1)S(1)}, u32[]{:S(2)}, u32[]{:S(2)}) %collective-permute-start.5) | collective-permute-done | bytes 262176 | tf_op jit(solution)/shard_map/ppermute | solution.py:22
  72.0 6.2 %collective-permute-done.6 = bf16[64,2048]{1,0:T(8,128)(2,1)S(1)} collective-permute-done((bf16[64,2048]{1,0:T(8,128)(2,1)}, bf16[64,2048]{1,0:T(8,128)(2,1)S(1)}, u32[]{:S(2)}, u32[]{:S(2)}) %collective-permute-start.6) | collective-permute-done | bytes 262176 | tf_op jit(solution)/shard_map/ppermute | solution.py:22
  79.6 6.4 %gate.1.gate_ref = f32[512,1024]{1,0:T(8,128)} custom-call(bf16[512,2048]{1,0:T(8,128)(2,1)} %copy-done, bf16[2048,1024]{1,0:T(8,128)(2,1)} %bitcast.3.w_ref.p_ref), custom_call_target="tpu_custom_call" | custom-call | flops 2147483648 | bytes 8388608 | tf_op jit(solution)/shard_map/gate/pallas_call | solution.py:48
  86.0 6.6 %up.1.up_ref = f32[512,1024]{1,0:T(8,128)} custom-call(s32[2]{0:T(128)} %pad_add_fusion.place, bf16[512,2048]{1,0:T(8,128)(2,1)} %copy-done, bf16[2,512,1024]{2,1,0:T(8,128)(2,1)} %pad_maximum_fusion.own_ref, bf16[2,512,1024]{2,1,0:T(8,128)(2,1)} %collective-permute-done.8.other_ref), custom_call_target="tpu_custom_call" | custom-call | flops 2147483648 | bytes 8388608 | tf_op jit(solution)/shard_map/up/pallas_call | solution.py:93
  92.6 7.7 %share.2 = (bf16[256,2048]{1,0:T(8,128)(2,1)}, bf16[64,2048]{1,0:T(8,128)(2,1)}, bf16[64,2048]{1,0:T(8,128)(2,1)}, bf16[64,2048]{1,0:T(8,128)(2,1)}, bf16[64,2048]{1,0:T(8,128)(2,1)}) custom-call(s32[2]{0:T(128)} %pad_add_fusion.place, f32[512,1024]{1,0:T(8,128)} %gate.1.gate_ref, f32[512,1024]{1,0:T(8,128)} %up.1.up_ref, ...), custom_call_target="tpu_custom_call" | custom-call | flops 2147483648 | bytes 10485760 | tf_op jit(solution)/shard_map/share/pallas_call | solution.py:149
  109.9 5.3 %collective-permute-done.14 = bf16[64,2048]{1,0:T(8,128)(2,1)S(1)} collective-permute-done((bf16[64,2048]{1,0:T(8,128)(2,1)}, bf16[64,2048]{1,0:T(8,128)(2,1)S(1)}, u32[]{:S(2)}, u32[]{:S(2)}) %collective-permute-start.14) | collective-permute-done | bytes 262176 | tf_op jit(solution)/shard_map/ppermute | solution.py:22
  131.6 9.1 %collective-permute-done.15 = bf16[64,2048]{1,0:T(8,128)(2,1)S(1)} collective-permute-done((bf16[64,2048]{1,0:T(8,128)(2,1)S(1)}, bf16[64,2048]{1,0:T(8,128)(2,1)S(1)}, u32[]{:S(2)}, u32[]{:S(2)}) %collective-permute-start.15) | collective-permute-done | bytes 262176 | tf_op jit(solution)/shard_map/ppermute | solution.py:18
  141.9 13.3 %fresh.1 = (bf16[2048,1024]{1,0:T(8,128)(2,1)}, f32[512,1024]{1,0:T(8,128)}) custom-call(f32[4]{0:T(128)} %pad_maximum_fusion.2.coef, bf16[512,2048]{1,0:T(8,128)(2,1)} %copy-done, bf16[2048,1024]{1,0:T(8,128)(2,1)} %bitcast.3.w_ref.p_ref, bf16[2048,1024]{1,0:T(8,128)(2,1)} %collective-permute-done.18.left_ref, ...), custom_call_target="tpu_custom_call" | custom-call | flops 2147483648 | bytes 25165824 | tf_op jit(solution)/shard_map/fresh/pallas_call | solution.py:251
  155.2 7.6 %share.3 = (bf16[256,2048]{1,0:T(8,128)(2,1)}, bf16[64,2048]{1,0:T(8,128)(2,1)}, bf16[64,2048]{1,0:T(8,128)(2,1)}, bf16[64,2048]{1,0:T(8,128)(2,1)}, bf16[64,2048]{1,0:T(8,128)(2,1)}) custom-call(s32[2]{0:T(128)} %pad_add_fusion.place, f32[512,1024]{1,0:T(8,128)} %get-tuple-element.23.gate_ref, f32[512,1024]{1,0:T(8,128)} %up.1.up_ref, ...), custom_call_target="tpu_custom_call" | custom-call | flops 2147483648 | bytes 10485760 | tf_op jit(solution)/shard_map/share/pallas_call | solution.py:149
  165.1 7.1 %collective-permute-done.21 = bf16[64,2048]{1,0:T(8,128)(2,1)S(1)} collective-permute-done((bf16[64,2048]{1,0:T(8,128)(2,1)}, bf16[64,2048]{1,0:T(8,128)(2,1)S(1)}, u32[]{:S(2)}, u32[]{:S(2)}) %collective-permute-start.21) | collective-permute-done | bytes 262176 | tf_op jit(solution)/shard_map/ppermute | solution.py:22
  172.2 5.6 %collective-permute-done.23 = bf16[64,2048]{1,0:T(8,128)(2,1)S(1)} collective-permute-done((bf16[64,2048]{1,0:T(8,128)(2,1)}, bf16[64,2048]{1,0:T(8,128)(2,1)S(1)}, u32[]{:S(2)}, u32[]{:S(2)}) %collective-permute-start.23) | collective-permute-done | bytes 262176 | tf_op jit(solution)/shard_map/ppermute | solution.py:22
  188.1 12.5 %collective-permute-start.24 = (bf16[64,2048]{1,0:T(8,128)(2,1)S(1)}, bf16[64,2048]{1,0:T(8,128)(2,1)S(1)}, u32[]{:S(2)}, u32[]{:S(2)}) collective-permute-start(bf16[64,2048]{1,0:T(8,128)(2,1)S(1)} %get-tuple-element.36), channel_id=1, source_target_pairs={{0,4},{1,5},{2,6},{3,7},{4,0},{5,1},{6,2},{7,3},{8,12},{9,13},{10,... | collective-permute-start | bytes 786440 | tf_op jit(solution)/shard_map/ppermute | solution.py:18
  200.7 6.5 %collective-permute-start.26 = (bf16[64,2048]{1,0:T(8,128)(2,1)S(1)}, bf16[64,2048]{1,0:T(8,128)(2,1)S(1)}, u32[]{:S(2)}, u32[]{:S(2)}) collective-permute-start(bf16[64,2048]{1,0:T(8,128)(2,1)S(1)} %get-tuple-element.35), channel_id=1, source_target_pairs={{0,2},{1,3},{2,4},{3,5},{4,6},{5,7},{6,0},{7,1},{8,10},{9,11},{10,... | collective-permute-start | bytes 786440 | tf_op jit(solution)/shard_map/ppermute | solution.py:18
  212.1 8.8 %collective-permute-done.24 = bf16[64,2048]{1,0:T(8,128)(2,1)S(1)} collective-permute-done((bf16[64,2048]{1,0:T(8,128)(2,1)S(1)}, bf16[64,2048]{1,0:T(8,128)(2,1)S(1)}, u32[]{:S(2)}, u32[]{:S(2)}) %collective-permute-start.24) | collective-permute-done | bytes 262176 | tf_op jit(solution)/shard_map/ppermute | solution.py:18
  237.7 9.9 %collective-permute-done.28.rest_2_ = bf16[64,2048]{1,0:T(8,128)(2,1)S(1)} collective-permute-done((bf16[64,2048]{1,0:T(8,128)(2,1)S(1)}, bf16[64,2048]{1,0:T(8,128)(2,1)S(1)}, u32[]{:S(2)}, u32[]{:S(2)}) %collective-permute-start.28) | collective-permute-done | bytes 262176 | tf_op jit(solution)/shard_map/ppermute | solution.py:18
  252.5 5.6 %collective-permute-done.32.rest_6_ = bf16[64,2048]{1,0:T(8,128)(2,1)S(1)} collective-permute-done((bf16[64,2048]{1,0:T(8,128)(2,1)S(1)}, bf16[64,2048]{1,0:T(8,128)(2,1)S(1)}, u32[]{:S(2)}, u32[]{:S(2)}) %collective-permute-start.32) | collective-permute-done | bytes 262176 | tf_op jit(solution)/shard_map/ppermute | solution.py:22
  263.8 8.6 %dgate.3.old_ref = bf16[512,1024]{1,0:T(8,128)(2,1)} custom-call(s32[2]{0:T(128)} %pad_add_fusion.place, f32[512,1024]{1,0:T(8,128)} %gate.1.gate_ref, f32[512,1024]{1,0:T(8,128)} %up.1.up_ref, bf16[2,1024,512]{2,1,0:T(8,128)(2,1)} %pad_maximum_fusion.1.own_ref, bf16[2,1024,512]{2,1,0:T(8,128)(2,1)} %collective-permute-done.10.other_ref, ...), custom_call_target="tpu_custom_call" | custom-call | flops 2147483648 | bytes 11534336 | tf_op jit(solution)/shard_map/dgate/pallas_call | solution.py:208
  272.4 8.5 %dgate.2.new_ref = bf16[512,1024]{1,0:T(8,128)(2,1)} custom-call(s32[2]{0:T(128)} %pad_add_fusion.place, f32[512,1024]{1,0:T(8,128)} %get-tuple-element.23.gate_ref, f32[512,1024]{1,0:T(8,128)} %up.1.up_ref, bf16[2,1024,512]{2,1,0:T(8,128)(2,1)} %pad_maximum_fusion.1.own_ref, bf16[2,1024,512]{2,1,0:T(8,128)(2,1)} %collective-permute-done.10.other_ref, ...), custom_call_target="tpu_custom_call" | custom-call | flops 2147483648 | bytes 11534336 | tf_op jit(solution)/shard_map/dgate/pallas_call | solution.py:208
  285.8 4.9 %final.5.rest_0_ = bf16[2048,1024]{1,0:T(8,128)(2,1)} custom-call(f32[4]{0:T(128)} %pad_maximum_fusion.2.coef, bf16[512,2048]{1,0:T(8,128)(2,1)} %copy-done, bf16[512,1024]{1,0:T(8,128)(2,1)} %dgate.2.new_ref, bf16[512,1024]{1,0:T(8,128)(2,1)} %dgate.3.old_ref, bf16[2048,1024]{1,0:T(8,128)(2,1)} %bitcast.26, ...), custom_call_target="tpu_custom_call", output_to_operand_aliasing={{}: (7, {})} | custom-call | flops 1073741824 | bytes 6291456 | tf_op jit(solution)/shard_map/final/pallas_call | solution.py:309
  295.5 4.9 %final.6.rest_0_ = bf16[2048,1024]{1,0:T(8,128)(2,1)} custom-call(f32[4]{0:T(128)} %pad_maximum_fusion.2.coef, bf16[512,2048]{1,0:T(8,128)(2,1)} %copy-done, bf16[512,1024]{1,0:T(8,128)(2,1)} %dgate.2.new_ref, bf16[512,1024]{1,0:T(8,128)(2,1)} %dgate.3.old_ref, bf16[2048,1024]{1,0:T(8,128)(2,1)} %bitcast.27, ...), custom_call_target="tpu_custom_call", output_to_operand_aliasing={{}: (7, {})} | custom-call | flops 1073741824 | bytes 6291456 | tf_op jit(solution)/shard_map/final/pallas_call | solution.py:309
  300.4 6.9 %collective-permute-done.42.right_ref = bf16[512,1024]{1,0:T(8,128)(2,1)} collective-permute-done((bf16[512,1024]{1,0:T(8,128)(2,1)}, bf16[512,1024]{1,0:T(8,128)(2,1)}, u32[]{:S(2)}, u32[]{:S(2)}) %collective-permute-start.42) | collective-permute-done | bytes 1048608 | tf_op jit(solution)/shard_map/ppermute | solution.py:18
  (161 shorter events, 111.2 us)
Async XLA Ops:
  0.6 27.3 %collective-permute-start.7 = (bf16[512,1024]{1,0:T(8,128)(2,1)}, bf16[512,1024]{1,0:T(8,128)(2,1)S(1)}, u32[]{:S(2)}, u32[]{:S(2)}) collective-permute-start(bf16[512,1024]{1,0:T(8,128)(2,1)} %param.12), channel_id=1, source_target_pairs={{0,16},{8,24},{16,0},{24,8},{1,17},{9,25},{17,1},{25,9},{2,18},{10... | collective-permute-start | bytes 3145736 | tf_op jit(solution)/shard_map/ppermute | solution.py:18
  3.7 46.8 %collective-permute-start.9 = (bf16[1024,512]{1,0:T(8,128)(2,1)}, bf16[1024,512]{1,0:T(8,128)(2,1)}, u32[]{:S(2)}, u32[]{:S(2)}) collective-permute-start(bf16[1024,512]{1,0:T(8,128)(2,1)} %param.13), channel_id=1, source_target_pairs={{0,16},{8,24},{16,0},{24,8},{1,17},{9,25},{17,1},{25,9},{2,18},{10... | collective-permute-start | bytes 3145736 | tf_op jit(solution)/shard_map/ppermute | solution.py:18
  3.7 27.0 %collective-permute-start = (bf16[64,2048]{1,0:T(8,128)(2,1)}, bf16[64,2048]{1,0:T(8,128)(2,1)S(1)}, u32[]{:S(2)}, u32[]{:S(2)}) collective-permute-start(bf16[64,2048]{1,0:T(8,128)(2,1)} %bitcast.33), channel_id=1, source_target_pairs={{0,2},{1,3},{2,4},{3,5},{4,6},{5,7},{6,0},{7,1},{8,10},{9,11},{10,... | collective-permute-start | bytes 786440 | tf_op jit(solution)/shard_map/ppermute | solution.py:18
  5.8 26.7 %collective-permute-start.1 = (bf16[64,2048]{1,0:T(8,128)(2,1)}, bf16[64,2048]{1,0:T(8,128)(2,1)S(1)}, u32[]{:S(2)}, u32[]{:S(2)}) collective-permute-start(bf16[64,2048]{1,0:T(8,128)(2,1)} %bitcast.34), channel_id=1, source_target_pairs={{0,4},{1,5},{2,6},{3,7},{4,0},{5,1},{6,2},{7,3},{8,12},{9,13},{10,... | collective-permute-start | bytes 786440 | tf_op jit(solution)/shard_map/ppermute | solution.py:18
  8.4 47.1 %collective-permute-start.2 = (bf16[64,2048]{1,0:T(8,128)(2,1)}, bf16[64,2048]{1,0:T(8,128)(2,1)}, u32[]{:S(2)}, u32[]{:S(2)}) collective-permute-start(bf16[64,2048]{1,0:T(8,128)(2,1)} %bitcast.35), channel_id=1, source_target_pairs={{0,6},{1,7},{2,0},{3,1},{4,2},{5,3},{6,4},{7,5},{8,14},{9,15},{10,... | collective-permute-start | bytes 786440 | tf_op jit(solution)/shard_map/ppermute | solution.py:18
  27.9 114.0 %collective-permute-start.18 = (bf16[2048,1024]{1,0:T(8,128)(2,1)}, bf16[2048,1024]{1,0:T(8,128)(2,1)}, u32[]{:S(2)}, u32[]{:S(2)}) collective-permute-start(bf16[2048,1024]{1,0:T(8,128)(2,1)} %bitcast.3.w_ref.p_ref), channel_id=1, source_target_pairs={{0,8},{8,16},{16,24},{24,0},{1,9},{9,17},{17,25},{25,1},{2,10},{10... | collective-permute-start | bytes 12582920 | tf_op jit(solution)/shard_map/ppermute | solution.py:18
  30.7 111.1 %collective-permute-start.19 = (bf16[2048,1024]{1,0:T(8,128)(2,1)}, bf16[2048,1024]{1,0:T(8,128)(2,1)}, u32[]{:S(2)}, u32[]{:S(2)}) collective-permute-start(bf16[2048,1024]{1,0:T(8,128)(2,1)} %bitcast.3.w_ref.p_ref), channel_id=1, source_target_pairs={{0,24},{8,0},{16,8},{24,16},{1,25},{9,1},{17,9},{25,17},{2,26},{10... | collective-permute-start | bytes 12582920 | tf_op jit(solution)/shard_map/ppermute | solution.py:18
  33.2 52.8 %collective-permute-start.8 = (bf16[2,512,1024]{2,1,0:T(8,128)(2,1)}, bf16[2,512,1024]{2,1,0:T(8,128)(2,1)}, u32[]{:S(2)}, u32[]{:S(2)}) collective-permute-start(bf16[2,512,1024]{2,1,0:T(8,128)(2,1)} %pad_maximum_fusion.own_ref), channel_id=1, source_target_pairs={{0,8},{8,0},{16,24},{24,16},{1,9},{9,1},{17,25},{25,17},{2,10},{10... | collective-permute-start | bytes 6291464 | tf_op jit(solution)/shard_map/ppermute | solution.py:22
  55.4 37.2 %collective-permute-start.10 = (bf16[2,1024,512]{2,1,0:T(8,128)(2,1)}, bf16[2,1024,512]{2,1,0:T(8,128)(2,1)}, u32[]{:S(2)}, u32[]{:S(2)}) collective-permute-start(bf16[2,1024,512]{2,1,0:T(8,128)(2,1)} %pad_maximum_fusion.1.own_ref), channel_id=1, source_target_pairs={{0,8},{8,0},{16,24},{24,16},{1,9},{9,1},{17,25},{25,17},{2,10},{10... | collective-permute-start | bytes 6291464 | tf_op jit(solution)/shard_map/ppermute | solution.py:22
  131.6 53.8 %collective-permute-start.47 = (bf16[512,1024]{1,0:T(8,128)(2,1)}, bf16[512,1024]{1,0:T(8,128)(2,1)S(1)}, u32[]{:S(2)}, u32[]{:S(2)}) collective-permute-start(bf16[512,1024]{1,0:T(8,128)(2,1)} %get-tuple-element.30), channel_id=1, source_target_pairs={{0,8},{8,16},{16,24},{24,0},{1,9},{9,17},{17,25},{25,1},{2,10},{10... | collective-permute-start | bytes 3145736 | tf_op jit(solution)/shard_map/ppermute | solution.py:18
  140.6 46.3 %collective-permute-start.48 = (bf16[512,1024]{1,0:T(8,128)(2,1)}, bf16[512,1024]{1,0:T(8,128)(2,1)S(1)}, u32[]{:S(2)}, u32[]{:S(2)}) collective-permute-start(bf16[512,1024]{1,0:T(8,128)(2,1)} %get-tuple-element.30), channel_id=1, source_target_pairs={{0,24},{8,0},{16,8},{24,16},{1,25},{9,1},{17,9},{25,17},{2,26},{10... | collective-permute-start | bytes 3145736 | tf_op jit(solution)/shard_map/ppermute | solution.py:18
  172.2 51.9 %collective-permute-start.45 = (bf16[512,1024]{1,0:T(8,128)(2,1)}, bf16[512,1024]{1,0:T(8,128)(2,1)S(1)}, u32[]{:S(2)}, u32[]{:S(2)}) collective-permute-start(bf16[512,1024]{1,0:T(8,128)(2,1)} %get-tuple-element.33), channel_id=1, source_target_pairs={{0,8},{8,16},{16,24},{24,0},{1,9},{9,17},{17,25},{25,1},{2,10},{10... | collective-permute-start | bytes 3145736 | tf_op jit(solution)/shard_map/ppermute | solution.py:18
  185.4 21.8 %collective-permute-start.20 = (bf16[64,2048]{1,0:T(8,128)(2,1)S(1)}, bf16[64,2048]{1,0:T(8,128)(2,1)S(1)}, u32[]{:S(2)}, u32[]{:S(2)}) collective-permute-start(bf16[64,2048]{1,0:T(8,128)(2,1)S(1)} %copy-done.28), channel_id=1, source_target_pairs={{0,1},{1,0},{2,3},{3,2},{4,5},{5,4},{6,7},{7,6},{8,9},{9,8},{10,11... | collective-permute-start | bytes 786440 | tf_op jit(solution)/shard_map/ppermute | solution.py:22
  187.0 23.1 %collective-permute-start.22 = (bf16[64,2048]{1,0:T(8,128)(2,1)S(1)}, bf16[64,2048]{1,0:T(8,128)(2,1)S(1)}, u32[]{:S(2)}, u32[]{:S(2)}) collective-permute-start(bf16[64,2048]{1,0:T(8,128)(2,1)S(1)} %get-tuple-element.34), channel_id=1, source_target_pairs={{0,6},{1,7},{2,0},{3,1},{4,2},{5,3},{6,4},{7,5},{8,14},{9,15},{10,... | collective-permute-start | bytes 786440 | tf_op jit(solution)/shard_map/ppermute | solution.py:18
  188.1 32.7 %collective-permute-start.24 = (bf16[64,2048]{1,0:T(8,128)(2,1)S(1)}, bf16[64,2048]{1,0:T(8,128)(2,1)S(1)}, u32[]{:S(2)}, u32[]{:S(2)}) collective-permute-start(bf16[64,2048]{1,0:T(8,128)(2,1)S(1)} %get-tuple-element.36), channel_id=1, source_target_pairs={{0,4},{1,5},{2,6},{3,7},{4,0},{5,1},{6,2},{7,3},{8,12},{9,13},{10,... | collective-permute-start | bytes 786440 | tf_op jit(solution)/shard_map/ppermute | solution.py:18
  200.7 20.7 %collective-permute-start.26 = (bf16[64,2048]{1,0:T(8,128)(2,1)S(1)}, bf16[64,2048]{1,0:T(8,128)(2,1)S(1)}, u32[]{:S(2)}, u32[]{:S(2)}) collective-permute-start(bf16[64,2048]{1,0:T(8,128)(2,1)S(1)} %get-tuple-element.35), channel_id=1, source_target_pairs={{0,2},{1,3},{2,4},{3,5},{4,6},{5,7},{6,0},{7,1},{8,10},{9,11},{10,... | collective-permute-start | bytes 786440 | tf_op jit(solution)/shard_map/ppermute | solution.py:18
  207.2 20.1 %collective-permute-start.36 = (bf16[64,2048]{1,0:T(8,128)(2,1)S(1)}, bf16[64,2048]{1,0:T(8,128)(2,1)S(1)}, u32[]{:S(2)}, u32[]{:S(2)}) collective-permute-start(bf16[64,2048]{1,0:T(8,128)(2,1)S(1)} %fusion.1.rest_0_), channel_id=1, source_target_pairs={{0,6},{1,7},{2,0},{3,1},{4,2},{5,3},{6,4},{7,5},{8,14},{9,15},{10,... | collective-permute-start | bytes 786440 | tf_op jit(solution)/shard_map/ppermute | solution.py:18
  210.1 20.5 %collective-permute-start.37 = (bf16[64,2048]{1,0:T(8,128)(2,1)S(1)}, bf16[64,2048]{1,0:T(8,128)(2,1)S(1)}, u32[]{:S(2)}, u32[]{:S(2)}) collective-permute-start(bf16[64,2048]{1,0:T(8,128)(2,1)S(1)} %fusion.1.rest_0_), channel_id=1, source_target_pairs={{0,1},{1,0},{2,3},{3,2},{4,5},{5,4},{6,7},{7,6},{8,9},{9,8},{10,11... | collective-permute-start | bytes 786440 | tf_op jit(solution)/shard_map/ppermute | solution.py:22
  227.3 20.3 %collective-permute-start.28 = (bf16[64,2048]{1,0:T(8,128)(2,1)S(1)}, bf16[64,2048]{1,0:T(8,128)(2,1)S(1)}, u32[]{:S(2)}, u32[]{:S(2)}) collective-permute-start(bf16[64,2048]{1,0:T(8,128)(2,1)S(1)} %fusion.3.rest_0_), channel_id=1, source_target_pairs={{0,4},{1,5},{2,6},{3,7},{4,0},{5,1},{6,2},{7,3},{8,12},{9,13},{10,... | collective-permute-start | bytes 786440 | tf_op jit(solution)/shard_map/ppermute | solution.py:18
  249.6 36.2 %collective-permute-start.46 = (bf16[512,1024]{1,0:T(8,128)(2,1)}, bf16[512,1024]{1,0:T(8,128)(2,1)}, u32[]{:S(2)}, u32[]{:S(2)}) collective-permute-start(bf16[512,1024]{1,0:T(8,128)(2,1)} %get-tuple-element.33), channel_id=1, source_target_pairs={{0,24},{8,0},{16,8},{24,16},{1,25},{9,1},{17,9},{25,17},{2,26},{10... | collective-permute-start | bytes 3145736 | tf_op jit(solution)/shard_map/ppermute | solution.py:18
  249.8 40.9 %collective-permute-start.43 = (bf16[512,1024]{1,0:T(8,128)(2,1)}, bf16[512,1024]{1,0:T(8,128)(2,1)}, u32[]{:S(2)}, u32[]{:S(2)}) collective-permute-start(bf16[512,1024]{1,0:T(8,128)(2,1)} %get-tuple-element.31), channel_id=1, source_target_pairs={{0,8},{8,16},{16,24},{24,0},{1,9},{9,17},{17,25},{25,1},{2,10},{10... | collective-permute-start | bytes 3145736 | tf_op jit(solution)/shard_map/ppermute | solution.py:18
  252.5 43.0 %collective-permute-start.44 = (bf16[512,1024]{1,0:T(8,128)(2,1)}, bf16[512,1024]{1,0:T(8,128)(2,1)}, u32[]{:S(2)}, u32[]{:S(2)}) collective-permute-start(bf16[512,1024]{1,0:T(8,128)(2,1)} %get-tuple-element.31), channel_id=1, source_target_pairs={{0,24},{8,0},{16,8},{24,16},{1,25},{9,1},{17,9},{25,17},{2,26},{10... | collective-permute-start | bytes 3145736 | tf_op jit(solution)/shard_map/ppermute | solution.py:18
  258.1 42.3 %collective-permute-start.41 = (bf16[512,1024]{1,0:T(8,128)(2,1)}, bf16[512,1024]{1,0:T(8,128)(2,1)}, u32[]{:S(2)}, u32[]{:S(2)}) collective-permute-start(bf16[512,1024]{1,0:T(8,128)(2,1)} %get-tuple-element.32), channel_id=1, source_target_pairs={{0,8},{8,16},{16,24},{24,0},{1,9},{9,17},{17,25},{25,1},{2,10},{10... | collective-permute-start | bytes 3145736 | tf_op jit(solution)/shard_map/ppermute | solution.py:18
  263.4 43.9 %collective-permute-start.42 = (bf16[512,1024]{1,0:T(8,128)(2,1)}, bf16[512,1024]{1,0:T(8,128)(2,1)}, u32[]{:S(2)}, u32[]{:S(2)}) collective-permute-start(bf16[512,1024]{1,0:T(8,128)(2,1)} %get-tuple-element.32), channel_id=1, source_target_pairs={{0,24},{8,0},{16,8},{24,16},{1,25},{9,1},{17,9},{25,17},{2,26},{10... | collective-permute-start | bytes 3145736 | tf_op jit(solution)/shard_map/ppermute | solution.py:18
  (54 other events, 1065.7 us)

commit v2 on v0

v2 whole, which is shorter than its diff:
```python
import functools

import jax
import jax.numpy as jnp
from jax import lax
from jax.experimental import pallas as pl
from jax.experimental.pallas import tpu as pltpu
from jax.sharding import PartitionSpec as P


F32 = jnp.float32
BF16 = jnp.bfloat16
PARTS = (4, 4, 4, 2, 2)
VMEM_LIMIT = 67043328


def shifted(value, axis, shift):
    count = lax.axis_size(axis)
    return lax.ppermute(value, axis, [(source, (source + shift) % count) for source in range(count)])


def paired(value, axis):
    return lax.ppermute(value, axis, [(source, source ^ 1) for source in range(lax.axis_size(axis))])


def jumped(value, axis, shift):
    return shifted(value, axis, 2 * shift)


def cost(flops, *arrays):
    return pl.CostEstimate(
        flops=flops, bytes_accessed=sum(a.size * a.dtype.itemsize for a in arrays), transcendentals=0
    )


def block_of(size, most):
    return most if size % most == 0 else size


def column_blocks(width):
    if width % 512 == 0:
        return [0, width // 2, 3 * width // 4, width]
    return [0, width // 2, width] if width % 256 == 0 else [0, width]


def like(shape, dtype):
    return jax.ShapeDtypeStruct(shape, dtype)


def dot(a, b, contract=(1, 0)):
    return lax.dot_general(a, b, (((contract[0],), (contract[1],)), ((), ())), preferred_element_type=F32)


SMEM = pl.BlockSpec(memory_space=pltpu.SMEM)
call = functools.partial(pl.pallas_call, compiler_params=pltpu.CompilerParams(vmem_limit_bytes=VMEM_LIMIT))


def columns(place, i, size):
    return pl.ds(pl.multiple_of(place[i] * size, size), size)


def pack_kernel(*refs):
    *pieces, out_ref, turned_ref = refs
    rows = pieces[0].shape[0]
    for k, ref in enumerate(pieces):
        out_ref[k * rows : (k + 1) * rows, :] = ref[...]
    turned_ref[...] = out_ref[...].T


def pack(pieces):
    rows, width = pieces[0].shape
    rows *= len(pieces)
    dtype = pieces[0].dtype
    return call(pack_kernel, out_shape=[like((rows, width), dtype), like((width, rows), dtype)], name="pack")(
        *pieces
    )


def gate_kernel(scale, tok_ref, w_ref, out_ref):
    out_ref[...] = dot(tok_ref[...], w_ref[...]) * scale


def gate_of(tok, weights, scale):
    rows, depth = tok.shape
    width = weights.shape[1]
    cols = block_of(width, 512)
    out = like((rows, width), F32)
    return call(
        functools.partial(gate_kernel, scale),
        grid=(width // cols,),
        in_specs=[
            pl.BlockSpec((rows, depth), lambda i: (0, 0)),
            pl.BlockSpec((depth, cols), lambda i: (0, i)),
        ],
        out_specs=pl.BlockSpec((rows, cols), lambda i: (0, i)),
        out_shape=out,
        cost_estimate=cost(2 * rows * depth * width, tok, weights, out),
        name="gate",
    )(tok, weights)


def up_kernel(place, tok_ref, *refs):
    total = None
    for i, ref in enumerate(refs[:-1]):
        term = dot(tok_ref[:, columns(place, i, ref.shape[0])], ref[...])
        total = term if total is None else total + term
    refs[-1][...] = total


def up_of(place, tok, pieces):
    depth, width = pieces[0].shape
    rows = tok.shape[0]
    cols = block_of(width, 256)
    out = like((rows, width), F32)
    return call(
        up_kernel,
        grid=(width // cols,),
        in_specs=[SMEM, pl.BlockSpec(tok.shape, lambda n: (0, 0))]
        + [pl.BlockSpec((depth, cols), lambda n: (0, n))] * len(pieces),
        out_specs=pl.BlockSpec((rows, cols), lambda n: (0, n)),
        out_shape=out,
        cost_estimate=cost(2 * rows * depth * width * len(pieces), tok, out, *pieces),
        name="up",
    )(place, tok, *pieces)


def add_share(place, gate, up_ref, weights, carry, outs, total):
    hidden = (jax.nn.sigmoid(gate) * gate * up_ref[...]).astype(BF16)
    n, last = pl.program_id(0), pl.num_programs(0) - 1
    for i, ref in enumerate(weights):
        term = dot(hidden, ref[...])

        @pl.when(n == 0)
        def _():
            total[i] = term if carry is None else carry[i] + term

        @pl.when(n > 0)
        def _():
            total[i] += term

    if not outs:
        return

    @pl.when(n == last)
    def _():
        cols = weights[0].shape[1]
        for i in range(len(weights)):
            start = 0
            for ref in outs:
                stop = start + ref.shape[0]
                ref[:, columns(place, i, cols)] = total[i, start:stop, :].astype(BF16)
                start = stop


def share_kernel(count, place, gate_ref, up_ref, *refs):
    add_share(place, gate_ref[...], up_ref, refs[:count], None, refs[count:-1], refs[-1])


def share_outs(rows, depth, pairs):
    near, piece = rows // 2, rows // 2 // pairs
    outs = [like((near, depth), BF16)] + [like((piece, depth), BF16)] * pairs
    return outs, [pl.BlockSpec(o.shape, lambda n: (0, 0)) for o in outs]


def share_of(place, gate, up, downs, pairs):
    rows, width = gate.shape
    cols = downs[0].shape[1]
    depth = cols * len(downs)
    block = block_of(width, 256)
    spec = pl.BlockSpec((rows, block), lambda n: (0, n))
    outs, out_specs = share_outs(rows, depth, pairs)
    return call(
        functools.partial(share_kernel, len(downs)),
        grid=(width // block,),
        in_specs=[SMEM, spec, spec] + [pl.BlockSpec((block, cols), lambda n: (n, 0))] * len(downs),
        out_specs=out_specs,
        out_shape=outs,
        scratch_shapes=[pltpu.VMEM((len(downs), rows, cols), F32)],
        cost_estimate=cost(2 * rows * width * depth, gate, up, *downs, *outs),
        name="share",
    )(place, gate, up, *downs)


def fresh_kernel(count, scale, first, last, place, coef, tok_ref, p_ref, left_ref, right_ref, t_ref, up_ref, *refs):
    weights, refs = refs[:count], refs[count:]
    carry = None
    if not first:
        carry, refs = refs[0], refs[3:]
    fresh_ref, gate_ref, *refs = refs
    mixed = (
        coef[0] * p_ref[...].astype(F32)
        + coef[1] * right_ref[...].astype(F32)
        + coef[2] * left_ref[...].astype(F32)
    )
    fresh = (mixed - coef[3] * t_ref[...].astype(F32)).astype(BF16)
    fresh_ref[...] = fresh
    gate = dot(tok_ref[...], fresh) * scale
    gate_ref[...] = gate
    outs, total = (refs[:-1], refs[-1]) if last else ([], refs[0])
    add_share(place, gate, up_ref, weights, carry, outs, total)


def fresh_of(place, coef, tok, param, left, right, track, up, downs, pairs, scale, start, so_far):
    depth, width = param.shape
    rows, part = tok.shape[0], left.shape[1]
    cols = downs[0].shape[1]
    block = block_of(part, 256)
    base = start // block
    first, last = so_far is None, start + part == width
    there = pl.BlockSpec((depth, block), lambda n: (0, base + n))
    here = pl.BlockSpec((depth, block), lambda n: (0, n))
    hidden = pl.BlockSpec((rows, block), lambda n: (0, base + n))
    operands = [place, coef, tok, param, left, right, track, up, *downs]
    specs = [SMEM, SMEM, pl.BlockSpec(tok.shape, lambda n: (0, 0)), there, here, here, there, hidden]
    specs += [pl.BlockSpec((block, cols), lambda n: (base + n, 0))] * len(downs)
    total = (len(downs), rows, cols)
    whole = pl.BlockSpec(total, lambda n: (0, 0, 0))
    aliases = {}
    if not first:
        aliases = {len(operands) + 1: 0, len(operands) + 2: 1}
        operands += [so_far[2], so_far[0], so_far[1]]
        specs += [whole, pl.BlockSpec(memory_space=pl.ANY), pl.BlockSpec(memory_space=pl.ANY)]
    outs, out_specs = [like((depth, width), BF16), like((rows, width), F32)], [there, hidden]
    scratch = []
    if last:
        more, more_specs = share_outs(rows, cols * len(downs), pairs)
        outs, out_specs = outs + more, out_specs + more_specs
        scratch = [pltpu.VMEM(total, F32)]
    else:
        outs, out_specs = outs + [like(total, F32)], out_specs + [whole]
    return call(
        functools.partial(fresh_kernel, len(downs), scale, first, last),
        grid=(part // block,),
        in_specs=specs,
        out_specs=out_specs,
        out_shape=outs,
        scratch_shapes=scratch,
        input_output_aliases=aliases,
        cost_estimate=cost(4 * rows * depth * part, left, left, right, right, left, up, *downs),
        name="fresh",
    )(*operands)


def join_kernel(mine_ref, other_ref, out_ref):
    out_ref[...] = (mine_ref[...].astype(F32) + other_ref[...].astype(F32)).astype(BF16)


def join(near, other, j):
    out = like(other.shape, BF16)
    whole = pl.BlockSpec(other.shape, lambda i: (0, 0))
    return call(
        join_kernel,
        grid=(1,),
        in_specs=[pl.BlockSpec(other.shape, lambda i: (j, 0)), whole],
        out_specs=whole,
        out_shape=out,
        cost_estimate=cost(out.size, other, other, out),
        name="join",
    )(near, other)


def dgate_block(count, place, gate_ref, up_ref, refs, err):
    weights, pieces = refs[:count], refs[count:]

    @pl.when(pl.program_id(0) == 0)
    def _():
        rows = pieces[0].shape[0]
        for k, ref in enumerate(pieces):
            err[k * rows : (k + 1) * rows, :] = ref[...]

    back = None
    for i, ref in enumerate(weights):
        term = dot(err[:, columns(place, i, ref.shape[1])], ref[...], (1, 1))
        back = term if back is None else back + term
    gate = gate_ref[...]
    sig = jax.nn.sigmoid(gate)
    return (back * up_ref[...] * sig * (1.0 + gate * (1.0 - sig))).astype(BF16)


def dgate_kernel(count, place, gate_ref, up_ref, *refs):
    refs[-2][...] = dgate_block(count, place, gate_ref, up_ref, refs[:-2], refs[-1])


def tail_kernel(count, scale, place, turned_ref, base_ref, gate_ref, up_ref, *refs):
    *refs, dgate_ref, out_ref, err = refs
    value = dgate_block(count, place, gate_ref, up_ref, refs, err)
    dgate_ref[...] = value
    out_ref[...] = (base_ref[...] + dot(turned_ref[...], value) * scale).astype(BF16)


def dgate_of(place, gate, up, downs, pieces, more=None):
    width, cols = downs[0].shape
    rows = gate.shape[0]
    block = block_of(width, 256)
    hidden = pl.BlockSpec((rows, block), lambda n: (0, n))
    whole = pl.BlockSpec(pieces[0].shape, lambda n: (0, 0))
    depth = cols * len(downs)
    operands, specs = [place], [SMEM]
    outs, out_specs = [like((rows, width), BF16)], [hidden]
    kernel, flops = functools.partial(dgate_kernel, len(downs)), 2 * rows * width * depth
    if more is not None:
        turned, base, out, scale = more
        tall = pl.BlockSpec((base.shape[0], block), lambda n: (0, n))
        operands += [turned, base]
        specs += [pl.BlockSpec((base.shape[0], rows), lambda n: (0, 0)), tall]
        outs, out_specs = outs + [out], out_specs + [tall]
        kernel, flops = functools.partial(tail_kernel, len(downs), scale), 2 * flops
    return call(
        kernel,
        grid=(width // block,),
        in_specs=specs
        + [hidden, hidden]
        + [pl.BlockSpec((block, cols), lambda n: (n, 0))] * len(downs)
        + [whole] * len(pieces),
        out_specs=out_specs,
        out_shape=outs,
        scratch_shapes=[pltpu.VMEM((rows, depth), BF16)],
        cost_estimate=cost(flops, gate, up, *outs, *downs, *pieces),
        name="dgate",
    )(*operands, gate, up, *downs, *pieces)


def base_kernel(scale, coef, turned_ref, old_ref, t_ref, left_ref, right_ref, *rest):
    mixed = (
        coef[0] * t_ref[...].astype(F32)
        + coef[1] * right_ref[...].astype(F32)
        + coef[2] * left_ref[...].astype(F32)
    )
    rest[-1][...] = mixed - dot(turned_ref[...], old_ref[...]) * scale


def last_kernel(scale, coef, turned_ref, new_ref, old_ref, t_ref, left_ref, right_ref, *rest):
    turned = turned_ref[...]
    change = dot(turned, new_ref[...]) - dot(turned, old_ref[...])
    mixed = (
        coef[0] * t_ref[...].astype(F32)
        + coef[1] * right_ref[...].astype(F32)
        + coef[2] * left_ref[...].astype(F32)
    )
    rest[-1][...] = (mixed + change * scale).astype(BF16)


def part_call(kernel, coef, turned, grads, track, left, right, start, out, so_far, name):
    width = track.shape[1]
    rows, part = turned.shape[1], left.shape[0]
    step = block_of(part, 256)
    base = start // step
    there = pl.BlockSpec((step, width), lambda k: (base + k, 0))
    here = pl.BlockSpec((step, width), lambda k: (k, 0))
    whole = pl.BlockSpec((rows, width), lambda k: (0, 0))
    operands = [coef, turned, *grads, track, left, right]
    specs = [SMEM, pl.BlockSpec((step, rows), lambda k: (base + k, 0))]
    specs += [whole] * len(grads) + [there, here, here]
    aliases = {}
    if so_far is not None:
        aliases = {len(operands): 0}
        operands.append(so_far)
        specs.append(pl.BlockSpec(memory_space=pl.ANY))
    return call(
        kernel,
        grid=(part // step,),
        in_specs=specs,
        out_specs=there,
        out_shape=out,
        input_output_aliases=aliases,
        cost_estimate=cost(2 * len(grads) * rows * part * width, left, right, left, left, *grads),
        name=name,
    )(*operands)


def spread(piece, axis, pairs):
    near = [piece] + [jumped(piece, axis, j) for j in range(1, pairs)]
    return near + [paired(part, axis) for part in near]


def on_device(tokens, targets, params, tracker, up_weight, down_weight, edge_weight, step_size):
    token_rows, target_rows, param, track = tokens[0], targets[0], params[0], tracker[0]
    agents, count = lax.axis_size("agent"), lax.axis_size("tp")
    half, pairs = agents // 2, count // 2
    depth = param.shape[0]
    piece = token_rows.shape[0]
    scale = 1.0 / depth**0.5

    index = lax.axis_index("agent")
    even, parity = index // 2, index % 2
    chips = [lax.rem(even - j + half, half) for j in range(half)]
    place = jnp.stack([2 * c + parity for c in chips] + [2 * c + 1 - parity for c in chips]).astype(jnp.int32)
    e_right = lax.dynamic_slice_in_dim(edge_weight, index, 1)[0]
    e_left = lax.dynamic_slice_in_dim(edge_weight, (index + agents - 1) % agents, 1)[0]
    coef = jnp.stack([1.0 - e_right - e_left, e_right, e_left, step_size[0]])

    def gathered(weight):
        own = [weight] + [jumped(weight, "agent", j) for j in range(1, half)]
        return own + [paired(w, "agent") for w in own]

    ups, downs = gathered(up_weight), gathered(down_weight)
    edges = column_blocks(param.shape[1])
    blocks = len(edges) - 1
    sides = []
    for start, end in zip(edges, edges[1:]):
        p = param[:, start:end]
        sides.append((shifted(p, "agent", 1), shifted(p, "agent", -1)))
    ends = [depth * sum(PARTS[: c + 1]) // sum(PARTS) for c in range(len(PARTS))]
    starts = [0] + ends[:-1]
    around = []
    for start, end in zip(starts, ends):
        t = track[start:end]
        around.append((shifted(t, "agent", 1), shifted(t, "agent", -1)))

    tok, turned = pack(spread(token_rows, "tp", pairs))
    gate = gate_of(tok, param, scale)
    up = up_of(place, tok, ups)

    def errors(shares):
        near, *far = shares
        order = list(range(1, pairs)) + [0]
        sent = {j: paired(far[j], "tp") for j in order}
        summed = []
        for j in range(1, pairs):
            value = join(near, sent[j], j)
            summed.append(jumped(value, "tp", -j))
        total = near[:piece].astype(F32) + sent[0].astype(F32)
        for value in summed:
            total = total + value.astype(F32)
        err = (2.0 * (total - target_rows.astype(F32))).astype(BF16)
        return spread(err, "tp", pairs)

    shares = share_of(place, gate, up, downs, pairs)
    made = None
    for h in range(blocks - 1):
        made = fresh_of(
            place, coef, tok, param, *sides[h], track, up, downs, pairs, scale, edges[h], made
        )
    old_pieces = errors(shares)
    later, old_pieces[0] = lax.optimization_barrier((coef, old_pieces[0]))
    fresh, new_gate, *shares = fresh_of(
        place, later, tok, param, *sides[-1], track, up, downs, pairs, scale, edges[-2], made
    )
    new_pieces = errors(shares)
    (old,) = dgate_of(place, gate, up, downs, old_pieces)
    base = None
    early_like, all_like = like((starts[-1], track.shape[1]), F32), like(track.shape, BF16)
    for c in range(len(PARTS) - 1):
        kernel = functools.partial(base_kernel, scale)
        base = part_call(kernel, coef, turned, [old], track, *around[c], starts[c], early_like, base, "base")
    new, out = dgate_of(place, new_gate, up, downs, new_pieces, (turned, base, all_like, scale))
    kernel = functools.partial(last_kernel, scale)
    out = part_call(
        kernel, coef, turned, [new, old], track, *around[-1], starts[-1], all_like, out, "last"
    )
    return (fresh[None], out[None])


def solution(mesh):
    return jax.shard_map(
        on_device,
        mesh=mesh,
        in_specs=(
            P("agent", "tp", None),
            P("agent", "tp", None),
            P("agent", None, "tp"),
            P("agent", None, "tp"),
            P("agent", "tp"),
            P("tp", "agent"),
            P(),
            P(),
        ),
        out_specs=(P("agent", None, "tp"), P("agent", None, "tp")),
        check_vma=False,
    )
```

time: 415 us -> 351 us (0.85)
  waiting for transfers between devices: 297 us -> 161 us
  Pallas kernels: 0 us -> 107 us
  matrix products: 60.8 us -> 0 us
  starting transfers between devices: 3.95 us -> 59.8 us
  local copies, waits for them, and re-layouts: 28.5 us -> 11.8 us
  between operations: 15.6 us -> 2.79 us
    psum x1 -> x0, waiting for transfers between devices: 159 us -> none  [dgate_of(): lax.psum(partial_value.astype(jnp.bfloat16), 'tp').astype(jnp.float32)]
    pallas_call x0 -> x20, Pallas kernels: none -> 107 us  [the longest x3 30.4 us: fresh_of(): call(functools.partial(fresh_kernel, len(downs), scale, first, last), gri...]
    ppermute x4 -> x57, waiting for transfers between devices: 67.1 us -> 161 us  [the longest x33 125 us: shifted(): lax.ppermute(value, axis, [(source, (source + shift) % count) for source...]
    all_gather x4 -> x0, waiting for transfers between devices: 69.5 us -> none  [the longest x1 34.6 us: on_device(): lax.all_gather(tokens[0], 'tp', axis=0, tiled=True)]
    dot_general x7 -> x0, matrix products: 60.8 us -> none  [the longest x2 33.1 us: weight_grad(): lax.dot_general(whole, dgate, (((0,), (0,)), ((), ())), preferred_element...]
    ppermute x4 -> x57, starting transfers between devices: 3.75 us -> 59.8 us  [the longest x33 38.6 us: shifted(): lax.ppermute(value, axis, [(source, (source + shift) % count) for source...]
    unnamed x20 -> x28, local copies, waits for them, and re-layouts: 27.9 us -> 0.77 us
    slice x0 -> x4, local copies, waits for them, and re-layouts: none -> 10.4 us  [the longest x2 5.87 us: on_device(): t = track[start:end]]
  transfers between devices with their start and end apart: 9 -> 57, of which waited for: 6 -> 22; matrix products, arithmetic and copies ran while one was open for 17% -> 5% of each run, Pallas kernels for 0% -> 30%
where the time goes in v2:
time: 351 us; the launch traced here: 349 us
  waiting for transfers between devices  161 us (46%)
  Pallas kernels  107 us (30%)
  starting transfers between devices  59.8 us (17%)
  local copies, waits for them, and re-layouts  11.8 us (3%)
  other arithmetic  6.79 us (2%)
    ppermute x33, waiting for transfers between devices, shifted(): lax.ppermute(value, axis, [(source, (source + shift) % count) for source...  125 us
    ppermute x33, starting transfers between devices, shifted(): lax.ppermute(value, axis, [(source, (source + shift) % count) for source...  38.6 us
    ppermute x24, waiting for transfers between devices, paired(): lax.ppermute(value, axis, [(source, source ^ 1) for source in range(lax.a...  35.9 us
    pallas_call x3, Pallas kernels, fresh_of(): call(functools.partial(fresh_kernel, len(downs), scale, first, last), gri...  30.4 us
    pallas_call x2, Pallas kernels, dgate_of(): call(kernel, grid=(width // block,), in_specs=specs + [hidden, hidden] +...  21.4 us
    ppermute x24, starting transfers between devices, paired(): lax.ppermute(value, axis, [(source, source ^ 1) for source in range(lax.a...  21.1 us
    pallas_call x5, Pallas kernels, part_call(): call(kernel, grid=(part // step,), in_specs=specs, out_specs=there, out_s...  19.2 us
    pallas_call x6, Pallas kernels, join(): call(join_kernel, grid=(1,), in_specs=[pl.BlockSpec(other.shape, lambda i...  10.8 us
  transfers between devices with their start and end apart: 57, of which 22 were waited for; matrix products, arithmetic and copies ran while one was open for 5% of the time, Pallas kernels for 30%

profile of v2, /device:TPU:0, one launch (start us, length us, event | category | flops | bytes accessed | tf_op | source)
XLA Modules:
  0.0 349.4 jit_solution(3188105953482004054)
XLA Ops:
  9.7 5.6 %collective-permute-done.refs_1_ = bf16[64,2048]{1,0:T(8,128)(2,1)S(1)} collective-permute-done((bf16[64,2048]{1,0:T(8,128)(2,1)}, bf16[64,2048]{1,0:T(8,128)(2,1)S(1)}, u32[]{:S(2)}, u32[]{:S(2)}) %collective-permute-start) | collective-permute-done | bytes 262176 | tf_op jit(solution)/shard_map/ppermute | solution.py:19
  17.1 8.1 %collective-permute-done.1.refs_2_ = bf16[64,2048]{1,0:T(8,128)(2,1)S(1)} collective-permute-done((bf16[64,2048]{1,0:T(8,128)(2,1)}, bf16[64,2048]{1,0:T(8,128)(2,1)S(1)}, u32[]{:S(2)}, u32[]{:S(2)}) %collective-permute-start.1) | collective-permute-done | bytes 262176 | tf_op jit(solution)/shard_map/ppermute | solution.py:19
  27.3 7.1 %collective-permute-done.4.refs_5_ = bf16[64,2048]{1,0:T(8,128)(2,1)S(1)} collective-permute-done((bf16[64,2048]{1,0:T(8,128)(2,1)S(1)}, bf16[64,2048]{1,0:T(8,128)(2,1)S(1)}, u32[]{:S(2)}, u32[]{:S(2)}) %collective-permute-start.4) | collective-permute-done | bytes 262176 | tf_op jit(solution)/shard_map/ppermute | solution.py:23
  34.4 5.1 %collective-permute-done.5.refs_6_ = bf16[64,2048]{1,0:T(8,128)(2,1)S(1)} collective-permute-done((bf16[64,2048]{1,0:T(8,128)(2,1)S(1)}, bf16[64,2048]{1,0:T(8,128)(2,1)S(1)}, u32[]{:S(2)}, u32[]{:S(2)}) %collective-permute-start.5) | collective-permute-done | bytes 262176 | tf_op jit(solution)/shard_map/ppermute | solution.py:23
  41.2 8.5 %collective-permute-done.10.refs_1_ = bf16[1024,512]{1,0:T(8,128)(2,1)} collective-permute-done((bf16[1024,512]{1,0:T(8,128)(2,1)}, bf16[1024,512]{1,0:T(8,128)(2,1)}, u32[]{:S(2)}, u32[]{:S(2)}) %collective-permute-start.10) | collective-permute-done | bytes 1048608 | tf_op jit(solution)/shard_map/ppermute | solution.py:19
  64.2 5.8 %gate.1.gate_ref = f32[512,1024]{1,0:T(8,128)} custom-call(bf16[512,2048]{1,0:T(8,128)(2,1)} %get-tuple-element.26.tok_ref, bf16[2048,1024]{1,0:T(8,128)(2,1)} %bitcast.32), custom_call_target="tpu_custom_call" | custom-call | flops 2147483648 | bytes 8388608 | tf_op jit(solution)/shard_map/gate/pallas_call | solution.py:88
  71.3 6.6 %up.1.up_ref = f32[512,1024]{1,0:T(8,128)} custom-call(s32[4]{0:T(128)} %pad_add_fusion.place, bf16[512,2048]{1,0:T(8,128)(2,1)} %get-tuple-element.26.tok_ref, bf16[512,1024]{1,0:T(8,128)(2,1)} %refs_0_.7, bf16[512,1024]{1,0:T(8,128)(2,1)} %collective-permute-done.7.refs_1_, bf16[512,1024]{1,0:T(8,128)(2,1)} %collective-permute-done.8.refs_2_, ...), custom_call_target="tpu_custom_call" | custom-call | flops 2147483648 | bytes 8388608 | tf_op jit(solution)/shard_map/up/pallas_call | solution.py:115
  77.8 9.3 %share.1 = (bf16[256,2048]{1,0:T(8,128)(2,1)}, bf16[64,2048]{1,0:T(8,128)(2,1)}, bf16[64,2048]{1,0:T(8,128)(2,1)}, bf16[64,2048]{1,0:T(8,128)(2,1)}, bf16[64,2048]{1,0:T(8,128)(2,1)}) custom-call(s32[4]{0:T(128)} %pad_add_fusion.place, f32[512,1024]{1,0:T(8,128)} %gate.1.gate_ref, f32[512,1024]{1,0:T(8,128)} %up.1.up_ref, bf16[1024,512]{1,0:T(8,128)(2,1)} %refs_0_.13, ...), custom_call_target="tpu_custom_call" | custom-call | flops 2147483648 | bytes 10485760 | tf_op jit(solution)/shard_map/share/pallas_call | solution.py:172
  87.1 34.7 %collective-permute-done.33.left_ref = bf16[256,1024]{1,0:T(8,128)(2,1)} collective-permute-done((bf16[256,1024]{1,0:T(8,128)(2,1)}, bf16[256,1024]{1,0:T(8,128)(2,1)}, u32[]{:S(2)}, u32[]{:S(2)}) %collective-permute-start.33) | collective-permute-done | bytes 524320 | tf_op jit(solution)/shard_map/ppermute | solution.py:19
  131.5 19.3 %collective-permute-done.23.right_ref = bf16[2048,256]{1,0:T(8,128)(2,1)} collective-permute-done((bf16[2048,256]{1,0:T(8,128)(2,1)}, bf16[2048,256]{1,0:T(8,128)(2,1)}, u32[]{:S(2)}, u32[]{:S(2)}) %collective-permute-start.23) | collective-permute-done | bytes 1048608 | tf_op jit(solution)/shard_map/ppermute | solution.py:19
  154.4 7.6 %collective-permute-done.21.right_ref = bf16[2048,256]{1,0:T(8,128)(2,1)} collective-permute-done((bf16[2048,256]{1,0:T(8,128)(2,1)}, bf16[2048,256]{1,0:T(8,128)(2,1)}, u32[]{:S(2)}, u32[]{:S(2)}) %collective-permute-start.21) | collective-permute-done | bytes 1048608 | tf_op jit(solution)/shard_map/ppermute | solution.py:19
  181.7 13.0 %fresh.3 = (bf16[2048,1024]{1,0:T(8,128)(2,1)}, f32[512,1024]{1,0:T(8,128)}, f32[4,512,512]{2,1,0:T(8,128)}) custom-call(s32[4]{0:T(128)} %pad_add_fusion.place, f32[4]{0:T(128)} %pad_maximum_fusion.coef, bf16[512,2048]{1,0:T(8,128)(2,1)} %get-tuple-element.26.tok_ref, bf16[2048,1024]{1,0:T(8,128)(2,1)} %bitcast.33, ...), custom_call_target="tpu_custom_call" | custom-call | flops 2147483648 | bytes 16777216 | tf_op jit(solution)/shard_map/fresh/pallas_call | solution.py:231
  194.8 9.0 %fresh.4 = (bf16[2048,1024]{1,0:T(8,128)(2,1)}, f32[512,1024]{1,0:T(8,128)}, f32[4,512,512]{2,1,0:T(8,128)}) custom-call(s32[4]{0:T(128)} %pad_add_fusion.place, f32[4]{0:T(128)} %pad_maximum_fusion.coef, bf16[512,2048]{1,0:T(8,128)(2,1)} %get-tuple-element.26.tok_ref, bf16[2048,1024]{1,0:T(8,128)(2,1)} %bitcast.34, ...), custom_call_target="tpu_custom_call", output_to_operand_aliasing={{0}: (13, {}), {1}: (14, {})} | custom-call | flops 1073741824 | bytes 11534336 | tf_op jit(solution)/shard_map/fresh/pallas_call | solution.py:231
  207.2 8.4 %fresh.5 = (bf16[2048,1024]{1,0:T(8,128)(2,1)}, f32[512,1024]{1,0:T(8,128)}, bf16[256,2048]{1,0:T(8,128)(2,1)}, bf16[64,2048]{1,0:T(8,128)(2,1)}, bf16[64,2048]{...) custom-call(s32[4]{0:T(128)} %pad_add_fusion.place, ...), custom_call_target="tpu_custom_call", output_to_operand_aliasing={{0}: (13, {}), {1}: (14, {})} | custom-call | flops 1073741824 | bytes 11534336 | tf_op jit(solution)/shard_map/fresh/pallas_call | solution.py:231
  218.2 7.0 %collective-permute-done.42.other_ref = bf16[64,2048]{1,0:T(8,128)(2,1)} collective-permute-done((bf16[64,2048]{1,0:T(8,128)(2,1)}, bf16[64,2048]{1,0:T(8,128)(2,1)}, u32[]{:S(2)}, u32[]{:S(2)}) %collective-permute-start.42) | collective-permute-done | bytes 262176 | tf_op jit(solution)/shard_map/ppermute | solution.py:23
  225.6 5.1 %collective-permute-done.44.other_ref = bf16[64,2048]{1,0:T(8,128)(2,1)} collective-permute-done((bf16[64,2048]{1,0:T(8,128)(2,1)}, bf16[64,2048]{1,0:T(8,128)(2,1)}, u32[]{:S(2)}, u32[]{:S(2)}) %collective-permute-start.44) | collective-permute-done | bytes 262176 | tf_op jit(solution)/shard_map/ppermute | solution.py:23
  253.0 4.5 %collective-permute-done.28.refs_7_ = bf16[64,2048]{1,0:T(8,128)(2,1)S(1)} collective-permute-done((bf16[64,2048]{1,0:T(8,128)(2,1)}, bf16[64,2048]{1,0:T(8,128)(2,1)S(1)}, u32[]{:S(2)}, u32[]{:S(2)}) %collective-permute-start.28) | collective-permute-done | bytes 262176 | tf_op jit(solution)/shard_map/ppermute | solution.py:19
  262.3 17.6 %collective-permute-done.45 = bf16[64,2048]{1,0:T(8,128)(2,1)S(1)} collective-permute-done((bf16[64,2048]{1,0:T(8,128)(2,1)}, bf16[64,2048]{1,0:T(8,128)(2,1)S(1)}, u32[]{:S(2)}, u32[]{:S(2)}) %collective-permute-start.45) | collective-permute-done | bytes 262176 | tf_op jit(solution)/shard_map/ppermute | solution.py:19
  284.1 5.2 %collective-permute-done.31.refs_10_ = bf16[64,2048]{1,0:T(8,128)(2,1)S(1)} collective-permute-done((bf16[64,2048]{1,0:T(8,128)(2,1)}, bf16[64,2048]{1,0:T(8,128)(2,1)S(1)}, u32[]{:S(2)}, u32[]{:S(2)}) %collective-permute-start.31) | collective-permute-done | bytes 262176 | tf_op jit(solution)/shard_map/ppermute | solution.py:23
  295.9 8.8 %collective-permute-done.49.refs_6_ = bf16[64,2048]{1,0:T(8,128)(2,1)} collective-permute-done((bf16[64,2048]{1,0:T(8,128)(2,1)}, bf16[64,2048]{1,0:T(8,128)(2,1)}, u32[]{:S(2)}, u32[]{:S(2)}) %collective-permute-start.49) | collective-permute-done | bytes 262176 | tf_op jit(solution)/shard_map/ppermute | solution.py:19
  306.7 7.5 %dgate.2.old_ref = bf16[512,1024]{1,0:T(8,128)(2,1)} custom-call(s32[4]{0:T(128)} %pad_add_fusion.place, f32[512,1024]{1,0:T(8,128)} %gate.1.gate_ref, f32[512,1024]{1,0:T(8,128)} %up.1.up_ref, bf16[1024,512]{1,0:T(8,128)(2,1)} %refs_0_.13, bf16[1024,512]{1,0:T(8,128)(2,1)} %collective-permute-done.10.refs_1_, ...), custom_call_target="tpu_custom_call" | custom-call | flops 2147483648 | bytes 11534336 | tf_op jit(solution)/shard_map/dgate/pallas_call | solution.py:308
  320.2 4.0 %base.5.rest_0_ = f32[1792,1024]{1,0:T(8,128)} custom-call(f32[4]{0:T(128)} %pad_maximum_fusion.coef, bf16[2048,512]{1,0:T(8,128)(2,1)} %get-tuple-element.40.turned_ref, bf16[512,1024]{1,0:T(8,128)(2,1)} %dgate.2.old_ref, bf16[2048,1024]{1,0:T(8,128)(2,1)} %bitcast.27, ...), custom_call_target="tpu_custom_call", output_to_operand_aliasing={{}: (6, {})} | custom-call | flops 536870912 | bytes 5242880 | tf_op jit(solution)/shard_map/base/pallas_call | solution.py:359
  324.3 4.1 %base.6.rest_0_ = f32[1792,1024]{1,0:T(8,128)} custom-call(f32[4]{0:T(128)} %pad_maximum_fusion.coef, bf16[2048,512]{1,0:T(8,128)(2,1)} %get-tuple-element.40.turned_ref, bf16[512,1024]{1,0:T(8,128)(2,1)} %dgate.2.old_ref, bf16[2048,1024]{1,0:T(8,128)(2,1)} %bitcast.28, ...), custom_call_target="tpu_custom_call", output_to_operand_aliasing={{}: (6, {})} | custom-call | flops 536870912 | bytes 5242880 | tf_op jit(solution)/shard_map/base/pallas_call | solution.py:359
  331.7 14.0 %dgate.3 = (bf16[512,1024]{1,0:T(8,128)(2,1)}, bf16[2048,1024]{1,0:T(8,128)(2,1)}) custom-call(s32[4]{0:T(128)} %pad_add_fusion.place, bf16[2048,512]{1,0:T(8,128)(2,1)} %get-tuple-element.40.turned_ref, f32[1792,1024]{1,0:T(8,128)} %base.7.base_ref, f32[512,1024]{1,0:T(8,128)} %get-tuple-element.42.gate_ref, f32[512,1024]{1,0:T(8,128)} %up.1.up_ref, ...), custom_call_target="tpu_custom_call" | custom-call | flops 4294967296 | bytes 15728640 | tf_op jit(solution)/shard_map/dgate/pallas_call | solution.py:308
  (147 shorter events, 120.9 us)
Async XLA Ops:
  0.6 40.4 %collective-permute-start.7 = (bf16[512,1024]{1,0:T(8,128)(2,1)}, bf16[512,1024]{1,0:T(8,128)(2,1)}, u32[]{:S(2)}, u32[]{:S(2)}) collective-permute-start(bf16[512,1024]{1,0:T(8,128)(2,1)} %refs_0_.7), channel_id=1, source_target_pairs={{0,16},{8,24},{16,0},{24,8},{1,17},{9,25},{17,1},{25,9},{2,18},{10... | collective-permute-start | bytes 3145736 | tf_op jit(solution)/shard_map/ppermute | solution.py:19
  3.7 45.9 %collective-permute-start.10 = (bf16[1024,512]{1,0:T(8,128)(2,1)}, bf16[1024,512]{1,0:T(8,128)(2,1)}, u32[]{:S(2)}, u32[]{:S(2)}) collective-permute-start(bf16[1024,512]{1,0:T(8,128)(2,1)} %refs_0_.13), channel_id=1, source_target_pairs={{0,16},{8,24},{16,0},{24,8},{1,17},{9,25},{17,1},{25,9},{2,18},{10... | collective-permute-start | bytes 3145736 | tf_op jit(solution)/shard_map/ppermute | solution.py:19
  25.1 30.3 %collective-permute-start.8 = (bf16[512,1024]{1,0:T(8,128)(2,1)}, bf16[512,1024]{1,0:T(8,128)(2,1)}, u32[]{:S(2)}, u32[]{:S(2)}) collective-permute-start(bf16[512,1024]{1,0:T(8,128)(2,1)} %refs_0_.7), channel_id=1, source_target_pairs={{0,8},{8,0},{16,24},{24,16},{1,9},{9,1},{17,25},{25,17},{2,10},{10... | collective-permute-start | bytes 3145736 | tf_op jit(solution)/shard_map/ppermute | solution.py:23
  34.4 29.3 %collective-permute-start.11 = (bf16[1024,512]{1,0:T(8,128)(2,1)}, bf16[1024,512]{1,0:T(8,128)(2,1)}, u32[]{:S(2)}, u32[]{:S(2)}) collective-permute-start(bf16[1024,512]{1,0:T(8,128)(2,1)} %refs_0_.13), channel_id=1, source_target_pairs={{0,8},{8,0},{16,24},{24,16},{1,9},{9,1},{17,25},{25,17},{2,10},{10... | collective-permute-start | bytes 3145736 | tf_op jit(solution)/shard_map/ppermute | solution.py:23
  41.1 28.9 %collective-permute-start.9 = (bf16[512,1024]{1,0:T(8,128)(2,1)}, bf16[512,1024]{1,0:T(8,128)(2,1)}, u32[]{:S(2)}, u32[]{:S(2)}) collective-permute-start(bf16[512,1024]{1,0:T(8,128)(2,1)} %collective-permute-done.7.refs_1_), channel_id=1, source_target_pairs={{0,8},{8,0},{16,24},{24,16},{1,9},{9,1},{17,25},{25,17},{2,10},{10... | collective-permute-start | bytes 3145736 | tf_op jit(solution)/shard_map/ppermute | solution.py:23
  54.9 108.8 %collective-permute-start.24 = (bf16[2048,512]{1,0:T(8,128)(2,1)}, bf16[2048,512]{1,0:T(8,128)(2,1)}, u32[]{:S(2)}, u32[]{:S(2)}) collective-permute-start(bf16[2048,512]{1,0:T(8,128)(2,1)} %slice.62), channel_id=1, source_target_pairs={{0,8},{8,16},{16,24},{24,0},{1,9},{9,17},{17,25},{25,1},{2,10},{10... | collective-permute-start | bytes 6291464 | tf_op jit(solution)/shard_map/ppermute | solution.py:19
  55.4 71.7 %collective-permute-start.22 = (bf16[2048,256]{1,0:T(8,128)(2,1)}, bf16[2048,256]{1,0:T(8,128)(2,1)}, u32[]{:S(2)}, u32[]{:S(2)}) collective-permute-start(bf16[2048,256]{1,0:T(8,128)(2,1)} %get-tuple-element.55), channel_id=1, source_target_pairs={{0,8},{8,16},{16,24},{24,0},{1,9},{9,17},{17,25},{25,1},{2,10},{10... | collective-permute-start | bytes 3145736 | tf_op jit(solution)/shard_map/ppermute | solution.py:19
  63.7 58.1 %collective-permute-start.33 = (bf16[256,1024]{1,0:T(8,128)(2,1)}, bf16[256,1024]{1,0:T(8,128)(2,1)}, u32[]{:S(2)}, u32[]{:S(2)}) collective-permute-start(bf16[256,1024]{1,0:T(8,128)(2,1)} %get-tuple-element.51), channel_id=1, source_target_pairs={{0,8},{8,16},{16,24},{24,0},{1,9},{9,17},{17,25},{25,1},{2,10},{10... | collective-permute-start | bytes 1572872 | tf_op jit(solution)/shard_map/ppermute | solution.py:19
  70.0 110.7 %collective-permute-start.25 = (bf16[2048,512]{1,0:T(8,128)(2,1)}, bf16[2048,512]{1,0:T(8,128)(2,1)}, u32[]{:S(2)}, u32[]{:S(2)}) collective-permute-start(bf16[2048,512]{1,0:T(8,128)(2,1)} %slice.62), channel_id=1, source_target_pairs={{0,24},{8,0},{16,8},{24,16},{1,25},{9,1},{17,9},{25,17},{2,26},{10... | collective-permute-start | bytes 6291464 | tf_op jit(solution)/shard_map/ppermute | solution.py:19
  71.2 53.7 %collective-permute-start.34 = (bf16[256,1024]{1,0:T(8,128)(2,1)}, bf16[256,1024]{1,0:T(8,128)(2,1)}, u32[]{:S(2)}, u32[]{:S(2)}) collective-permute-start(bf16[256,1024]{1,0:T(8,128)(2,1)} %get-tuple-element.51), channel_id=1, source_target_pairs={{0,24},{8,0},{16,8},{24,16},{1,25},{9,1},{17,9},{25,17},{2,26},{10... | collective-permute-start | bytes 1572872 | tf_op jit(solution)/shard_map/ppermute | solution.py:19
  129.7 32.4 %collective-permute-start.21 = (bf16[2048,256]{1,0:T(8,128)(2,1)}, bf16[2048,256]{1,0:T(8,128)(2,1)}, u32[]{:S(2)}, u32[]{:S(2)}) collective-permute-start(bf16[2048,256]{1,0:T(8,128)(2,1)} %get-tuple-element.56), channel_id=1, source_target_pairs={{0,24},{8,0},{16,8},{24,16},{1,25},{9,1},{17,9},{25,17},{2,26},{10... | collective-permute-start | bytes 3145736 | tf_op jit(solution)/shard_map/ppermute | solution.py:19
  170.9 44.7 %collective-permute-start.39 = (bf16[512,1024]{1,0:T(8,128)(2,1)}, bf16[512,1024]{1,0:T(8,128)(2,1)}, u32[]{:S(2)}, u32[]{:S(2)}) collective-permute-start(bf16[512,1024]{1,0:T(8,128)(2,1)} %get-tuple-element.52), channel_id=1, source_target_pairs={{0,8},{8,16},{16,24},{24,0},{1,9},{9,17},{17,25},{25,1},{2,10},{10... | collective-permute-start | bytes 3145736 | tf_op jit(solution)/shard_map/ppermute | solution.py:19
  171.5 44.7 %collective-permute-start.40 = (bf16[512,1024]{1,0:T(8,128)(2,1)}, bf16[512,1024]{1,0:T(8,128)(2,1)}, u32[]{:S(2)}, u32[]{:S(2)}) collective-permute-start(bf16[512,1024]{1,0:T(8,128)(2,1)} %get-tuple-element.52), channel_id=1, source_target_pairs={{0,24},{8,0},{16,8},{24,16},{1,25},{9,1},{17,9},{25,17},{2,26},{10... | collective-permute-start | bytes 3145736 | tf_op jit(solution)/shard_map/ppermute | solution.py:19
  180.7 37.0 %collective-permute-start.37 = (bf16[512,1024]{1,0:T(8,128)(2,1)}, bf16[512,1024]{1,0:T(8,128)(2,1)}, u32[]{:S(2)}, u32[]{:S(2)}) collective-permute-start(bf16[512,1024]{1,0:T(8,128)(2,1)} %get-tuple-element.53), channel_id=1, source_target_pairs={{0,8},{8,16},{16,24},{24,0},{1,9},{9,17},{17,25},{25,1},{2,10},{10... | collective-permute-start | bytes 3145736 | tf_op jit(solution)/shard_map/ppermute | solution.py:19
  203.8 40.2 %collective-permute-start.38 = (bf16[512,1024]{1,0:T(8,128)(2,1)}, bf16[512,1024]{1,0:T(8,128)(2,1)}, u32[]{:S(2)}, u32[]{:S(2)}) collective-permute-start(bf16[512,1024]{1,0:T(8,128)(2,1)} %get-tuple-element.53), channel_id=1, source_target_pairs={{0,24},{8,0},{16,8},{24,16},{1,25},{9,1},{17,9},{25,17},{2,26},{10... | collective-permute-start | bytes 3145736 | tf_op jit(solution)/shard_map/ppermute | solution.py:19
  204.9 41.7 %collective-permute-start.35 = (bf16[512,1024]{1,0:T(8,128)(2,1)}, bf16[512,1024]{1,0:T(8,128)(2,1)}, u32[]{:S(2)}, u32[]{:S(2)}) collective-permute-start(bf16[512,1024]{1,0:T(8,128)(2,1)} %get-tuple-element.54), channel_id=1, source_target_pairs={{0,8},{8,16},{16,24},{24,0},{1,9},{9,17},{17,25},{25,1},{2,10},{10... | collective-permute-start | bytes 3145736 | tf_op jit(solution)/shard_map/ppermute | solution.py:19
  246.7 33.2 %collective-permute-start.45 = (bf16[64,2048]{1,0:T(8,128)(2,1)}, bf16[64,2048]{1,0:T(8,128)(2,1)S(1)}, u32[]{:S(2)}, u32[]{:S(2)}) collective-permute-start(bf16[64,2048]{1,0:T(8,128)(2,1)} %join.10), channel_id=1, source_target_pairs={{0,4},{1,5},{2,6},{3,7},{4,0},{5,1},{6,2},{7,3},{8,12},{9,13},{10,... | collective-permute-start | bytes 786440 | tf_op jit(solution)/shard_map/ppermute | solution.py:19
  247.5 32.9 %collective-permute-start.47 = (bf16[64,2048]{1,0:T(8,128)(2,1)}, bf16[64,2048]{1,0:T(8,128)(2,1)S(1)}, u32[]{:S(2)}, u32[]{:S(2)}) collective-permute-start(bf16[64,2048]{1,0:T(8,128)(2,1)} %join.11), channel_id=1, source_target_pairs={{0,2},{1,3},{2,4},{3,5},{4,6},{5,7},{6,0},{7,1},{8,10},{9,11},{10,... | collective-permute-start | bytes 786440 | tf_op jit(solution)/shard_map/ppermute | solution.py:19
  252.4 65.8 %collective-permute-start.36 = (bf16[512,1024]{1,0:T(8,128)(2,1)}, bf16[512,1024]{1,0:T(8,128)(2,1)}, u32[]{:S(2)}, u32[]{:S(2)}) collective-permute-start(bf16[512,1024]{1,0:T(8,128)(2,1)} %get-tuple-element.54), channel_id=1, source_target_pairs={{0,24},{8,0},{16,8},{24,16},{1,25},{9,1},{17,9},{25,17},{2,26},{10... | collective-permute-start | bytes 3145736 | tf_op jit(solution)/shard_map/ppermute | solution.py:19
  257.5 26.5 %collective-permute-start.29 = (bf16[64,2048]{1,0:T(8,128)(2,1)}, bf16[64,2048]{1,0:T(8,128)(2,1)S(1)}, u32[]{:S(2)}, u32[]{:S(2)}) collective-permute-start(bf16[64,2048]{1,0:T(8,128)(2,1)} %fusion.1.refs_4_), channel_id=1, source_target_pairs={{0,1},{1,0},{2,3},{3,2},{4,5},{5,4},{6,7},{7,6},{8,9},{9,8},{10,11... | collective-permute-start | bytes 786440 | tf_op jit(solution)/shard_map/ppermute | solution.py:23
  295.4 36.3 %collective-permute-start.52 = (bf16[64,2048]{1,0:T(8,128)(2,1)}, bf16[64,2048]{1,0:T(8,128)(2,1)}, u32[]{:S(2)}, u32[]{:S(2)}) collective-permute-start(bf16[64,2048]{1,0:T(8,128)(2,1)} %collective-permute-done.48.refs_5_), channel_id=1, source_target_pairs={{0,1},{1,0},{2,3},{3,2},{4,5},{5,4},{6,7},{7,6},{8,9},{9,8},{10,11... | collective-permute-start | bytes 786440 | tf_op jit(solution)/shard_map/ppermute | solution.py:23
  304.7 27.0 %collective-permute-start.53 = (bf16[64,2048]{1,0:T(8,128)(2,1)}, bf16[64,2048]{1,0:T(8,128)(2,1)}, u32[]{:S(2)}, u32[]{:S(2)}) collective-permute-start(bf16[64,2048]{1,0:T(8,128)(2,1)} %collective-permute-done.49.refs_6_), channel_id=1, source_target_pairs={{0,1},{1,0},{2,3},{3,2},{4,5},{5,4},{6,7},{7,6},{8,9},{9,8},{10,11... | collective-permute-start | bytes 786440 | tf_op jit(solution)/shard_map/ppermute | solution.py:23
  318.2 27.4 %collective-permute-start.55 = (bf16[256,1024]{1,0:T(8,128)(2,1)}, bf16[256,1024]{1,0:T(8,128)(2,1)}, u32[]{:S(2)}, u32[]{:S(2)}) collective-permute-start(bf16[256,1024]{1,0:T(8,128)(2,1)} %get-tuple-element.50), channel_id=1, source_target_pairs={{0,8},{8,16},{16,24},{24,0},{1,9},{9,17},{17,25},{25,1},{2,10},{10... | collective-permute-start | bytes 1572872 | tf_op jit(solution)/shard_map/ppermute | solution.py:19
  318.5 27.2 %collective-permute-start.56 = (bf16[256,1024]{1,0:T(8,128)(2,1)}, bf16[256,1024]{1,0:T(8,128)(2,1)}, u32[]{:S(2)}, u32[]{:S(2)}) collective-permute-start(bf16[256,1024]{1,0:T(8,128)(2,1)} %get-tuple-element.50), channel_id=1, source_target_pairs={{0,24},{8,0},{16,8},{24,16},{1,25},{9,1},{17,9},{25,17},{2,26},{10... | collective-permute-start | bytes 1572872 | tf_op jit(solution)/shard_map/ppermute | solution.py:19
  (47 other events, 783.1 us)

commit v3 on v2

--- a/solution.py
+++ b/solution.py
@@ -1,4 +1,5 @@
 import functools
+import math
 
 import jax
 import jax.numpy as jnp
@@ -10,7 +11,7 @@
 
 F32 = jnp.float32
 BF16 = jnp.bfloat16
-PARTS = (4, 4, 4, 2, 2)
+PARTS = (4, 6, 4, 2)
 VMEM_LIMIT = 67043328
 
 
@@ -52,7 +53,11 @@
 
 
 SMEM = pl.BlockSpec(memory_space=pltpu.SMEM)
-call = functools.partial(pl.pallas_call, compiler_params=pltpu.CompilerParams(vmem_limit_bytes=VMEM_LIMIT))
+ANY = pl.BlockSpec(memory_space=pl.ANY)
+
+
+def call(kernel, **options):
+    return pl.pallas_call(kernel, compiler_params=pltpu.CompilerParams(vmem_limit_bytes=VMEM_LIMIT), **options)
 
 
 def columns(place, i, size):
@@ -124,11 +129,20 @@
     )(place, tok, *pieces)
 
 
-def add_share(place, gate, up_ref, weights, carry, outs, total):
+def add_share(place, gate, up_ref, weights, carry, bring, outs, total):
     hidden = (jax.nn.sigmoid(gate) * gate * up_ref[...]).astype(BF16)
     n, last = pl.program_id(0), pl.num_programs(0) - 1
+    if bring is not None:
+
+        @pl.when(n == 0)
+        def _():
+            bring.wait()
+
     for i, ref in enumerate(weights):
         term = dot(hidden, ref[...])
+        if bring is not None:
+            total[i] += term
+            continue
 
         @pl.when(n == 0)
         def _():
@@ -153,7 +167,7 @@
 
 
 def share_kernel(count, place, gate_ref, up_ref, *refs):
-    add_share(place, gate_ref[...], up_ref, refs[:count], None, refs[count:-1], refs[-1])
+    add_share(place, gate_ref[...], up_ref, refs[:count], None, None, refs[count:-1], refs[-1])
 
 
 def share_outs(rows, depth, pairs):
@@ -183,9 +197,16 @@
 
 def fresh_kernel(count, scale, first, last, place, coef, tok_ref, p_ref, left_ref, right_ref, t_ref, up_ref, *refs):
     weights, refs = refs[:count], refs[count:]
-    carry = None
+    carry = bring = None
     if not first:
         carry, refs = refs[0], refs[3:]
+    if carry is not None and last:
+        bring, refs = pltpu.make_async_copy(carry, refs[-2], refs[-1]), refs[:-1]
+
+        @pl.when(pl.program_id(0) == 0)
+        def _():
+            bring.start()
+
     fresh_ref, gate_ref, *refs = refs
     mixed = (
         coef[0] * p_ref[...].astype(F32)
@@ -196,15 +217,14 @@
     fresh_ref[...] = fresh
     gate = dot(tok_ref[...], fresh) * scale
     gate_ref[...] = gate
-    outs, total = (refs[:-1], refs[-1]) if last else ([], refs[0])
-    add_share(place, gate, up_ref, weights, carry, outs, total)
+    add_share(place, gate, up_ref, weights, carry, bring, refs[:-1], refs[-1])
 
 
 def fresh_of(place, coef, tok, param, left, right, track, up, downs, pairs, scale, start, so_far):
     depth, width = param.shape
     rows, part = tok.shape[0], left.shape[1]
     cols = downs[0].shape[1]
-    block = block_of(part, 256)
+    block = math.gcd(256, start, part)
     base = start // block
     first, last = so_far is None, start + part == width
     there = pl.BlockSpec((depth, block), lambda n: (0, base + n))
@@ -219,13 +239,13 @@
     if not first:
         aliases = {len(operands) + 1: 0, len(operands) + 2: 1}
         operands += [so_far[2], so_far[0], so_far[1]]
-        specs += [whole, pl.BlockSpec(memory_space=pl.ANY), pl.BlockSpec(memory_space=pl.ANY)]
+        specs += [ANY if last else whole, ANY, ANY]
     outs, out_specs = [like((depth, width), BF16), like((rows, width), F32)], [there, hidden]
     scratch = []
     if last:
         more, more_specs = share_outs(rows, cols * len(downs), pairs)
         outs, out_specs = outs + more, out_specs + more_specs
-        scratch = [pltpu.VMEM(total, F32)]
+        scratch = [pltpu.VMEM(total, F32)] + ([] if first else [pltpu.SemaphoreType.DMA(())])
     else:
         outs, out_specs = outs + [like(total, F32)], out_specs + [whole]
     return call(
@@ -281,11 +301,25 @@
     refs[-2][...] = dgate_block(count, place, gate_ref, up_ref, refs[:-2], refs[-1])
 
 
-def tail_kernel(count, scale, place, turned_ref, base_ref, gate_ref, up_ref, *refs):
-    *refs, dgate_ref, out_ref, err = refs
+def tail_kernel(count, scale, place, turned_hbm, base_ref, gate_ref, up_ref, *refs):
+    *refs, out_ref, late_ref, err, turned, turned_sem = refs
+    bring_turned = pltpu.make_async_copy(turned_hbm, turned, turned_sem)
+    first = pl.program_id(0) == 0
+
+    @pl.when(first)
+    def _():
+        bring_turned.start()
+
     value = dgate_block(count, place, gate_ref, up_ref, refs, err)
-    dgate_ref[...] = value
-    out_ref[...] = (base_ref[...] + dot(turned_ref[...], value) * scale).astype(BF16)
+
+    @pl.when(first)
+    def _():
+        bring_turned.wait()
+
+    rows = out_ref.shape[0]
+    total = base_ref[...] + dot(turned[...], value) * scale
+    out_ref[...] = total[:rows].astype(BF16)
+    late_ref[...] = total[rows:]
 
 
 def dgate_of(place, gate, up, downs, pieces, more=None):
@@ -295,15 +329,17 @@
     hidden = pl.BlockSpec((rows, block), lambda n: (0, n))
     whole = pl.BlockSpec(pieces[0].shape, lambda n: (0, 0))
     depth = cols * len(downs)
-    operands, specs = [place], [SMEM]
+    operands, specs, scratch = [place], [SMEM], [pltpu.VMEM((rows, depth), BF16)]
     outs, out_specs = [like((rows, width), BF16)], [hidden]
     kernel, flops = functools.partial(dgate_kernel, len(downs)), 2 * rows * width * depth
     if more is not None:
-        turned, base, out, scale = more
-        tall = pl.BlockSpec((base.shape[0], block), lambda n: (0, n))
+        turned, base, out, done, scale = more
+        tall = base.shape[0]
         operands += [turned, base]
-        specs += [pl.BlockSpec((base.shape[0], rows), lambda n: (0, 0)), tall]
-        outs, out_specs = outs + [out], out_specs + [tall]
+        specs += [ANY, pl.BlockSpec((tall, block), lambda n: (0, n))]
+        scratch += [pltpu.VMEM(turned.shape, turned.dtype), pltpu.SemaphoreType.DMA(())]
+        outs = [out, like((tall - done, width), F32)]
+        out_specs = [pl.BlockSpec((size, block), lambda n: (0, n)) for size in (done, tall - done)]
         kernel, flops = functools.partial(tail_kernel, len(downs), scale), 2 * flops
     return call(
         kernel,
@@ -314,58 +350,67 @@
         + [whole] * len(pieces),
         out_specs=out_specs,
         out_shape=outs,
-        scratch_shapes=[pltpu.VMEM((rows, depth), BF16)],
+        scratch_shapes=scratch,
         cost_estimate=cost(flops, gate, up, *outs, *downs, *pieces),
         name="dgate",
     )(*operands, gate, up, *downs, *pieces)
 
 
-def base_kernel(scale, coef, turned_ref, old_ref, t_ref, left_ref, right_ref, *rest):
-    mixed = (
-        coef[0] * t_ref[...].astype(F32)
-        + coef[1] * right_ref[...].astype(F32)
-        + coef[2] * left_ref[...].astype(F32)
-    )
+def base_kernel(scale, coef, turned_ref, old_ref, t_ref, *rest):
+    mixed = coef[0] * t_ref[...].astype(F32)
+    if len(rest) > 2:
+        mixed = mixed + coef[1] * rest[1][...].astype(F32) + coef[2] * rest[0][...].astype(F32)
     rest[-1][...] = mixed - dot(turned_ref[...], old_ref[...]) * scale
 
 
-def last_kernel(scale, coef, turned_ref, new_ref, old_ref, t_ref, left_ref, right_ref, *rest):
-    turned = turned_ref[...]
-    change = dot(turned, new_ref[...]) - dot(turned, old_ref[...])
-    mixed = (
-        coef[0] * t_ref[...].astype(F32)
-        + coef[1] * right_ref[...].astype(F32)
-        + coef[2] * left_ref[...].astype(F32)
-    )
-    rest[-1][...] = (mixed + change * scale).astype(BF16)
-
-
-def part_call(kernel, coef, turned, grads, track, left, right, start, out, so_far, name):
-    width = track.shape[1]
-    rows, part = turned.shape[1], left.shape[0]
-    step = block_of(part, 256)
+def base_of(coef, turned, old, track, sides, start, part, so_far, scale):
+    depth, width = track.shape
+    rows = turned.shape[1]
+    step = math.gcd(256, start, part)
     base = start // step
     there = pl.BlockSpec((step, width), lambda k: (base + k, 0))
     here = pl.BlockSpec((step, width), lambda k: (k, 0))
-    whole = pl.BlockSpec((rows, width), lambda k: (0, 0))
-    operands = [coef, turned, *grads, track, left, right]
+    operands = [coef, turned, old, track, *sides]
     specs = [SMEM, pl.BlockSpec((step, rows), lambda k: (base + k, 0))]
-    specs += [whole] * len(grads) + [there, here, here]
+    specs += [pl.BlockSpec((rows, width), lambda k: (0, 0)), there] + [here] * len(sides)
     aliases = {}
     if so_far is not None:
         aliases = {len(operands): 0}
         operands.append(so_far)
-        specs.append(pl.BlockSpec(memory_space=pl.ANY))
-    return call(
-        kernel,
+        specs.append(ANY)
+    return call(
+        functools.partial(base_kernel, scale),
         grid=(part // step,),
         in_specs=specs,
         out_specs=there,
-        out_shape=out,
+        out_shape=like((depth, width), F32),
         input_output_aliases=aliases,
-        cost_estimate=cost(2 * len(grads) * rows * part * width, left, right, left, left, *grads),
-        name=name,
+        cost_estimate=cost(2 * rows * part * width, like((part, width), F32), old, *sides),
+        name="base",
     )(*operands)
+
+
+def last_kernel(coef, late_ref, left_ref, right_ref, so_far, out_ref):
+    mixed = coef[1] * right_ref[...].astype(F32) + coef[2] * left_ref[...].astype(F32)
+    out_ref[...] = (late_ref[...] + mixed).astype(BF16)
+
+
+def last_of(coef, late, left, right, out):
+    part, width = late.shape
+    start = out.shape[0] - part
+    step = math.gcd(128, start, part)
+    base = start // step
+    here = pl.BlockSpec((step, width), lambda k: (k, 0))
+    return call(
+        last_kernel,
+        grid=(part // step,),
+        in_specs=[SMEM, here, here, here, ANY],
+        out_specs=pl.BlockSpec((step, width), lambda k: (base + k, 0)),
+        out_shape=like(out.shape, BF16),
+        input_output_aliases={4: 0},
+        cost_estimate=cost(late.size, late, left, right, left),
+        name="last",
+    )(coef, late, left, right, out)
 
 
 def spread(piece, axis, pairs):
@@ -416,7 +461,7 @@
         order = list(range(1, pairs)) + [0]
         sent = {j: paired(far[j], "tp") for j in order}
         summed = []
-        for j in range(1, pairs):
+        for j in order[:-1]:
             value = join(near, sent[j], j)
             summed.append(jumped(value, "tp", -j))
         total = near[:piece].astype(F32) + sent[0].astype(F32)
@@ -439,15 +484,13 @@
     new_pieces = errors(shares)
     (old,) = dgate_of(place, gate, up, downs, old_pieces)
     base = None
-    early_like, all_like = like((starts[-1], track.shape[1]), F32), like(track.shape, BF16)
-    for c in range(len(PARTS) - 1):
-        kernel = functools.partial(base_kernel, scale)
-        base = part_call(kernel, coef, turned, [old], track, *around[c], starts[c], early_like, base, "base")
-    new, out = dgate_of(place, new_gate, up, downs, new_pieces, (turned, base, all_like, scale))
-    kernel = functools.partial(last_kernel, scale)
-    out = part_call(
-        kernel, coef, turned, [new, old], track, *around[-1], starts[-1], all_like, out, "last"
-    )
+    final = len(PARTS) - 1
+    for c in [final] + list(range(final)):
+        sides_y = () if c == final else around[c]
+        base = base_of(coef, turned, old, track, sides_y, starts[c], ends[c] - starts[c], base, scale)
+    more = (turned, base, like(track.shape, BF16), starts[final], scale)
+    out, late = dgate_of(place, new_gate, up, downs, new_pieces, more)
+    out = last_of(coef, late, *around[final], out)
     return (fresh[None], out[None])
 
 

time: 351 us -> 348 us (level); the launches traced: 349 us -> 341 us
  waiting for transfers between devices: 161 us -> 148 us
    ppermute x33 -> x31, waiting for transfers between devices: 125 us -> 99.4 us  [shifted(): lax.ppermute(value, axis, [(source, (source + shift) % count) for source...]
    ppermute x24, waiting for transfers between devices: 35.9 us -> 48.4 us  [paired(): lax.ppermute(value, axis, [(source, source ^ 1) for source in range(lax.a...]
    slice x2 -> x3, local copies, waits for them, and re-layouts: 5.87 us -> 7.65 us  [on_device(): t = track[start:end]]
    ppermute x33 -> x31, starting transfers between devices: 38.6 us -> 39.3 us  [shifted(): lax.ppermute(value, axis, [(source, (source + shift) % count) for source...]
  transfers between devices with their start and end apart: 57 -> 55, of which waited for: 22 -> 21; matrix products, arithmetic and copies ran while one was open for 5% -> 6% of each run, Pallas kernels for 30% -> 31%
where the time goes in v3:
time: 348 us; the launch traced here: 341 us
  waiting for transfers between devices  148 us (43%)
  Pallas kernels  109 us (31%)
  starting transfers between devices  60.8 us (17%)
  local copies, waits for them, and re-layouts  14.4 us (4%)
  other arithmetic  6.87 us (2%)
    ppermute x31, waiting for transfers between devices, shifted(): lax.ppermute(value, axis, [(source, (source + shift) % count) for source...  99.4 us
    ppermute x24, waiting for transfers between devices, paired(): lax.ppermute(value, axis, [(source, source ^ 1) for source in range(lax.a...  48.4 us
    ppermute x31, starting transfers between devices, shifted(): lax.ppermute(value, axis, [(source, (source + shift) % count) for source...  39.3 us
    pallas_call x3, Pallas kernels, fresh_of(): call(functools.partial(fresh_kernel, len(downs), scale, first, last), gri...  30.1 us
    pallas_call x2, Pallas kernels, dgate_of(): call(kernel, grid=(width // block,), in_specs=specs + [hidden, hidden] +...  22.4 us
    ppermute x24, starting transfers between devices, paired(): lax.ppermute(value, axis, [(source, source ^ 1) for source in range(lax.a...  21.5 us
    pallas_call x4, Pallas kernels, base_of(): call(functools.partial(base_kernel, scale), grid=(part // step,), in_spec...  17.3 us
    pallas_call x6, Pallas kernels, join(): call(join_kernel, grid=(1,), in_specs=[pl.BlockSpec(other.shape, lambda i...  10.8 us
  transfers between devices with their start and end apart: 55, of which 21 were waited for; matrix products, arithmetic and copies ran while one was open for 6% of the time, Pallas kernels for 31%

profile of v3, /device:TPU:0, one launch (start us, length us, event | category | flops | bytes accessed | tf_op | source)
XLA Modules:
  0.0 341.3 jit_solution(9762165388541506099)
XLA Ops:
  9.7 5.6 %collective-permute-done.refs_1_ = bf16[64,2048]{1,0:T(8,128)(2,1)S(1)} collective-permute-done((bf16[64,2048]{1,0:T(8,128)(2,1)}, bf16[64,2048]{1,0:T(8,128)(2,1)S(1)}, u32[]{:S(2)}, u32[]{:S(2)}) %collective-permute-start) | collective-permute-done | bytes 262176 | tf_op jit(solution)/shard_map/ppermute | solution.py:20
  17.1 8.1 %collective-permute-done.1.refs_2_ = bf16[64,2048]{1,0:T(8,128)(2,1)S(1)} collective-permute-done((bf16[64,2048]{1,0:T(8,128)(2,1)}, bf16[64,2048]{1,0:T(8,128)(2,1)S(1)}, u32[]{:S(2)}, u32[]{:S(2)}) %collective-permute-start.1) | collective-permute-done | bytes 262176 | tf_op jit(solution)/shard_map/ppermute | solution.py:20
  30.1 7.1 %collective-permute-done.4.refs_5_ = bf16[64,2048]{1,0:T(8,128)(2,1)S(1)} collective-permute-done((bf16[64,2048]{1,0:T(8,128)(2,1)S(1)}, bf16[64,2048]{1,0:T(8,128)(2,1)S(1)}, u32[]{:S(2)}, u32[]{:S(2)}) %collective-permute-start.4) | collective-permute-done | bytes 262176 | tf_op jit(solution)/shard_map/ppermute | solution.py:24
  37.2 5.4 %collective-permute-done.5.refs_6_ = bf16[64,2048]{1,0:T(8,128)(2,1)S(1)} collective-permute-done((bf16[64,2048]{1,0:T(8,128)(2,1)S(1)}, bf16[64,2048]{1,0:T(8,128)(2,1)S(1)}, u32[]{:S(2)}, u32[]{:S(2)}) %collective-permute-start.5) | collective-permute-done | bytes 262176 | tf_op jit(solution)/shard_map/ppermute | solution.py:24
  44.4 5.3 %collective-permute-done.10.refs_1_ = bf16[1024,512]{1,0:T(8,128)(2,1)} collective-permute-done((bf16[1024,512]{1,0:T(8,128)(2,1)}, bf16[1024,512]{1,0:T(8,128)(2,1)}, u32[]{:S(2)}, u32[]{:S(2)}) %collective-permute-start.10) | collective-permute-done | bytes 1048608 | tf_op jit(solution)/shard_map/ppermute | solution.py:20
  62.6 5.8 %gate.1.gate_ref = f32[512,1024]{1,0:T(8,128)} custom-call(bf16[512,2048]{1,0:T(8,128)(2,1)} %get-tuple-element.26.tok_ref, bf16[2048,1024]{1,0:T(8,128)(2,1)} %bitcast.29), custom_call_target="tpu_custom_call" | custom-call | flops 2147483648 | bytes 8388608 | tf_op jit(solution)/shard_map/gate/pallas_call | solution.py:93
  68.3 6.6 %up.1.up_ref = f32[512,1024]{1,0:T(8,128)} custom-call(s32[4]{0:T(128)} %pad_add_fusion.place, bf16[512,2048]{1,0:T(8,128)(2,1)} %get-tuple-element.26.tok_ref, bf16[512,1024]{1,0:T(8,128)(2,1)} %refs_0_.7, bf16[512,1024]{1,0:T(8,128)(2,1)} %copy-done.1, bf16[512,1024]{1,0:T(8,128)(2,1)} %copy-done.2, bf16[512,1024]{1,0:T(8,128)(2,1)} %copy-done.3), custom_call_target="tpu_custom_call" | custom-call | flops 2147483648 | bytes 8388608 | tf_op jit(solution)/shard_map/up/pallas_call | solution.py:120
  74.9 9.4 %share.1 = (bf16[256,2048]{1,0:T(8,128)(2,1)}, bf16[64,2048]{1,0:T(8,128)(2,1)}, bf16[64,2048]{1,0:T(8,128)(2,1)}, bf16[64,2048]{1,0:T(8,128)(2,1)}, bf16[64,2048]{1,0:T(8,128)(2,1)}) custom-call(s32[4]{0:T(128)} %pad_add_fusion.place, f32[512,1024]{1,0:T(8,128)} %gate.1.gate_ref, f32[512,1024]{1,0:T(8,128)} %up.1.up_ref, bf16[1024,512]{1,0:T(8,128)(2,1)} %refs_0_.13, ...), custom_call_target="tpu_custom_call" | custom-call | flops 2147483648 | bytes 10485760 | tf_op jit(solution)/shard_map/share/pallas_call | solution.py:186
  86.6 7.1 %collective-permute-done.14.other_ref = bf16[64,2048]{1,0:T(8,128)(2,1)} collective-permute-done((bf16[64,2048]{1,0:T(8,128)(2,1)}, bf16[64,2048]{1,0:T(8,128)(2,1)}, u32[]{:S(2)}, u32[]{:S(2)}) %collective-permute-start.14) | collective-permute-done | bytes 262176 | tf_op jit(solution)/shard_map/ppermute | solution.py:24
  93.7 5.6 %collective-permute-done.16.other_ref = bf16[64,2048]{1,0:T(8,128)(2,1)} collective-permute-done((bf16[64,2048]{1,0:T(8,128)(2,1)}, bf16[64,2048]{1,0:T(8,128)(2,1)}, u32[]{:S(2)}, u32[]{:S(2)}) %collective-permute-start.16) | collective-permute-done | bytes 262176 | tf_op jit(solution)/shard_map/ppermute | solution.py:24
  106.0 20.6 %collective-permute-done.23.right_ref = bf16[2048,256]{1,0:T(8,128)(2,1)} collective-permute-done((bf16[2048,256]{1,0:T(8,128)(2,1)}, bf16[2048,256]{1,0:T(8,128)(2,1)}, u32[]{:S(2)}, u32[]{:S(2)}) %collective-permute-start.23) | collective-permute-done | bytes 1048608 | tf_op jit(solution)/shard_map/ppermute | solution.py:20
  128.8 13.4 %collective-permute-done.20.left_ref = bf16[2048,256]{1,0:T(8,128)(2,1)} collective-permute-done((bf16[2048,256]{1,0:T(8,128)(2,1)}, bf16[2048,256]{1,0:T(8,128)(2,1)}, u32[]{:S(2)}, u32[]{:S(2)}) %collective-permute-start.20) | collective-permute-done | bytes 1048608 | tf_op jit(solution)/shard_map/ppermute | solution.py:20
  144.0 5.0 %collective-permute-done.21.right_ref = bf16[2048,256]{1,0:T(8,128)(2,1)} collective-permute-done((bf16[2048,256]{1,0:T(8,128)(2,1)}, bf16[2048,256]{1,0:T(8,128)(2,1)}, u32[]{:S(2)}, u32[]{:S(2)}) %collective-permute-start.21) | collective-permute-done | bytes 1048608 | tf_op jit(solution)/shard_map/ppermute | solution.py:20
  173.1 13.0 %fresh.3 = (bf16[2048,1024]{1,0:T(8,128)(2,1)}, f32[512,1024]{1,0:T(8,128)}, f32[4,512,512]{2,1,0:T(8,128)}) custom-call(s32[4]{0:T(128)} %pad_add_fusion.place, f32[4]{0:T(128)} %pad_maximum_fusion.coef, bf16[512,2048]{1,0:T(8,128)(2,1)} %get-tuple-element.26.tok_ref, bf16[2048,1024]{1,0:T(8,128)(2,1)} %bitcast.30, ...), custom_call_target="tpu_custom_call" | custom-call | flops 2147483648 | bytes 16777216 | tf_op jit(solution)/shard_map/fresh/pallas_call | solution.py:251
  186.1 9.0 %fresh.4 = (bf16[2048,1024]{1,0:T(8,128)(2,1)}, f32[512,1024]{1,0:T(8,128)}, f32[4,512,512]{2,1,0:T(8,128)}) custom-call(s32[4]{0:T(128)} %pad_add_fusion.place, f32[4]{0:T(128)} %pad_maximum_fusion.coef, bf16[512,2048]{1,0:T(8,128)(2,1)} %get-tuple-element.26.tok_ref, bf16[2048,1024]{1,0:T(8,128)(2,1)} %bitcast.31, ...), custom_call_target="tpu_custom_call", output_to_operand_aliasing={{0}: (13, {}), {1}: (14, {})} | custom-call | flops 1073741824 | bytes 11534336 | tf_op jit(solution)/shard_map/fresh/pallas_call | solution.py:251
  198.0 8.0 %fresh.5 = (bf16[2048,1024]{1,0:T(8,128)(2,1)}, f32[512,1024]{1,0:T(8,128)}, bf16[256,2048]{1,0:T(8,128)(2,1)}, bf16[64,2048]{1,0:T(8,128)(2,1)}, bf16[64,2048]{...) custom-call(s32[4]{0:T(128)} %pad_add_fusion.place, ...), custom_call_target="tpu_custom_call", output_to_operand_aliasing={{0}: (13, {}), {1}: (14, {})} | custom-call | flops 1073741824 | bytes 11534336 | tf_op jit(solution)/shard_map/fresh/pallas_call | solution.py:251
  208.7 7.0 %collective-permute-done.40.other_ref = bf16[64,2048]{1,0:T(8,128)(2,1)} collective-permute-done((bf16[64,2048]{1,0:T(8,128)(2,1)}, bf16[64,2048]{1,0:T(8,128)(2,1)}, u32[]{:S(2)}, u32[]{:S(2)}) %collective-permute-start.40) | collective-permute-done | bytes 262176 | tf_op jit(solution)/shard_map/ppermute | solution.py:24
  215.7 5.6 %collective-permute-done.42.other_ref = bf16[64,2048]{1,0:T(8,128)(2,1)} collective-permute-done((bf16[64,2048]{1,0:T(8,128)(2,1)}, bf16[64,2048]{1,0:T(8,128)(2,1)}, u32[]{:S(2)}, u32[]{:S(2)}) %collective-permute-start.42) | collective-permute-done | bytes 262176 | tf_op jit(solution)/shard_map/ppermute | solution.py:24
  221.8 5.1 %collective-permute-done.44.other_ref = bf16[64,2048]{1,0:T(8,128)(2,1)} collective-permute-done((bf16[64,2048]{1,0:T(8,128)(2,1)}, bf16[64,2048]{1,0:T(8,128)(2,1)}, u32[]{:S(2)}, u32[]{:S(2)}) %collective-permute-start.44) | collective-permute-done | bytes 262176 | tf_op jit(solution)/shard_map/ppermute | solution.py:24
  239.3 20.5 %collective-permute-done.27.refs_6_ = bf16[64,2048]{1,0:T(8,128)(2,1)S(1)} collective-permute-done((bf16[64,2048]{1,0:T(8,128)(2,1)}, bf16[64,2048]{1,0:T(8,128)(2,1)S(1)}, u32[]{:S(2)}, u32[]{:S(2)}) %collective-permute-start.27) | collective-permute-done | bytes 262176 | tf_op jit(solution)/shard_map/ppermute | solution.py:20
  261.4 9.6 %collective-permute-done.43 = bf16[64,2048]{1,0:T(8,128)(2,1)S(1)} collective-permute-done((bf16[64,2048]{1,0:T(8,128)(2,1)}, bf16[64,2048]{1,0:T(8,128)(2,1)S(1)}, u32[]{:S(2)}, u32[]{:S(2)}) %collective-permute-start.43) | collective-permute-done | bytes 262176 | tf_op jit(solution)/shard_map/ppermute | solution.py:20
  297.4 7.4 %dgate.2.old_ref = bf16[512,1024]{1,0:T(8,128)(2,1)} custom-call(s32[4]{0:T(128)} %pad_add_fusion.place, f32[512,1024]{1,0:T(8,128)} %gate.1.gate_ref, f32[512,1024]{1,0:T(8,128)} %up.1.up_ref, bf16[1024,512]{1,0:T(8,128)(2,1)} %refs_0_.13, bf16[1024,512]{1,0:T(8,128)(2,1)} %collective-permute-done.10.refs_1_, ...), custom_call_target="tpu_custom_call" | custom-call | flops 2147483648 | bytes 11534336 | tf_op jit(solution)/shard_map/dgate/pallas_call | solution.py:344
  313.6 6.2 %base.6.rest_2_ = f32[2048,1024]{1,0:T(8,128)} custom-call(f32[4]{0:T(128)} %pad_maximum_fusion.coef, bf16[2048,512]{1,0:T(8,128)(2,1)} %get-tuple-element.40.turned_ref.turned_hbm, bf16[512,1024]{1,0:T(8,128)(2,1)} %dgate.2.old_ref, bf16[2048,1024]{1,0:T(8,128)(2,1)} %bitcast.26, ...), custom_call_target="tpu_custom_call", output_to_operand_aliasing={{}: (6, {})} | custom-call | flops 805306368 | bytes 7340032 | tf_op jit(solution)/shard_map/base/pallas_call | solution.py:381
  324.0 15.0 %dgate.3 = (bf16[2048,1024]{1,0:T(8,128)(2,1)}, f32[256,1024]{1,0:T(8,128)}) custom-call(s32[4]{0:T(128)} %pad_add_fusion.place, bf16[2048,512]{1,0:T(8,128)(2,1)} %get-tuple-element.40.turned_ref.turned_hbm, f32[2048,1024]{1,0:T(8,128)} %base.7.base_ref, f32[512,1024]{1,0:T(8,128)} %get-tuple-element.42.gate_ref, f32[512,1024]{1,0:T(8,128)} %up.1.up_ref, ...), custom_call_target="tpu_custom_call" | custom-call | flops 4294967296 | bytes 15728640 | tf_op jit(solution)/shard_map/dgate/pallas_call | solution.py:344
  (150 shorter events, 127.3 us)
Async XLA Ops:
  0.6 27.3 %collective-permute-start.7 = (bf16[512,1024]{1,0:T(8,128)(2,1)}, bf16[512,1024]{1,0:T(8,128)(2,1)S(1)}, u32[]{:S(2)}, u32[]{:S(2)}) collective-permute-start(bf16[512,1024]{1,0:T(8,128)(2,1)} %refs_0_.7), channel_id=1, source_target_pairs={{0,16},{8,24},{16,0},{24,8},{1,17},{9,25},{17,1},{25,9},{2,18},{10... | collective-permute-start | bytes 3145736 | tf_op jit(solution)/shard_map/ppermute | solution.py:20
  3.7 45.9 %collective-permute-start.10 = (bf16[1024,512]{1,0:T(8,128)(2,1)}, bf16[1024,512]{1,0:T(8,128)(2,1)}, u32[]{:S(2)}, u32[]{:S(2)}) collective-permute-start(bf16[1024,512]{1,0:T(8,128)(2,1)} %refs_0_.13), channel_id=1, source_target_pairs={{0,16},{8,24},{16,0},{24,8},{1,17},{9,25},{17,1},{25,9},{2,18},{10... | collective-permute-start | bytes 3145736 | tf_op jit(solution)/shard_map/ppermute | solution.py:20
  25.1 30.3 %collective-permute-start.8 = (bf16[512,1024]{1,0:T(8,128)(2,1)}, bf16[512,1024]{1,0:T(8,128)(2,1)S(1)}, u32[]{:S(2)}, u32[]{:S(2)}) collective-permute-start(bf16[512,1024]{1,0:T(8,128)(2,1)} %refs_0_.7), channel_id=1, source_target_pairs={{0,8},{8,0},{16,24},{24,16},{1,9},{9,1},{17,25},{25,17},{2,10},{10... | collective-permute-start | bytes 3145736 | tf_op jit(solution)/shard_map/ppermute | solution.py:24
  27.9 29.0 %collective-permute-start.9 = (bf16[512,1024]{1,0:T(8,128)(2,1)S(1)}, bf16[512,1024]{1,0:T(8,128)(2,1)S(1)}, u32[]{:S(2)}, u32[]{:S(2)}) collective-permute-start(bf16[512,1024]{1,0:T(8,128)(2,1)S(1)} %collective-permute-done.7.refs_1_), channel_id=1, source_target_pairs={{0,8},{8,0},{16,24},{24,16},{1,9},{9,1},{17,25},{25,17},{2,10},{10... | collective-permute-start | bytes 3145736 | tf_op jit(solution)/shard_map/ppermute | solution.py:24
  37.2 37.7 %collective-permute-start.11 = (bf16[1024,512]{1,0:T(8,128)(2,1)}, bf16[1024,512]{1,0:T(8,128)(2,1)}, u32[]{:S(2)}, u32[]{:S(2)}) collective-permute-start(bf16[1024,512]{1,0:T(8,128)(2,1)} %refs_0_.13), channel_id=1, source_target_pairs={{0,8},{8,0},{16,24},{24,16},{1,9},{9,1},{17,25},{25,17},{2,10},{10... | collective-permute-start | bytes 3145736 | tf_op jit(solution)/shard_map/ppermute | solution.py:24
  53.4 32.9 %collective-permute-start.22 = (bf16[2048,256]{1,0:T(8,128)(2,1)}, bf16[2048,256]{1,0:T(8,128)(2,1)}, u32[]{:S(2)}, u32[]{:S(2)}) collective-permute-start(bf16[2048,256]{1,0:T(8,128)(2,1)} %get-tuple-element.52), channel_id=1, source_target_pairs={{0,8},{8,16},{16,24},{24,0},{1,9},{9,17},{17,25},{25,1},{2,10},{10... | collective-permute-start | bytes 3145736 | tf_op jit(solution)/shard_map/ppermute | solution.py:20
  55.5 95.3 %collective-permute-start.24 = (bf16[2048,512]{1,0:T(8,128)(2,1)}, bf16[2048,512]{1,0:T(8,128)(2,1)}, u32[]{:S(2)}, u32[]{:S(2)}) collective-permute-start(bf16[2048,512]{1,0:T(8,128)(2,1)} %slice.54), channel_id=1, source_target_pairs={{0,8},{8,16},{16,24},{24,0},{1,9},{9,17},{17,25},{25,1},{2,10},{10... | collective-permute-start | bytes 6291464 | tf_op jit(solution)/shard_map/ppermute | solution.py:20
  56.9 97.5 %collective-permute-start.25 = (bf16[2048,512]{1,0:T(8,128)(2,1)}, bf16[2048,512]{1,0:T(8,128)(2,1)}, u32[]{:S(2)}, u32[]{:S(2)}) collective-permute-start(bf16[2048,512]{1,0:T(8,128)(2,1)} %slice.54), channel_id=1, source_target_pairs={{0,24},{8,0},{16,8},{24,16},{1,25},{9,1},{17,9},{25,17},{2,26},{10... | collective-permute-start | bytes 6291464 | tf_op jit(solution)/shard_map/ppermute | solution.py:20
  86.3 40.3 %collective-permute-start.23 = (bf16[2048,256]{1,0:T(8,128)(2,1)}, bf16[2048,256]{1,0:T(8,128)(2,1)}, u32[]{:S(2)}, u32[]{:S(2)}) collective-permute-start(bf16[2048,256]{1,0:T(8,128)(2,1)} %get-tuple-element.52), channel_id=1, source_target_pairs={{0,24},{8,0},{16,8},{24,16},{1,25},{9,1},{17,9},{25,17},{2,26},{10... | collective-permute-start | bytes 3145736 | tf_op jit(solution)/shard_map/ppermute | solution.py:20
  93.7 48.5 %collective-permute-start.20 = (bf16[2048,256]{1,0:T(8,128)(2,1)}, bf16[2048,256]{1,0:T(8,128)(2,1)}, u32[]{:S(2)}, u32[]{:S(2)}) collective-permute-start(bf16[2048,256]{1,0:T(8,128)(2,1)} %get-tuple-element.53), channel_id=1, source_target_pairs={{0,8},{8,16},{16,24},{24,0},{1,9},{9,17},{17,25},{25,1},{2,10},{10... | collective-permute-start | bytes 3145736 | tf_op jit(solution)/shard_map/ppermute | solution.py:20
  99.3 49.8 %collective-permute-start.21 = (bf16[2048,256]{1,0:T(8,128)(2,1)}, bf16[2048,256]{1,0:T(8,128)(2,1)}, u32[]{:S(2)}, u32[]{:S(2)}) collective-permute-start(bf16[2048,256]{1,0:T(8,128)(2,1)} %get-tuple-element.53), channel_id=1, source_target_pairs={{0,24},{8,0},{16,8},{24,16},{1,25},{9,1},{17,9},{25,17},{2,26},{10... | collective-permute-start | bytes 3145736 | tf_op jit(solution)/shard_map/ppermute | solution.py:20
  126.6 79.5 %collective-permute-start.37 = (bf16[512,1024]{1,0:T(8,128)(2,1)}, bf16[512,1024]{1,0:T(8,128)(2,1)}, u32[]{:S(2)}, u32[]{:S(2)}) collective-permute-start(bf16[512,1024]{1,0:T(8,128)(2,1)} %get-tuple-element.50), channel_id=1, source_target_pairs={{0,8},{8,16},{16,24},{24,0},{1,9},{9,17},{17,25},{25,1},{2,10},{10... | collective-permute-start | bytes 3145736 | tf_op jit(solution)/shard_map/ppermute | solution.py:20
  157.0 49.7 %collective-permute-start.38 = (bf16[512,1024]{1,0:T(8,128)(2,1)}, bf16[512,1024]{1,0:T(8,128)(2,1)}, u32[]{:S(2)}, u32[]{:S(2)}) collective-permute-start(bf16[512,1024]{1,0:T(8,128)(2,1)} %get-tuple-element.50), channel_id=1, source_target_pairs={{0,24},{8,0},{16,8},{24,16},{1,25},{9,1},{17,9},{25,17},{2,26},{10... | collective-permute-start | bytes 3145736 | tf_op jit(solution)/shard_map/ppermute | solution.py:20
  158.7 77.5 %collective-permute-start.35 = (bf16[768,1024]{1,0:T(8,128)(2,1)}, bf16[768,1024]{1,0:T(8,128)(2,1)}, u32[]{:S(2)}, u32[]{:S(2)}) collective-permute-start(bf16[768,1024]{1,0:T(8,128)(2,1)} %slice_bitcast_fusion), channel_id=1, source_target_pairs={{0,8},{8,16},{16,24},{24,0},{1,9},{9,17},{17,25},{25,1},{2,10},{10... | collective-permute-start | bytes 4718600 | tf_op jit(solution)/shard_map/ppermute | solution.py:20
  160.6 47.6 %collective-permute-start.33 = (bf16[512,1024]{1,0:T(8,128)(2,1)}, bf16[512,1024]{1,0:T(8,128)(2,1)}, u32[]{:S(2)}, u32[]{:S(2)}) collective-permute-start(bf16[512,1024]{1,0:T(8,128)(2,1)} %get-tuple-element.51), channel_id=1, source_target_pairs={{0,8},{8,16},{16,24},{24,0},{1,9},{9,17},{17,25},{25,1},{2,10},{10... | collective-permute-start | bytes 3145736 | tf_op jit(solution)/shard_map/ppermute | solution.py:20
  195.1 37.5 %collective-permute-start.34 = (bf16[512,1024]{1,0:T(8,128)(2,1)}, bf16[512,1024]{1,0:T(8,128)(2,1)}, u32[]{:S(2)}, u32[]{:S(2)}) collective-permute-start(bf16[512,1024]{1,0:T(8,128)(2,1)} %get-tuple-element.51), channel_id=1, source_target_pairs={{0,24},{8,0},{16,8},{24,16},{1,25},{9,1},{17,9},{25,17},{2,26},{10... | collective-permute-start | bytes 3145736 | tf_op jit(solution)/shard_map/ppermute | solution.py:20
  215.7 96.2 %collective-permute-start.36 = (bf16[768,1024]{1,0:T(8,128)(2,1)}, bf16[768,1024]{1,0:T(8,128)(2,1)}, u32[]{:S(2)}, u32[]{:S(2)}) collective-permute-start(bf16[768,1024]{1,0:T(8,128)(2,1)} %slice_bitcast_fusion), channel_id=1, source_target_pairs={{0,24},{8,0},{16,8},{24,16},{1,25},{9,1},{17,9},{25,17},{2,26},{10... | collective-permute-start | bytes 4718600 | tf_op jit(solution)/shard_map/ppermute | solution.py:20
  232.6 27.2 %collective-permute-start.27 = (bf16[64,2048]{1,0:T(8,128)(2,1)}, bf16[64,2048]{1,0:T(8,128)(2,1)S(1)}, u32[]{:S(2)}, u32[]{:S(2)}) collective-permute-start(bf16[64,2048]{1,0:T(8,128)(2,1)} %fusion.1.refs_4_), channel_id=1, source_target_pairs={{0,4},{1,5},{2,6},{3,7},{4,0},{5,1},{6,2},{7,3},{8,12},{9,13},{10,... | collective-permute-start | bytes 786440 | tf_op jit(solution)/shard_map/ppermute | solution.py:20
  238.6 32.3 %collective-permute-start.43 = (bf16[64,2048]{1,0:T(8,128)(2,1)}, bf16[64,2048]{1,0:T(8,128)(2,1)S(1)}, u32[]{:S(2)}, u32[]{:S(2)}) collective-permute-start(bf16[64,2048]{1,0:T(8,128)(2,1)} %join.10), channel_id=1, source_target_pairs={{0,4},{1,5},{2,6},{3,7},{4,0},{5,1},{6,2},{7,3},{8,12},{9,13},{10,... | collective-permute-start | bytes 786440 | tf_op jit(solution)/shard_map/ppermute | solution.py:20
  238.6 32.8 %collective-permute-start.45 = (bf16[64,2048]{1,0:T(8,128)(2,1)}, bf16[64,2048]{1,0:T(8,128)(2,1)S(1)}, u32[]{:S(2)}, u32[]{:S(2)}) collective-permute-start(bf16[64,2048]{1,0:T(8,128)(2,1)} %join.11), channel_id=1, source_target_pairs={{0,2},{1,3},{2,4},{3,5},{4,6},{5,7},{6,0},{7,1},{8,10},{9,11},{10,... | collective-permute-start | bytes 786440 | tf_op jit(solution)/shard_map/ppermute | solution.py:20
  289.6 34.4 %collective-permute-start.50 = (bf16[64,2048]{1,0:T(8,128)(2,1)}, bf16[64,2048]{1,0:T(8,128)(2,1)}, u32[]{:S(2)}, u32[]{:S(2)}) collective-permute-start(bf16[64,2048]{1,0:T(8,128)(2,1)} %collective-permute-done.46.refs_5_), channel_id=1, source_target_pairs={{0,1},{1,0},{2,3},{3,2},{4,5},{5,4},{6,7},{7,6},{8,9},{9,8},{10,11... | collective-permute-start | bytes 786440 | tf_op jit(solution)/shard_map/ppermute | solution.py:24
  295.4 28.6 %collective-permute-start.51 = (bf16[64,2048]{1,0:T(8,128)(2,1)}, bf16[64,2048]{1,0:T(8,128)(2,1)}, u32[]{:S(2)}, u32[]{:S(2)}) collective-permute-start(bf16[64,2048]{1,0:T(8,128)(2,1)} %collective-permute-done.47.refs_6_), channel_id=1, source_target_pairs={{0,1},{1,0},{2,3},{3,2},{4,5},{5,4},{6,7},{7,6},{8,9},{9,8},{10,11... | collective-permute-start | bytes 786440 | tf_op jit(solution)/shard_map/ppermute | solution.py:24
  296.9 27.1 %collective-permute-start.52 = (bf16[64,2048]{1,0:T(8,128)(2,1)}, bf16[64,2048]{1,0:T(8,128)(2,1)}, u32[]{:S(2)}, u32[]{:S(2)}) collective-permute-start(bf16[64,2048]{1,0:T(8,128)(2,1)} %collective-permute-done.48.refs_7_), channel_id=1, source_target_pairs={{0,1},{1,0},{2,3},{3,2},{4,5},{5,4},{6,7},{7,6},{8,9},{9,8},{10,11... | collective-permute-start | bytes 786440 | tf_op jit(solution)/shard_map/ppermute | solution.py:24
  311.8 27.1 %collective-permute-start.53 = (bf16[256,1024]{1,0:T(8,128)(2,1)}, bf16[256,1024]{1,0:T(8,128)(2,1)}, u32[]{:S(2)}, u32[]{:S(2)}) collective-permute-start(bf16[256,1024]{1,0:T(8,128)(2,1)} %slice_bitcast_fusion.3), channel_id=1, source_target_pairs={{0,8},{8,16},{16,24},{24,0},{1,9},{9,17},{17,25},{25,1},{2,10},{10... | collective-permute-start | bytes 1572872 | tf_op jit(solution)/shard_map/ppermute | solution.py:20
  (48 other events, 697.3 us)

commit v4 on v3

--- a/solution.py
+++ b/solution.py
@@ -11,7 +11,7 @@
 
 F32 = jnp.float32
 BF16 = jnp.bfloat16
-PARTS = (4, 6, 4, 2)
+PARTS = (2, 8, 4, 2)
 VMEM_LIMIT = 67043328
 
 
@@ -62,6 +62,12 @@
 
 def columns(place, i, size):
     return pl.ds(pl.multiple_of(place[i] * size, size), size)
+
+
+def mixing(place, edge):
+    agent, agents = place[0], edge.shape[0]
+    right, left = edge[agent], edge[lax.rem(agent + agents - 1, agents)]
+    return 1.0 - right - left, right, left
 
 
 def pack_kernel(*refs):
@@ -195,7 +201,7 @@
     )(place, gate, up, *downs)
 
 
-def fresh_kernel(count, scale, first, last, place, coef, tok_ref, p_ref, left_ref, right_ref, t_ref, up_ref, *refs):
+def fresh_kernel(count, scale, first, last, place, edge, size, tok_ref, p_ref, left_ref, right_ref, t_ref, up_ref, *refs):
     weights, refs = refs[:count], refs[count:]
     carry = bring = None
     if not first:
@@ -208,19 +214,20 @@
             bring.start()
 
     fresh_ref, gate_ref, *refs = refs
+    own, e_right, e_left = mixing(place, edge)
     mixed = (
-        coef[0] * p_ref[...].astype(F32)
-        + coef[1] * right_ref[...].astype(F32)
-        + coef[2] * left_ref[...].astype(F32)
+        own * p_ref[...].astype(F32)
+        + e_right * right_ref[...].astype(F32)
+        + e_left * left_ref[...].astype(F32)
     )
-    fresh = (mixed - coef[3] * t_ref[...].astype(F32)).astype(BF16)
+    fresh = (mixed - size[0] * t_ref[...].astype(F32)).astype(BF16)
     fresh_ref[...] = fresh
     gate = dot(tok_ref[...], fresh) * scale
     gate_ref[...] = gate
     add_share(place, gate, up_ref, weights, carry, bring, refs[:-1], refs[-1])
 
 
-def fresh_of(place, coef, tok, param, left, right, track, up, downs, pairs, scale, start, so_far):
+def fresh_of(place, edge, size, tok, param, left, right, track, up, downs, pairs, scale, start, so_far):
     depth, width = param.shape
     rows, part = tok.shape[0], left.shape[1]
     cols = downs[0].shape[1]
@@ -230,8 +237,8 @@
     there = pl.BlockSpec((depth, block), lambda n: (0, base + n))
     here = pl.BlockSpec((depth, block), lambda n: (0, n))
     hidden = pl.BlockSpec((rows, block), lambda n: (0, base + n))
-    operands = [place, coef, tok, param, left, right, track, up, *downs]
-    specs = [SMEM, SMEM, pl.BlockSpec(tok.shape, lambda n: (0, 0)), there, here, here, there, hidden]
+    operands = [place, edge, size, tok, param, left, right, track, up, *downs]
+    specs = [SMEM, SMEM, SMEM, pl.BlockSpec(tok.shape, lambda n: (0, 0)), there, here, here, there, hidden]
     specs += [pl.BlockSpec((block, cols), lambda n: (base + n, 0))] * len(downs)
     total = (len(downs), rows, cols)
     whole = pl.BlockSpec(total, lambda n: (0, 0, 0))
@@ -279,6 +286,26 @@
     )(near, other)
 
 
+def err_kernel(near_ref, target_ref, *refs):
+    total = near_ref[...].astype(F32)
+    for ref in refs[:-1]:
+        total = total + ref[...].astype(F32)
+    refs[-1][...] = (2.0 * (total - target_ref[...].astype(F32))).astype(BF16)
+
+
+def err_of(near, targets, others):
+    whole = pl.BlockSpec(targets.shape, lambda i: (0, 0))
+    return call(
+        err_kernel,
+        grid=(1,),
+        in_specs=[whole] * (2 + len(others)),
+        out_specs=whole,
+        out_shape=like(targets.shape, BF16),
+        cost_estimate=cost(targets.size * 4, targets, targets, targets, *others),
+        name="err",
+    )(near, targets, *others)
+
+
 def dgate_block(count, place, gate_ref, up_ref, refs, err):
     weights, pieces = refs[:count], refs[count:]
 
@@ -325,7 +352,7 @@
 def dgate_of(place, gate, up, downs, pieces, more=None):
     width, cols = downs[0].shape
     rows = gate.shape[0]
-    block = block_of(width, 256)
+    block = block_of(width, 512)
     hidden = pl.BlockSpec((rows, block), lambda n: (0, n))
     whole = pl.BlockSpec(pieces[0].shape, lambda n: (0, 0))
     depth = cols * len(downs)
@@ -356,22 +383,23 @@
     )(*operands, gate, up, *downs, *pieces)
 
 
-def base_kernel(scale, coef, turned_ref, old_ref, t_ref, *rest):
-    mixed = coef[0] * t_ref[...].astype(F32)
+def base_kernel(scale, place, edge, turned_ref, old_ref, t_ref, *rest):
+    own, e_right, e_left = mixing(place, edge)
+    mixed = own * t_ref[...].astype(F32)
     if len(rest) > 2:
-        mixed = mixed + coef[1] * rest[1][...].astype(F32) + coef[2] * rest[0][...].astype(F32)
+        mixed = mixed + e_right * rest[1][...].astype(F32) + e_left * rest[0][...].astype(F32)
     rest[-1][...] = mixed - dot(turned_ref[...], old_ref[...]) * scale
 
 
-def base_of(coef, turned, old, track, sides, start, part, so_far, scale):
+def base_of(place, edge, turned, old, track, sides, start, part, so_far, scale):
     depth, width = track.shape
     rows = turned.shape[1]
     step = math.gcd(256, start, part)
     base = start // step
     there = pl.BlockSpec((step, width), lambda k: (base + k, 0))
     here = pl.BlockSpec((step, width), lambda k: (k, 0))
-    operands = [coef, turned, old, track, *sides]
-    specs = [SMEM, pl.BlockSpec((step, rows), lambda k: (base + k, 0))]
+    operands = [place, edge, turned, old, track, *sides]
+    specs = [SMEM, SMEM, pl.BlockSpec((step, rows), lambda k: (base + k, 0))]
     specs += [pl.BlockSpec((rows, width), lambda k: (0, 0)), there] + [here] * len(sides)
     aliases = {}
     if so_far is not None:
@@ -390,12 +418,13 @@
     )(*operands)
 
 
-def last_kernel(coef, late_ref, left_ref, right_ref, so_far, out_ref):
-    mixed = coef[1] * right_ref[...].astype(F32) + coef[2] * left_ref[...].astype(F32)
+def last_kernel(place, edge, late_ref, left_ref, right_ref, so_far, out_ref):
+    _, e_right, e_left = mixing(place, edge)
+    mixed = e_right * right_ref[...].astype(F32) + e_left * left_ref[...].astype(F32)
     out_ref[...] = (late_ref[...] + mixed).astype(BF16)
 
 
-def last_of(coef, late, left, right, out):
+def last_of(place, edge, late, left, right, out):
     part, width = late.shape
     start = out.shape[0] - part
     step = math.gcd(128, start, part)
@@ -404,13 +433,13 @@
     return call(
         last_kernel,
         grid=(part // step,),
-        in_specs=[SMEM, here, here, here, ANY],
+        in_specs=[SMEM, SMEM, here, here, here, ANY],
         out_specs=pl.BlockSpec((step, width), lambda k: (base + k, 0)),
         out_shape=like(out.shape, BF16),
-        input_output_aliases={4: 0},
+        input_output_aliases={5: 0},
         cost_estimate=cost(late.size, late, left, right, left),
         name="last",
-    )(coef, late, left, right, out)
+    )(place, edge, late, left, right, out)
 
 
 def spread(piece, axis, pairs):
@@ -423,16 +452,12 @@
     agents, count = lax.axis_size("agent"), lax.axis_size("tp")
     half, pairs = agents // 2, count // 2
     depth = param.shape[0]
-    piece = token_rows.shape[0]
     scale = 1.0 / depth**0.5
 
     index = lax.axis_index("agent")
     even, parity = index // 2, index % 2
     chips = [lax.rem(even - j + half, half) for j in range(half)]
     place = jnp.stack([2 * c + parity for c in chips] + [2 * c + 1 - parity for c in chips]).astype(jnp.int32)
-    e_right = lax.dynamic_slice_in_dim(edge_weight, index, 1)[0]
-    e_left = lax.dynamic_slice_in_dim(edge_weight, (index + agents - 1) % agents, 1)[0]
-    coef = jnp.stack([1.0 - e_right - e_left, e_right, e_left, step_size[0]])
 
     def gathered(weight):
         own = [weight] + [jumped(weight, "agent", j) for j in range(1, half)]
@@ -464,22 +489,19 @@
         for j in order[:-1]:
             value = join(near, sent[j], j)
             summed.append(jumped(value, "tp", -j))
-        total = near[:piece].astype(F32) + sent[0].astype(F32)
-        for value in summed:
-            total = total + value.astype(F32)
-        err = (2.0 * (total - target_rows.astype(F32))).astype(BF16)
+        err = err_of(near, target_rows, [sent[0], *summed])
         return spread(err, "tp", pairs)
 
     shares = share_of(place, gate, up, downs, pairs)
     made = None
     for h in range(blocks - 1):
         made = fresh_of(
-            place, coef, tok, param, *sides[h], track, up, downs, pairs, scale, edges[h], made
+            place, edge_weight, step_size, tok, param, *sides[h], track, up, downs, pairs, scale, edges[h], made
         )
     old_pieces = errors(shares)
-    later, old_pieces[0] = lax.optimization_barrier((coef, old_pieces[0]))
+    later, old_pieces[0] = lax.optimization_barrier((step_size, old_pieces[0]))
     fresh, new_gate, *shares = fresh_of(
-        place, later, tok, param, *sides[-1], track, up, downs, pairs, scale, edges[-2], made
+        place, edge_weight, later, tok, param, *sides[-1], track, up, downs, pairs, scale, edges[-2], made
     )
     new_pieces = errors(shares)
     (old,) = dgate_of(place, gate, up, downs, old_pieces)
@@ -487,10 +509,10 @@
     final = len(PARTS) - 1
     for c in [final] + list(range(final)):
         sides_y = () if c == final else around[c]
-        base = base_of(coef, turned, old, track, sides_y, starts[c], ends[c] - starts[c], base, scale)
+        base = base_of(place, edge_weight, turned, old, track, sides_y, starts[c], ends[c] - starts[c], base, scale)
     more = (turned, base, like(track.shape, BF16), starts[final], scale)
     out, late = dgate_of(place, new_gate, up, downs, new_pieces, more)
-    out = last_of(coef, late, *around[final], out)
+    out = last_of(place, edge_weight, late, *around[final], out)
     return (fresh[None], out[None])
 
 

time: 348 us -> 407 us (1.17)
  waiting for transfers between devices: 148 us -> 196 us
  starting transfers between devices: 60.8 us -> 80.8 us
  other arithmetic: 6.87 us -> 0.64 us
    ppermute x31, waiting for transfers between devices: 99.4 us -> 162 us  [shifted(): lax.ppermute(value, axis, [(source, (source + shift) % count) for source...]
    ppermute x31, starting transfers between devices: 39.3 us -> 55.8 us  [shifted(): lax.ppermute(value, axis, [(source, (source + shift) % count) for source...]
    ppermute x24, waiting for transfers between devices: 48.4 us -> 33.7 us  [paired(): lax.ppermute(value, axis, [(source, source ^ 1) for source in range(lax.a...]
    pallas_call x1 -> x3, Pallas kernels: 2.36 us -> 6.87 us  [the longest x2 4.51 us: err_of(): call(err_kernel, grid=(1,), in_specs=[whole] * (2 + len(others)), out_spe...]
    convert_element_type x2 -> x0, other arithmetic: 4.33 us -> none  [errors(): err = (2.0 * (total - target_rows.astype(F32))).astype(BF16)]
  transfers between devices with their start and end apart: 55 -> 55, of which waited for: 21 -> 19; matrix products, arithmetic and copies ran while one was open for 6% -> 2% of each run, Pallas kernels for 31% -> 27%
where the time goes in v4:
time: 407 us; the launch traced here: 403 us
  waiting for transfers between devices  196 us (48%)
  Pallas kernels  110 us (27%)
  starting transfers between devices  80.8 us (20%)
  local copies, waits for them, and re-layouts  13.5 us (3%)
    ppermute x31, waiting for transfers between devices, shifted(): lax.ppermute(value, axis, [(source, (source + shift) % count) for source...  162 us
    ppermute x31, starting transfers between devices, shifted(): lax.ppermute(value, axis, [(source, (source + shift) % count) for source...  55.8 us
    ppermute x24, waiting for transfers between devices, paired(): lax.ppermute(value, axis, [(source, source ^ 1) for source in range(lax.a...  33.7 us
    pallas_call x3, Pallas kernels, fresh_of(): call(functools.partial(fresh_kernel, len(downs), scale, first, last), gri...  30.1 us
    ppermute x24, starting transfers between devices, paired(): lax.ppermute(value, axis, [(source, source ^ 1) for source in range(lax.a...  25 us
    pallas_call x2, Pallas kernels, dgate_of(): call(kernel, grid=(width // block,), in_specs=specs + [hidden, hidden] +...  19.8 us
    pallas_call x4, Pallas kernels, base_of(): call(functools.partial(base_kernel, scale), grid=(part // step,), in_spec...  17.2 us
    pallas_call x6, Pallas kernels, join(): call(join_kernel, grid=(1,), in_specs=[pl.BlockSpec(other.shape, lambda i...  10.7 us
  transfers between devices with their start and end apart: 55, of which 19 were waited for; matrix products, arithmetic and copies ran while one was open for 2% of the time, Pallas kernels for 27%

profile of v4, /device:TPU:0, one launch (start us, length us, event | category | flops | bytes accessed | tf_op | source)
XLA Modules:
  0.0 403.0 jit_solution(3057588644946702844)
XLA Ops:
  15.0 8.6 %collective-permute-done.1.refs_2_ = bf16[64,2048]{1,0:T(8,128)(2,1)S(1)} collective-permute-done((bf16[64,2048]{1,0:T(8,128)(2,1)}, bf16[64,2048]{1,0:T(8,128)(2,1)S(1)}, u32[]{:S(2)}, u32[]{:S(2)}) %collective-permute-start.1) | collective-permute-done | bytes 262176 | tf_op jit(solution)/shard_map/ppermute | solution.py:20
  27.2 5.6 %collective-permute-done.5.refs_6_ = bf16[64,2048]{1,0:T(8,128)(2,1)S(1)} collective-permute-done((bf16[64,2048]{1,0:T(8,128)(2,1)S(1)}, bf16[64,2048]{1,0:T(8,128)(2,1)S(1)}, u32[]{:S(2)}, u32[]{:S(2)}) %collective-permute-start.5) | collective-permute-done | bytes 262176 | tf_op jit(solution)/shard_map/ppermute | solution.py:24
  41.9 35.5 %collective-permute-done.38.rest_1_ = bf16[256,1024]{1,0:T(8,128)(2,1)S(1)} collective-permute-done((bf16[256,1024]{1,0:T(8,128)(2,1)S(1)}, bf16[256,1024]{1,0:T(8,128)(2,1)S(1)}, u32[]{:S(2)}, u32[]{:S(2)}) %collective-permute-start.38) | collective-permute-done | bytes 524320 | tf_op jit(solution)/shard_map/ppermute | solution.py:20
  82.5 19.0 %collective-permute-done.22.left_ref = bf16[2048,256]{1,0:T(8,128)(2,1)S(1)} collective-permute-done((bf16[2048,256]{1,0:T(8,128)(2,1)S(1)}, bf16[2048,256]{1,0:T(8,128)(2,1)S(1)}, u32[]{:S(2)}, u32[]{:S(2)}) %collective-permute-start.22) | collective-permute-done | bytes 1048608 | tf_op jit(solution)/shard_map/ppermute | solution.py:20
  106.0 53.3 %collective-permute-done.20.left_ref = bf16[2048,256]{1,0:T(8,128)(2,1)S(1)} collective-permute-done((bf16[2048,256]{1,0:T(8,128)(2,1)}, bf16[2048,256]{1,0:T(8,128)(2,1)S(1)}, u32[]{:S(2)}, u32[]{:S(2)}) %collective-permute-start.20) | collective-permute-done | bytes 1048608 | tf_op jit(solution)/shard_map/ppermute | solution.py:20
  170.9 5.7 %gate.1.gate_ref = f32[512,1024]{1,0:T(8,128)} custom-call(bf16[512,2048]{1,0:T(8,128)(2,1)} %get-tuple-element.26.tok_ref, bf16[2048,1024]{1,0:T(8,128)(2,1)} %bitcast.26), custom_call_target="tpu_custom_call" | custom-call | flops 2147483648 | bytes 8388608 | tf_op jit(solution)/shard_map/gate/pallas_call | solution.py:99
  176.7 6.6 %up.1.up_ref = f32[512,1024]{1,0:T(8,128)} custom-call(s32[4]{0:T(128)} %pad_add_fusion.place, bf16[512,2048]{1,0:T(8,128)(2,1)} %get-tuple-element.26.tok_ref, bf16[512,1024]{1,0:T(8,128)(2,1)} %refs_0_.7, bf16[512,1024]{1,0:T(8,128)(2,1)} %copy-done.5, bf16[512,1024]{1,0:T(8,128)(2,1)} %copy-done.7, bf16[512,1024]{1,0:T(8,128)(2,1)} %copy-done.10), custom_call_target="tpu_custom_call" | custom-call | flops 2147483648 | bytes 8388608 | tf_op jit(solution)/shard_map/up/pallas_call | solution.py:126
  183.3 9.3 %share.1 = (bf16[256,2048]{1,0:T(8,128)(2,1)}, bf16[64,2048]{1,0:T(8,128)(2,1)}, bf16[64,2048]{1,0:T(8,128)(2,1)}, bf16[64,2048]{1,0:T(8,128)(2,1)}, bf16[64,2048]{1,0:T(8,128)(2,1)}) custom-call(s32[4]{0:T(128)} %pad_add_fusion.place, f32[512,1024]{1,0:T(8,128)} %gate.1.gate_ref, f32[512,1024]{1,0:T(8,128)} %up.1.up_ref, bf16[1024,512]{1,0:T(8,128)(2,1)} %refs_0_.13, ...), custom_call_target="tpu_custom_call" | custom-call | flops 2147483648 | bytes 10485760 | tf_op jit(solution)/shard_map/share/pallas_call | solution.py:192
  194.1 13.1 %fresh.3 = (bf16[2048,1024]{1,0:T(8,128)(2,1)}, f32[512,1024]{1,0:T(8,128)}, f32[4,512,512]{2,1,0:T(8,128)}) custom-call(s32[4]{0:T(128)} %pad_add_fusion.place, f32[4]{0:T(128)} %edge.15, f32[1]{0:T(128)S(6)} %copy.26.size, bf16[512,2048]{1,0:T(8,128)(2,1)} %get-tuple-element.26.tok_ref, bf16[2048,1024]{1,0:T(8,128)(2,1)} %bitcast.27, ...), custom_call_target="tpu_custom_call" | custom-call | flops 2147483648 | bytes 16777216 | tf_op jit(solution)/shard_map/fresh/pallas_call | solution.py:258
  207.2 9.0 %fresh.4 = (bf16[2048,1024]{1,0:T(8,128)(2,1)}, f32[512,1024]{1,0:T(8,128)}, f32[4,512,512]{2,1,0:T(8,128)}) custom-call(s32[4]{0:T(128)} %pad_add_fusion.place, f32[4]{0:T(128)} %edge.15, f32[1]{0:T(128)S(6)} %copy.26.size, bf16[512,2048]{1,0:T(8,128)(2,1)} %get-tuple-element.26.tok_ref, ...), custom_call_target="tpu_custom_call", output_to_operand_aliasing={{0}: (14, {}), {1}: (15, {})} | custom-call | flops 1073741824 | bytes 11534336 | tf_op jit(solution)/shard_map/fresh/pallas_call | solution.py:258
  218.2 8.0 %fresh.5 = (bf16[2048,1024]{1,0:T(8,128)(2,1)}, f32[512,1024]{1,0:T(8,128)}, bf16[256,2048]{1,0:T(8,128)(2,1)}, bf16[64,2048]{1,0:T(8,128)(2,1)}, bf16[64,2048]{...) custom-call(s32[4]{0:T(128)} %pad_add_fusion.place, ...), custom_call_target="tpu_custom_call", output_to_operand_aliasing={{0}: (14, {}), {1}: (15, {})} | custom-call | flops 1073741824 | bytes 11534336 | tf_op jit(solution)/shard_map/fresh/pallas_call | solution.py:258
  229.9 5.9 %collective-permute-done.18.other_ref = bf16[64,2048]{1,0:T(8,128)(2,1)} collective-permute-done((bf16[64,2048]{1,0:T(8,128)(2,1)}, bf16[64,2048]{1,0:T(8,128)(2,1)}, u32[]{:S(2)}, u32[]{:S(2)}) %collective-permute-start.18) | collective-permute-done | bytes 262176 | tf_op jit(solution)/shard_map/ppermute | solution.py:24
  252.7 5.9 %collective-permute-start.45 = (bf16[64,2048]{1,0:T(8,128)(2,1)}, bf16[64,2048]{1,0:T(8,128)(2,1)}, u32[]{:S(2)}, u32[]{:S(2)}) collective-permute-start(bf16[64,2048]{1,0:T(8,128)(2,1)} %join.11), channel_id=1, source_target_pairs={{0,2},{1,3},{2,4},{3,5},{4,6},{5,7},{6,0},{7,1},{8,10},{9,11},{10,... | collective-permute-start | bytes 786440 | tf_op jit(solution)/shard_map/ppermute | solution.py:20
  258.7 4.7 %collective-permute-start.43 = (bf16[64,2048]{1,0:T(8,128)(2,1)}, bf16[64,2048]{1,0:T(8,128)(2,1)}, u32[]{:S(2)}, u32[]{:S(2)}) collective-permute-start(bf16[64,2048]{1,0:T(8,128)(2,1)} %join.10), channel_id=1, source_target_pairs={{0,4},{1,5},{2,6},{3,7},{4,0},{5,1},{6,2},{7,3},{8,12},{9,13},{10,... | collective-permute-start | bytes 786440 | tf_op jit(solution)/shard_map/ppermute | solution.py:20
  274.9 11.4 %collective-permute-start.17 = (bf16[64,2048]{1,0:T(8,128)(2,1)}, bf16[64,2048]{1,0:T(8,128)(2,1)}, u32[]{:S(2)}, u32[]{:S(2)}) collective-permute-start(bf16[64,2048]{1,0:T(8,128)(2,1)} %join.7), channel_id=1, source_target_pairs={{0,4},{1,5},{2,6},{3,7},{4,0},{5,1},{6,2},{7,3},{8,12},{9,13},{10,... | collective-permute-start | bytes 786440 | tf_op jit(solution)/shard_map/ppermute | solution.py:20
  288.1 5.3 %collective-permute-start.19 = (bf16[64,2048]{1,0:T(8,128)(2,1)}, bf16[64,2048]{1,0:T(8,128)(2,1)}, u32[]{:S(2)}, u32[]{:S(2)}) collective-permute-start(bf16[64,2048]{1,0:T(8,128)(2,1)} %join.8), channel_id=1, source_target_pairs={{0,2},{1,3},{2,4},{3,5},{4,6},{5,7},{6,0},{7,1},{8,10},{9,11},{10,... | collective-permute-start | bytes 786440 | tf_op jit(solution)/shard_map/ppermute | solution.py:20
  295.6 21.9 %collective-permute-done.17.refs_2_ = bf16[64,2048]{1,0:T(8,128)(2,1)} collective-permute-done((bf16[64,2048]{1,0:T(8,128)(2,1)}, bf16[64,2048]{1,0:T(8,128)(2,1)}, u32[]{:S(2)}, u32[]{:S(2)}) %collective-permute-start.17) | collective-permute-done | bytes 262176 | tf_op jit(solution)/shard_map/ppermute | solution.py:20
  324.7 10.0 %collective-permute-done.47.refs_6_ = bf16[64,2048]{1,0:T(8,128)(2,1)} collective-permute-done((bf16[64,2048]{1,0:T(8,128)(2,1)}, bf16[64,2048]{1,0:T(8,128)(2,1)}, u32[]{:S(2)}, u32[]{:S(2)}) %collective-permute-start.47) | collective-permute-done | bytes 262176 | tf_op jit(solution)/shard_map/ppermute | solution.py:20
  339.1 6.8 %collective-permute-done.27.refs_6_ = bf16[64,2048]{1,0:T(8,128)(2,1)S(1)} collective-permute-done((bf16[64,2048]{1,0:T(8,128)(2,1)}, bf16[64,2048]{1,0:T(8,128)(2,1)S(1)}, u32[]{:S(2)}, u32[]{:S(2)}) %collective-permute-start.27) | collective-permute-done | bytes 262176 | tf_op jit(solution)/shard_map/ppermute | solution.py:20
  350.1 5.0 %collective-permute-done.31.refs_10_ = bf16[64,2048]{1,0:T(8,128)(2,1)S(1)} collective-permute-done((bf16[64,2048]{1,0:T(8,128)(2,1)S(1)}, bf16[64,2048]{1,0:T(8,128)(2,1)S(1)}, u32[]{:S(2)}, u32[]{:S(2)}) %collective-permute-start.31) | collective-permute-done | bytes 262176 | tf_op jit(solution)/shard_map/ppermute | solution.py:24
  355.5 5.2 %collective-permute-done.32.refs_11_ = bf16[64,2048]{1,0:T(8,128)(2,1)S(1)} collective-permute-done((bf16[64,2048]{1,0:T(8,128)(2,1)S(1)}, bf16[64,2048]{1,0:T(8,128)(2,1)S(1)}, u32[]{:S(2)}, u32[]{:S(2)}) %collective-permute-start.32) | collective-permute-done | bytes 262176 | tf_op jit(solution)/shard_map/ppermute | solution.py:24
  361.9 7.1 %dgate.2.old_ref = bf16[512,1024]{1,0:T(8,128)(2,1)} custom-call(s32[4]{0:T(128)} %pad_add_fusion.place, f32[512,1024]{1,0:T(8,128)} %gate.1.gate_ref, f32[512,1024]{1,0:T(8,128)} %up.1.up_ref, bf16[1024,512]{1,0:T(8,128)(2,1)} %refs_0_.13, bf16[1024,512]{1,0:T(8,128)(2,1)} %copy-done.2, bf16[1024,512]{1,0:T(8,128)(2,1)} %copy-done.3, ...), custom_call_target="tpu_custom_call" | custom-call | flops 2147483648 | bytes 11534336 | tf_op jit(solution)/shard_map/dgate/pallas_call | solution.py:371
  376.9 6.8 %base.6.rest_2_ = f32[2048,1024]{1,0:T(8,128)} custom-call(s32[4]{0:T(128)} %pad_add_fusion.place, f32[4]{0:T(128)} %edge.15, bf16[2048,512]{1,0:T(8,128)(2,1)} %get-tuple-element.40.turned_ref.turned_hbm, bf16[512,1024]{1,0:T(8,128)(2,1)} %dgate.2.old_ref, bf16[2048,1024]{1,0:T(8,128)(2,1)} %bitcast.23, ...), custom_call_target="tpu_custom_call", output_to_operand_aliasing={{}: (7, {})} | custom-call | flops 1073741824 | bytes 9437184 | tf_op jit(solution)/shard_map/base/pallas_call | solution.py:409
  387.9 12.7 %dgate.3 = (bf16[2048,1024]{1,0:T(8,128)(2,1)}, f32[256,1024]{1,0:T(8,128)}) custom-call(s32[4]{0:T(128)} %pad_add_fusion.place, bf16[2048,512]{1,0:T(8,128)(2,1)} %get-tuple-element.40.turned_ref.turned_hbm, f32[2048,1024]{1,0:T(8,128)} %base.7.base_ref, f32[512,1024]{1,0:T(8,128)} %get-tuple-element.42.gate_ref, f32[512,1024]{1,0:T(8,128)} %up.1.up_ref, ...), custom_call_target="tpu_custom_call" | custom-call | flops 4294967296 | bytes 15728640 | tf_op jit(solution)/shard_map/dgate/pallas_call | solution.py:371
  (168 shorter events, 118.7 us)
Async XLA Ops:
  9.8 27.7 %collective-permute-start.37 = (bf16[256,1024]{1,0:T(8,128)(2,1)S(1)}, bf16[256,1024]{1,0:T(8,128)(2,1)S(1)}, u32[]{:S(2)}, u32[]{:S(2)}) collective-permute-start(bf16[256,1024]{1,0:T(8,128)(2,1)S(1)} %get-tuple-element.51), channel_id=1, source_target_pairs={{0,8},{8,16},{16,24},{24,0},{1,9},{9,17},{17,25},{25,1},{2,10},{10... | collective-permute-start | bytes 1572872 | tf_op jit(solution)/shard_map/ppermute | solution.py:20
  25.7 52.6 %collective-permute-start.7 = (bf16[512,1024]{1,0:T(8,128)(2,1)}, bf16[512,1024]{1,0:T(8,128)(2,1)S(1)}, u32[]{:S(2)}, u32[]{:S(2)}) collective-permute-start(bf16[512,1024]{1,0:T(8,128)(2,1)} %refs_0_.7), channel_id=1, source_target_pairs={{0,16},{8,24},{16,0},{24,8},{1,17},{9,25},{17,1},{25,9},{2,18},{10... | collective-permute-start | bytes 3145736 | tf_op jit(solution)/shard_map/ppermute | solution.py:20
  27.2 54.5 %collective-permute-start.8 = (bf16[512,1024]{1,0:T(8,128)(2,1)}, bf16[512,1024]{1,0:T(8,128)(2,1)S(1)}, u32[]{:S(2)}, u32[]{:S(2)}) collective-permute-start(bf16[512,1024]{1,0:T(8,128)(2,1)} %refs_0_.7), channel_id=1, source_target_pairs={{0,8},{8,0},{16,24},{24,16},{1,9},{9,1},{17,25},{25,17},{2,10},{10... | collective-permute-start | bytes 3145736 | tf_op jit(solution)/shard_map/ppermute | solution.py:24
  32.8 48.9 %collective-permute-start.10 = (bf16[1024,512]{1,0:T(8,128)(2,1)}, bf16[1024,512]{1,0:T(8,128)(2,1)S(1)}, u32[]{:S(2)}, u32[]{:S(2)}) collective-permute-start(bf16[1024,512]{1,0:T(8,128)(2,1)} %refs_0_.13), channel_id=1, source_target_pairs={{0,16},{8,24},{16,0},{24,8},{1,17},{9,25},{17,1},{25,9},{2,18},{10... | collective-permute-start | bytes 3145736 | tf_op jit(solution)/shard_map/ppermute | solution.py:20
  37.4 45.0 %collective-permute-start.11 = (bf16[1024,512]{1,0:T(8,128)(2,1)}, bf16[1024,512]{1,0:T(8,128)(2,1)S(1)}, u32[]{:S(2)}, u32[]{:S(2)}) collective-permute-start(bf16[1024,512]{1,0:T(8,128)(2,1)} %refs_0_.13), channel_id=1, source_target_pairs={{0,8},{8,0},{16,24},{24,16},{1,9},{9,1},{17,25},{25,17},{2,10},{10... | collective-permute-start | bytes 3145736 | tf_op jit(solution)/shard_map/ppermute | solution.py:24
  37.4 40.0 %collective-permute-start.38 = (bf16[256,1024]{1,0:T(8,128)(2,1)S(1)}, bf16[256,1024]{1,0:T(8,128)(2,1)S(1)}, u32[]{:S(2)}, u32[]{:S(2)}) collective-permute-start(bf16[256,1024]{1,0:T(8,128)(2,1)S(1)} %get-tuple-element.51), channel_id=1, source_target_pairs={{0,24},{8,0},{16,8},{24,16},{1,25},{9,1},{17,9},{25,17},{2,26},{10... | collective-permute-start | bytes 1572872 | tf_op jit(solution)/shard_map/ppermute | solution.py:20
  81.7 94.9 %collective-permute-start.24 = (bf16[2048,512]{1,0:T(8,128)(2,1)}, bf16[2048,512]{1,0:T(8,128)(2,1)}, u32[]{:S(2)}, u32[]{:S(2)}) collective-permute-start(bf16[2048,512]{1,0:T(8,128)(2,1)} %slice.46), channel_id=1, source_target_pairs={{0,8},{8,16},{16,24},{24,0},{1,9},{9,17},{17,25},{25,1},{2,10},{10... | collective-permute-start | bytes 6291464 | tf_op jit(solution)/shard_map/ppermute | solution.py:20
  81.7 77.5 %collective-permute-start.20 = (bf16[2048,256]{1,0:T(8,128)(2,1)}, bf16[2048,256]{1,0:T(8,128)(2,1)S(1)}, u32[]{:S(2)}, u32[]{:S(2)}) collective-permute-start(bf16[2048,256]{1,0:T(8,128)(2,1)} %get-tuple-element.53), channel_id=1, source_target_pairs={{0,8},{8,16},{16,24},{24,0},{1,9},{9,17},{17,25},{25,1},{2,10},{10... | collective-permute-start | bytes 3145736 | tf_op jit(solution)/shard_map/ppermute | solution.py:20
  82.4 76.9 %collective-permute-start.9 = (bf16[512,1024]{1,0:T(8,128)(2,1)S(1)}, bf16[512,1024]{1,0:T(8,128)(2,1)S(1)}, u32[]{:S(2)}, u32[]{:S(2)}) collective-permute-start(bf16[512,1024]{1,0:T(8,128)(2,1)S(1)} %collective-permute-done.7.refs_1_), channel_id=1, source_target_pairs={{0,8},{8,0},{16,24},{24,16},{1,9},{9,1},{17,25},{25,17},{2,10},{10... | collective-permute-start | bytes 3145736 | tf_op jit(solution)/shard_map/ppermute | solution.py:24
  101.4 91.1 %collective-permute-start.25 = (bf16[2048,512]{1,0:T(8,128)(2,1)}, bf16[2048,512]{1,0:T(8,128)(2,1)}, u32[]{:S(2)}, u32[]{:S(2)}) collective-permute-start(bf16[2048,512]{1,0:T(8,128)(2,1)} %slice.46), channel_id=1, source_target_pairs={{0,24},{8,0},{16,8},{24,16},{1,25},{9,1},{17,9},{25,17},{2,26},{10... | collective-permute-start | bytes 6291464 | tf_op jit(solution)/shard_map/ppermute | solution.py:20
  103.7 59.2 %collective-permute-start.12 = (bf16[1024,512]{1,0:T(8,128)(2,1)S(1)}, bf16[1024,512]{1,0:T(8,128)(2,1)S(1)}, u32[]{:S(2)}, u32[]{:S(2)}) collective-permute-start(bf16[1024,512]{1,0:T(8,128)(2,1)S(1)} %collective-permute-done.10.refs_1_), channel_id=1, source_target_pairs={{0,8},{8,0},{16,24},{24,16},{1,9},{9,1},{17,25},{25,17},{2,10},{10... | collective-permute-start | bytes 3145736 | tf_op jit(solution)/shard_map/ppermute | solution.py:24
  159.2 57.0 %collective-permute-start.21 = (bf16[2048,256]{1,0:T(8,128)(2,1)}, bf16[2048,256]{1,0:T(8,128)(2,1)}, u32[]{:S(2)}, u32[]{:S(2)}) collective-permute-start(bf16[2048,256]{1,0:T(8,128)(2,1)} %get-tuple-element.53), channel_id=1, source_target_pairs={{0,24},{8,0},{16,8},{24,16},{1,25},{9,1},{17,9},{25,17},{2,26},{10... | collective-permute-start | bytes 3145736 | tf_op jit(solution)/shard_map/ppermute | solution.py:20
  161.2 56.5 %collective-permute-start.33 = (bf16[512,1024]{1,0:T(8,128)(2,1)}, bf16[512,1024]{1,0:T(8,128)(2,1)}, u32[]{:S(2)}, u32[]{:S(2)}) collective-permute-start(bf16[512,1024]{1,0:T(8,128)(2,1)} %slice_bitcast_fusion.1), channel_id=1, source_target_pairs={{0,8},{8,16},{16,24},{24,0},{1,9},{9,17},{17,25},{25,1},{2,10},{10... | collective-permute-start | bytes 3145736 | tf_op jit(solution)/shard_map/ppermute | solution.py:20
  163.9 62.4 %collective-permute-start.34 = (bf16[512,1024]{1,0:T(8,128)(2,1)}, bf16[512,1024]{1,0:T(8,128)(2,1)}, u32[]{:S(2)}, u32[]{:S(2)}) collective-permute-start(bf16[512,1024]{1,0:T(8,128)(2,1)} %slice_bitcast_fusion.1), channel_id=1, source_target_pairs={{0,24},{8,0},{16,8},{24,16},{1,25},{9,1},{17,9},{25,17},{2,26},{10... | collective-permute-start | bytes 3145736 | tf_op jit(solution)/shard_map/ppermute | solution.py:20
  176.7 143.1 %collective-permute-start.35 = (bf16[1024,1024]{1,0:T(8,128)(2,1)}, bf16[1024,1024]{1,0:T(8,128)(2,1)}, u32[]{:S(2)}, u32[]{:S(2)}) collective-permute-start(bf16[1024,1024]{1,0:T(8,128)(2,1)} %slice_bitcast_fusion), channel_id=1, source_target_pairs={{0,8},{8,16},{16,24},{24,0},{1,9},{9,17},{17,25},{25,1},{2,10},{10... | collective-permute-start | bytes 6291464 | tf_op jit(solution)/shard_map/ppermute | solution.py:20
  192.5 35.3 %collective-permute-start.14 = (bf16[64,2048]{1,0:T(8,128)(2,1)}, bf16[64,2048]{1,0:T(8,128)(2,1)}, u32[]{:S(2)}, u32[]{:S(2)}) collective-permute-start(bf16[64,2048]{1,0:T(8,128)(2,1)} %get-tuple-element.29), channel_id=1, source_target_pairs={{0,1},{1,0},{2,3},{3,2},{4,5},{5,4},{6,7},{7,6},{8,9},{9,8},{10,11... | collective-permute-start | bytes 786440 | tf_op jit(solution)/shard_map/ppermute | solution.py:24
  216.2 158.9 %collective-permute-start.36 = (bf16[1024,1024]{1,0:T(8,128)(2,1)}, bf16[1024,1024]{1,0:T(8,128)(2,1)}, u32[]{:S(2)}, u32[]{:S(2)}) collective-permute-start(bf16[1024,1024]{1,0:T(8,128)(2,1)} %slice_bitcast_fusion), channel_id=1, source_target_pairs={{0,24},{8,0},{16,8},{24,16},{1,25},{9,1},{17,9},{25,17},{2,26},{10... | collective-permute-start | bytes 6291464 | tf_op jit(solution)/shard_map/ppermute | solution.py:20
  274.9 42.6 %collective-permute-start.17 = (bf16[64,2048]{1,0:T(8,128)(2,1)}, bf16[64,2048]{1,0:T(8,128)(2,1)}, u32[]{:S(2)}, u32[]{:S(2)}) collective-permute-start(bf16[64,2048]{1,0:T(8,128)(2,1)} %join.7), channel_id=1, source_target_pairs={{0,4},{1,5},{2,6},{3,7},{4,0},{5,1},{6,2},{7,3},{8,12},{9,13},{10,... | collective-permute-start | bytes 786440 | tf_op jit(solution)/shard_map/ppermute | solution.py:20
  288.1 29.4 %collective-permute-start.19 = (bf16[64,2048]{1,0:T(8,128)(2,1)}, bf16[64,2048]{1,0:T(8,128)(2,1)}, u32[]{:S(2)}, u32[]{:S(2)}) collective-permute-start(bf16[64,2048]{1,0:T(8,128)(2,1)} %join.8), channel_id=1, source_target_pairs={{0,2},{1,3},{2,4},{3,5},{4,6},{5,7},{6,0},{7,1},{8,10},{9,11},{10,... | collective-permute-start | bytes 786440 | tf_op jit(solution)/shard_map/ppermute | solution.py:20
  295.6 26.2 %collective-permute-start.46 = (bf16[64,2048]{1,0:T(8,128)(2,1)}, bf16[64,2048]{1,0:T(8,128)(2,1)}, u32[]{:S(2)}, u32[]{:S(2)}) collective-permute-start(bf16[64,2048]{1,0:T(8,128)(2,1)} %err.3.refs_4_), channel_id=1, source_target_pairs={{0,2},{1,3},{2,4},{3,5},{4,6},{5,7},{6,0},{7,1},{8,10},{9,11},{10,... | collective-permute-start | bytes 786440 | tf_op jit(solution)/shard_map/ppermute | solution.py:20
  348.0 27.2 %collective-permute-start.49 = (bf16[64,2048]{1,0:T(8,128)(2,1)}, bf16[64,2048]{1,0:T(8,128)(2,1)}, u32[]{:S(2)}, u32[]{:S(2)}) collective-permute-start(bf16[64,2048]{1,0:T(8,128)(2,1)} %err.3.refs_4_), channel_id=1, source_target_pairs={{0,1},{1,0},{2,3},{3,2},{4,5},{5,4},{6,7},{7,6},{8,9},{9,8},{10,11... | collective-permute-start | bytes 786440 | tf_op jit(solution)/shard_map/ppermute | solution.py:24
  348.3 39.6 %collective-permute-start.50 = (bf16[64,2048]{1,0:T(8,128)(2,1)}, bf16[64,2048]{1,0:T(8,128)(2,1)}, u32[]{:S(2)}, u32[]{:S(2)}) collective-permute-start(bf16[64,2048]{1,0:T(8,128)(2,1)} %collective-permute-done.46.refs_5_), channel_id=1, source_target_pairs={{0,1},{1,0},{2,3},{3,2},{4,5},{5,4},{6,7},{7,6},{8,9},{9,8},{10,11... | collective-permute-start | bytes 786440 | tf_op jit(solution)/shard_map/ppermute | solution.py:24
  355.1 32.8 %collective-permute-start.51 = (bf16[64,2048]{1,0:T(8,128)(2,1)}, bf16[64,2048]{1,0:T(8,128)(2,1)}, u32[]{:S(2)}, u32[]{:S(2)}) collective-permute-start(bf16[64,2048]{1,0:T(8,128)(2,1)} %collective-permute-done.47.refs_6_), channel_id=1, source_target_pairs={{0,1},{1,0},{2,3},{3,2},{4,5},{5,4},{6,7},{7,6},{8,9},{9,8},{10,11... | collective-permute-start | bytes 786440 | tf_op jit(solution)/shard_map/ppermute | solution.py:24
  361.4 26.4 %collective-permute-start.52 = (bf16[64,2048]{1,0:T(8,128)(2,1)}, bf16[64,2048]{1,0:T(8,128)(2,1)}, u32[]{:S(2)}, u32[]{:S(2)}) collective-permute-start(bf16[64,2048]{1,0:T(8,128)(2,1)} %collective-permute-done.48.refs_7_), channel_id=1, source_target_pairs={{0,1},{1,0},{2,3},{3,2},{4,5},{5,4},{6,7},{7,6},{8,9},{9,8},{10,11... | collective-permute-start | bytes 786440 | tf_op jit(solution)/shard_map/ppermute | solution.py:24
  (58 other events, 1332.8 us)
